TPU v7x, 32 devices: a whole 2x2x4 slice. The times are simulated.
32 devices in a mesh: gx: 16 (over z, y, x), gy: 2 (over core).
Axes of the slice: x: 2, y: 2, z: 4, core: 2. Of those that a mesh axis runs over, the one named last changes fastest.
Arguments:
- fields: float32 [5, 192, 32, 128], P(None, 'gx', 'gy'), may hold values from -1.5 to 6, as said below
- phase_map: int32 [192, 32, 128], P('gx', 'gy'), may hold values from 0 to 1, as said below
- lagged_speed: float32 [1], replicated, may hold values from 7 to 17, as said below
- step_count: int32 [1], replicated, may hold values from 0 to 1023
Outputs:
- advanced: float32 [5, 192, 32, 128], P(None, 'gx', 'gy')
- next_speed: float32 [1], replicated
Inputs may be any that keep to these rules, and one draw needn't show every extreme that they name: `phase_map`: in each column (fixed first and second index) the cells below a level between 32 and 96, drawn per column, are 1 and the cells above it are 0. Density lies within 1 to 2 in cells of phase 0 and within 1 to 4 in cells of phase 1; the pressure P(fields) lies within 0.6 to 1.6 and every velocity m_k / rho within -0.3 to 0.3. lagged_speed[0] lies between 1.01 and 1.31 times the largest over all cells of fields of |v_1| + |v_2| + |v_3| + 3 sqrt(gamma_cell (P + pinf_cell) / rho).
All inputs are finite; a program needn't handle non-finite values.
Results may differ from a plain program's by a relative error of at most 0.00002.
Values sent between devices are 32-bit elements; how exact they have to be, the bound alone decides.
No kernel may reach another device: no remote copies, remote signals or barrier semaphores. Data moves between devices by JAX's collectives and lax.ppermute only.
A program may use at most 128 MiB of HBM per device.

v0:
```python
import math

import jax
import jax.numpy as jnp
from jax import lax
from jax.sharding import PartitionSpec as P

PERIOD = 64


gamma_air = 1.4
gamma_water = 4.4
pinf_water = 3.0
cfl_number = 0.9
gravity = 1.0
shake_amp = 0.8
two_pi = 2.0 * math.pi
coef_one = 0.75
coef_two = -0.15
coef_three = 1.0 / 60.0
one_third = 1.0 / 3.0
two_thirds = 2.0 / 3.0


def padded(array, sides, width):
    for axis, dim in sides:
        count, length = (lax.axis_size(axis), array.shape[dim])
        up = [(i, (i + 1) % count) for i in range(count)]
        down = [(j, i) for i, j in up]
        last = lax.slice_in_dim(array, length - width, length, axis=dim)
        leading = lax.slice_in_dim(array, 0, width, axis=dim)
        before = lax.ppermute(last, axis, up)
        after = lax.ppermute(leading, axis, down)
        array = jnp.concatenate([before, array, after], axis=dim)
    return array


def pressure(fields, gamma_cell, pinf_cell):
    inverse = 1.0 / fields[0]
    kinetic = 0.5 * (
        fields[1] * (fields[1] * inverse)
        + fields[2] * (fields[2] * inverse)
        + fields[3] * (fields[3] * inverse)
    )
    return (gamma_cell - 1.0) * (fields[4] - kinetic) - gamma_cell * pinf_cell


def fluxes(fields, press_now, direction):
    inverse = 1.0 / fields[0]
    velocity = fields[1 + direction] * inverse
    pieces = [fields[1 + direction]]
    for member in range(3):
        moment = fields[1 + member] * velocity
        if member == direction:
            moment = moment + press_now
        pieces.append(moment)
    pieces.append((fields[4] + press_now) * velocity)
    return jnp.stack(pieces)


def roll_one(values, along):

    def shifted(offset):
        return jnp.roll(values, -offset, along)

    return (
        coef_one * (shifted(1) - shifted(-1))
        + coef_two * (shifted(2) - shifted(-2))
        + coef_three * (shifted(3) - shifted(-3))
    )


def slope_roll(values, along):
    return jnp.stack([roll_one(values[member], along - 1) for member in range(values.shape[0])])


def slide_along(values, along):
    length = values.shape[along] - 6

    def window(offset):
        return lax.slice_in_dim(values, 3 + offset, 3 + offset + length, axis=along)

    return (
        coef_one * (window(1) - window(-1))
        + coef_two * (window(2) - window(-2))
        + coef_three * (window(3) - window(-3))
    )


def sources(fields, gravity_now):
    blank = jnp.zeros_like(fields[0])
    return jnp.stack([blank, blank, blank, fields[0] * gravity_now, fields[3] * gravity_now])


def local(fields, phase_map, lagged_speed, step_count):
    water_frac = phase_map.astype(jnp.float32)
    gamma_cell = gamma_air + (gamma_water - gamma_air) * water_frac
    pinf_cell = pinf_water * water_frac
    time_step = cfl_number / lagged_speed[0]
    gravity_now = gravity * (
        1.0 + shake_amp * jnp.cos(two_pi * step_count[0].astype(jnp.float32) / PERIOD)
    )

    def section_rates(state, gamma_here, pinf_here):
        press_now = pressure(state, gamma_here, pinf_here)
        along_first = fluxes(state, press_now, 0)
        along_second = fluxes(state, press_now, 1)
        wide_first = padded(along_first, (("gx", 1),), 3)
        wide_second = padded(along_second, (("gy", 2),), 3)
        divergence = slide_along(wide_first, 1) + slide_along(wide_second, 2)
        divergence = divergence + slope_roll(fluxes(state, press_now, 2), 3)
        return sources(state, gravity_now) - divergence

    section_one = fields + time_step * section_rates(fields, gamma_cell, pinf_cell)
    section_two = 0.75 * fields + 0.25 * (
        section_one + time_step * section_rates(section_one, gamma_cell, pinf_cell)
    )
    advanced = one_third * fields + two_thirds * (
        section_two + time_step * section_rates(section_two, gamma_cell, pinf_cell)
    )
    press_now = pressure(advanced, gamma_cell, pinf_cell)
    inverse = 1.0 / advanced[0]
    local_speed = (
        jnp.abs(advanced[1] * inverse)
        + jnp.abs(advanced[2] * inverse)
        + jnp.abs(advanced[3] * inverse)
    )
    local_speed = local_speed + 3.0 * jnp.sqrt(gamma_cell * (press_now + pinf_cell) * inverse)
    largest = lax.pmax(jnp.max(local_speed), ("gx", "gy"))
    return (advanced, jnp.reshape(largest, (1,)))


def solution(mesh):
    return jax.shard_map(
        local,
        mesh=mesh,
        in_specs=(P(None, "gx", "gy", None), P("gx", "gy", None), P(), P()),
        out_specs=(P(None, "gx", "gy", None), P()),
        check_vma=False,
    )
```

profile of v0, /device:TPU:0, one launch (start us, length us, event | category | flops | bytes accessed | tf_op | source)
XLA Modules:
  0.0 82.5 jit_solution(13267985178277835018)
XLA Ops:
  1.4 0.9 %constant_dynamic-update-slice_fusion.1 = f32[5,12,16,128]{3,2,1,0:T(8,128)S(1)} fusion(f32[5,12,16,128]{3,2,1,0:T(8,128)} %param.4), kind=kLoop, calls=%fused_computation.538 | loop fusion | bytes 196608
  2.3 1.0 %multiply_dynamic-update-slice_fusion.9 = f32[5,12,16,128]{3,2,1,0:T(8,128)S(1)} fusion(f32[5,12,16,128]{3,2,1,0:T(8,128)S(1)} %constant_dynamic-update-slice_fusion.1, f32[5,12,16,128]{3,2,1,0:T(8,128)} %param.4), kind=kLoop, calls=%fused_computation.533 | loop fusion | flops 73728 | bytes 393216
  3.7 3.0 %collective-permute-start.1 = (f32[5,3,16,128]{3,2,1,0:T(8,128)S(1)}, f32[5,3,16,128]{3,2,1,0:T(8,128)S(1)}, u32[]{:S(2)}, u32[]{:S(2)}) collective-permute-start(f32[5,3,16,128]{3,2,1,0:T(8,128)S(1)} %get-tuple-element.56), channel_id=1, source_target_pairs={{0,2},{2,4},{4,6},{6,8},{8,10},{10,12},{12,14},{14,16},{16,18},{18... | collective-permute-start | bytes 368648 | tf_op jit(solution)/shard_map/ppermute | solution.py:32
  6.7 4.1 %collective-permute-start = (f32[5,3,16,128]{3,2,1,0:T(8,128)S(1)}, f32[5,3,16,128]{3,2,1,0:T(8,128)S(1)}, u32[]{:S(2)}, u32[]{:S(2)}) collective-permute-start(f32[5,3,16,128]{3,2,1,0:T(8,128)S(1)} %get-tuple-element.55), channel_id=1, source_target_pairs={{2,0},{4,2},{6,4},{8,6},{10,8},{12,10},{14,12},{16,14},{18,16},{20... | collective-permute-start | bytes 368648 | tf_op jit(solution)/shard_map/ppermute | solution.py:33
  10.9 0.5 collective-permute-start.2
  11.9 0.1 slice_bitcast_fusion.174
  12.0 0.1 slice_bitcast_fusion.159
  12.1 0.1 slice_bitcast_fusion.158
  12.2 0.1 slice_bitcast_fusion.155
  12.4 0.1 slice_bitcast_fusion.154
  12.5 0.1 slice_bitcast_fusion.151
  12.6 0.1 slice_bitcast_fusion.150
  12.7 0.1 slice_bitcast_fusion.135
  12.9 0.1 slice_bitcast_fusion.134
  13.0 0.1 slice_bitcast_fusion.131
  13.1 0.1 slice_bitcast_fusion.130
  13.2 0.1 slice_bitcast_fusion.127
  13.4 0.1 slice_bitcast_fusion.126
  13.5 0.2 fusion.104
  13.7 0.2 fusion.110
  13.9 0.2 fusion.116
  14.2 0.2 fusion.122
  14.4 0.2 fusion.128
  15.4 0.7 fusion.43
  16.5 0.1 slice_bitcast_fusion.121
  17.1 0.1 slice_bitcast_fusion.109
  17.2 0.1 slice_bitcast_fusion.106
  17.6 0.1 slice_bitcast_fusion.98
  17.7 0.1 slice_bitcast_fusion.97
  17.8 0.1 slice_bitcast_fusion.94
  18.2 0.1 slice_bitcast_fusion.85
  18.3 0.1 slice_bitcast_fusion.82
  18.8 0.1 slice_bitcast_fusion.73
  18.9 0.1 slice_bitcast_fusion.70
  19.0 0.1 slice_bitcast_fusion.69
  19.4 5.6 %collective-permute-start.4 = (f32[5,3,16,128]{3,2,1,0:T(8,128)S(1)}, f32[5,3,16,128]{3,2,1,0:T(8,128)S(1)}, u32[]{:S(2)}, u32[]{:S(2)}) collective-permute-start(f32[5,3,16,128]{3,2,1,0:T(8,128)S(1)} %get-tuple-element.45), channel_id=1, source_target_pairs={{2,0},{4,2},{6,4},{8,6},{10,8},{12,10},{14,12},{16,14},{18,16},{20... | collective-permute-start | bytes 368648 | tf_op jit(solution)/shard_map/ppermute | solution.py:33
  25.2 0.5 collective-permute-start.6
  25.7 0.2 fusion.134
  25.9 0.2 fusion.140
  26.1 0.2 fusion.146
  26.4 0.2 fusion.152
  26.6 0.2 fusion.158
  26.9 1.5 %collective-permute-done.5 = f32[5,3,16,128]{3,2,1,0:T(8,128)S(1)} collective-permute-done((f32[5,3,16,128]{3,2,1,0:T(8,128)S(1)}, f32[5,3,16,128]{3,2,1,0:T(8,128)S(1)}, u32[]{:S(2)}, u32[]{:S(2)}) %collective-permute-start.5) | collective-permute-done | bytes 122912 | tf_op jit(solution)/shard_map/ppermute | solution.py:32
  28.3 0.7 fusion.28
  29.7 0.1 slice_bitcast_fusion.53
  29.8 0.1 slice_bitcast_fusion.52
  30.1 0.1 slice_bitcast_fusion.45
  30.2 0.1 slice_bitcast_fusion.44
  30.7 0.1 slice_bitcast_fusion.33
  30.8 0.1 slice_bitcast_fusion.32
  30.9 0.1 slice_bitcast_fusion.29
  31.3 0.1 slice_bitcast_fusion.21
  31.4 0.1 slice_bitcast_fusion.20
  32.4 5.6 %collective-permute-start.8 = (f32[5,3,16,128]{3,2,1,0:T(8,128)S(1)}, f32[5,3,16,128]{3,2,1,0:T(8,128)S(1)}, u32[]{:S(2)}, u32[]{:S(2)}) collective-permute-start(f32[5,3,16,128]{3,2,1,0:T(8,128)S(1)} %get-tuple-element.35), channel_id=1, source_target_pairs={{2,0},{4,2},{6,4},{8,6},{10,8},{12,10},{14,12},{16,14},{18,16},{20... | collective-permute-start | bytes 368648 | tf_op jit(solution)/shard_map/ppermute | solution.py:33
  38.1 0.5 collective-permute-start.10
  38.6 0.2 fusion.164
  38.8 0.2 fusion.170
  39.1 0.2 fusion.176
  39.3 0.2 fusion.182
  39.5 0.2 fusion.188
  39.8 1.1 %collective-permute-done.9 = f32[5,3,16,128]{3,2,1,0:T(8,128)S(1)} collective-permute-done((f32[5,3,16,128]{3,2,1,0:T(8,128)S(1)}, f32[5,3,16,128]{3,2,1,0:T(8,128)S(1)}, u32[]{:S(2)}, u32[]{:S(2)}) %collective-permute-start.9) | collective-permute-done | bytes 122912 | tf_op jit(solution)/shard_map/ppermute | solution.py:32
  40.9 0.7 fusion.11
  41.6 0.7 fusion.95
  42.3 40.2 %pmax.7 = f32[1]{0:T(128)} all-reduce(f32[1]{0:T(128)} %bitcast.214), channel_id=1, replica_groups=mesh['gx'=16,'gy'=2] {'gx','gy'}, use_global_device_ids=true, to_apply=%region_1.2 | all-reduce | flops 1 | bytes 8 | tf_op jit(solution)/shard_map/pmax | solution.py:129
  (99 shorter events, 5.4 us)
Async XLA Ops:
  0.6 2.7 %copy-start = (f32[5,12,16,128]{3,2,1,0:T(8,128)S(1)}, f32[5,12,16,128]{3,2,1,0:T(8,128)}, u32[]{:S(2)}) copy-start(f32[5,12,16,128]{3,2,1,0:T(8,128)} %param.4) | copy-start | bytes 1474564
  2.3 1.1 %copy-start.2 = (s32[12,16,128]{2,1,0:T(8,128)S(1)}, s32[12,16,128]{2,1,0:T(8,128)}, u32[]{:S(2)}) copy-start(s32[12,16,128]{2,1,0:T(8,128)} %param.5) | copy-start | bytes 294916
  3.7 11.7 %collective-permute-start.1 = (f32[5,3,16,128]{3,2,1,0:T(8,128)S(1)}, f32[5,3,16,128]{3,2,1,0:T(8,128)S(1)}, u32[]{:S(2)}, u32[]{:S(2)}) collective-permute-start(f32[5,3,16,128]{3,2,1,0:T(8,128)S(1)} %get-tuple-element.56), channel_id=1, source_target_pairs={{0,2},{2,4},{4,6},{6,8},{8,10},{10,12},{12,14},{14,16},{16,18},{18... | collective-permute-start | bytes 368648 | tf_op jit(solution)/shard_map/ppermute | solution.py:32
  6.7 8.7 %collective-permute-start = (f32[5,3,16,128]{3,2,1,0:T(8,128)S(1)}, f32[5,3,16,128]{3,2,1,0:T(8,128)S(1)}, u32[]{:S(2)}, u32[]{:S(2)}) collective-permute-start(f32[5,3,16,128]{3,2,1,0:T(8,128)S(1)} %get-tuple-element.55), channel_id=1, source_target_pairs={{2,0},{4,2},{6,4},{8,6},{10,8},{12,10},{14,12},{16,14},{18,16},{20... | collective-permute-start | bytes 368648 | tf_op jit(solution)/shard_map/ppermute | solution.py:33
  10.8 4.6 %collective-permute-start.3 = (f32[5,12,3,128]{3,2,1,0:T(4,128)S(1)}, f32[5,12,3,128]{3,2,1,0:T(4,128)S(1)}, u32[]{:S(2)}, u32[]{:S(2)}) collective-permute-start(f32[5,12,3,128]{3,2,1,0:T(4,128)S(1)} %get-tuple-element.54), channel_id=1, source_target_pairs={{0,1},{1,0},{2,3},{3,2},{4,5},{5,4},{6,7},{7,6},{8,9},{9,8},{10,11... | collective-permute-start | bytes 276488 | tf_op jit(solution)/shard_map/ppermute | solution.py:32
  10.9 4.5 %collective-permute-start.2 = (f32[5,12,3,128]{3,2,1,0:T(4,128)S(1)}, f32[5,12,3,128]{3,2,1,0:T(4,128)S(1)}, u32[]{:S(2)}, u32[]{:S(2)}) collective-permute-start(f32[5,12,3,128]{3,2,1,0:T(4,128)S(1)} %get-tuple-element.53), channel_id=1, source_target_pairs={{1,0},{0,1},{3,2},{2,3},{5,4},{4,5},{7,6},{6,7},{9,8},{8,9},{11,10... | collective-permute-start | bytes 276488 | tf_op jit(solution)/shard_map/ppermute | solution.py:33
  19.4 9.0 %collective-permute-start.5 = (f32[5,3,16,128]{3,2,1,0:T(8,128)S(1)}, f32[5,3,16,128]{3,2,1,0:T(8,128)S(1)}, u32[]{:S(2)}, u32[]{:S(2)}) collective-permute-start(f32[5,3,16,128]{3,2,1,0:T(8,128)S(1)} %get-tuple-element.46), channel_id=1, source_target_pairs={{0,2},{2,4},{4,6},{6,8},{8,10},{10,12},{12,14},{14,16},{16,18},{18... | collective-permute-start | bytes 368648 | tf_op jit(solution)/shard_map/ppermute | solution.py:32
  19.4 8.9 %collective-permute-start.4 = (f32[5,3,16,128]{3,2,1,0:T(8,128)S(1)}, f32[5,3,16,128]{3,2,1,0:T(8,128)S(1)}, u32[]{:S(2)}, u32[]{:S(2)}) collective-permute-start(f32[5,3,16,128]{3,2,1,0:T(8,128)S(1)} %get-tuple-element.45), channel_id=1, source_target_pairs={{2,0},{4,2},{6,4},{8,6},{10,8},{12,10},{14,12},{16,14},{18,16},{20... | collective-permute-start | bytes 368648 | tf_op jit(solution)/shard_map/ppermute | solution.py:33
  25.1 1.7 %collective-permute-start.7 = (f32[5,12,3,128]{3,2,1,0:T(4,128)S(1)}, f32[5,12,3,128]{3,2,1,0:T(4,128)S(1)}, u32[]{:S(2)}, u32[]{:S(2)}) collective-permute-start(f32[5,12,3,128]{3,2,1,0:T(4,128)S(1)} %get-tuple-element.44), channel_id=1, source_target_pairs={{0,1},{1,0},{2,3},{3,2},{4,5},{5,4},{6,7},{7,6},{8,9},{9,8},{10,11... | collective-permute-start | bytes 276488 | tf_op jit(solution)/shard_map/ppermute | solution.py:32
  25.2 1.7 %collective-permute-start.6 = (f32[5,12,3,128]{3,2,1,0:T(4,128)S(1)}, f32[5,12,3,128]{3,2,1,0:T(4,128)S(1)}, u32[]{:S(2)}, u32[]{:S(2)}) collective-permute-start(f32[5,12,3,128]{3,2,1,0:T(4,128)S(1)} %get-tuple-element.43), channel_id=1, source_target_pairs={{1,0},{0,1},{3,2},{2,3},{5,4},{4,5},{7,6},{6,7},{9,8},{8,9},{11,10... | collective-permute-start | bytes 276488 | tf_op jit(solution)/shard_map/ppermute | solution.py:33
  32.3 8.5 %collective-permute-start.9 = (f32[5,3,16,128]{3,2,1,0:T(8,128)S(1)}, f32[5,3,16,128]{3,2,1,0:T(8,128)S(1)}, u32[]{:S(2)}, u32[]{:S(2)}) collective-permute-start(f32[5,3,16,128]{3,2,1,0:T(8,128)S(1)} %get-tuple-element.36), channel_id=1, source_target_pairs={{0,2},{2,4},{4,6},{6,8},{8,10},{10,12},{12,14},{14,16},{16,18},{18... | collective-permute-start | bytes 368648 | tf_op jit(solution)/shard_map/ppermute | solution.py:32
  32.4 8.5 %collective-permute-start.8 = (f32[5,3,16,128]{3,2,1,0:T(8,128)S(1)}, f32[5,3,16,128]{3,2,1,0:T(8,128)S(1)}, u32[]{:S(2)}, u32[]{:S(2)}) collective-permute-start(f32[5,3,16,128]{3,2,1,0:T(8,128)S(1)} %get-tuple-element.35), channel_id=1, source_target_pairs={{2,0},{4,2},{6,4},{8,6},{10,8},{12,10},{14,12},{16,14},{18,16},{20... | collective-permute-start | bytes 368648 | tf_op jit(solution)/shard_map/ppermute | solution.py:33
  38.0 1.7 %collective-permute-start.11 = (f32[5,12,3,128]{3,2,1,0:T(4,128)S(1)}, f32[5,12,3,128]{3,2,1,0:T(4,128)S(1)}, u32[]{:S(2)}, u32[]{:S(2)}) collective-permute-start(f32[5,12,3,128]{3,2,1,0:T(4,128)S(1)} %get-tuple-element.34), channel_id=1, source_target_pairs={{0,1},{1,0},{2,3},{3,2},{4,5},{5,4},{6,7},{7,6},{8,9},{9,8},{10,11... | collective-permute-start | bytes 276488 | tf_op jit(solution)/shard_map/ppermute | solution.py:32
  38.1 1.7 %collective-permute-start.10 = (f32[5,12,3,128]{3,2,1,0:T(4,128)S(1)}, f32[5,12,3,128]{3,2,1,0:T(4,128)S(1)}, u32[]{:S(2)}, u32[]{:S(2)}) collective-permute-start(f32[5,12,3,128]{3,2,1,0:T(4,128)S(1)} %get-tuple-element.33), channel_id=1, source_target_pairs={{1,0},{0,1},{3,2},{2,3},{5,4},{4,5},{7,6},{6,7},{9,8},{8,9},{11,10... | collective-permute-start | bytes 276488 | tf_op jit(solution)/shard_map/ppermute | solution.py:33
  41.6 40.9 %copy-start.1 = (f32[5,12,16,128]{3,2,1,0:T(8,128)}, f32[5,12,16,128]{3,2,1,0:T(8,128)S(1)}, u32[]{:S(2)}) copy-start(f32[5,12,16,128]{3,2,1,0:T(8,128)S(1)} %fusion.11) | copy-start | bytes 1474564
where the time goes:
time: 82.8 us; the launch traced here: 82.5 us
  blocking collectives  40.2 us (49%)
  starting transfers between devices  20.1 us (24%)
  other arithmetic  8.27 us (10%)
  local copies, waits for them, and re-layouts  8.25 us (10%)
  between operations  3.14 us (4%)
  waiting for transfers between devices  2.57 us (3%)
    pmax x1, blocking collectives, local(): largest = lax.pmax(jnp.max(local_speed), ('gx', 'gy'))  40.2 us
    ppermute x6, starting transfers between devices, padded(): after = lax.ppermute(leading, axis, down)  16.8 us
    concatenate x78, local copies, waits for them, and re-layouts, shifted(): return jnp.roll(values, -offset, along)  7.12 us
    unnamed x24, other arithmetic  4.17 us
    ppermute x6, starting transfers between devices, padded(): before = lax.ppermute(last, axis, up)  3.35 us
    ppermute x6, waiting for transfers between devices, padded(): before = lax.ppermute(last, axis, up)  2.55 us
  transfers between devices with their start and end apart: 12, of which 2 were waited for; matrix products, arithmetic and copies ran while one was open for 7% of the time, Pallas kernels for 0%

commit v1 on v0

--- a/solution.py
+++ b/solution.py
@@ -126,7 +126,9 @@
         + jnp.abs(advanced[3] * inverse)
     )
     local_speed = local_speed + 3.0 * jnp.sqrt(gamma_cell * (press_now + pinf_cell) * inverse)
-    largest = lax.pmax(jnp.max(local_speed), ("gx", "gy"))
+    members = lax.axis_size("gx") * lax.axis_size("gy")
+    copies = jnp.broadcast_to(jnp.max(local_speed), (members,))
+    largest = jnp.max(lax.all_to_all(copies, ("gx", "gy"), 0, 0, tiled=True))
     return (advanced, jnp.reshape(largest, (1,)))
 
 

time: 82.8 us -> 56.8 us (0.69)
  blocking collectives: 40.2 us -> 13 us
    pmax x1 -> x0, blocking collectives: 40.2 us -> none  [local(): largest = lax.pmax(jnp.max(local_speed), ('gx', 'gy'))]
    all_to_all x0 -> x1, blocking collectives: none -> 13 us  [local(): largest = jnp.max(lax.all_to_all(copies, ('gx', 'gy'), 0, 0, tiled=True))]
  transfers between devices with their start and end apart: 12 -> 12, of which waited for: 2 -> 2; matrix products, arithmetic and copies ran while one was open for 7% -> 10% of each run, Pallas kernels for 0% -> 0%
where the time goes in v1:
time: 56.8 us; the launch traced here: 56.6 us
  starting transfers between devices  20.1 us (35%)
  blocking collectives  13 us (23%)
  local copies, waits for them, and re-layouts  8.9 us (16%)
  other arithmetic  8.9 us (16%)
  between operations  3.14 us (6%)
  waiting for transfers between devices  2.57 us (5%)
    ppermute x6, starting transfers between devices, padded(): after = lax.ppermute(leading, axis, down)  16.8 us
    all_to_all x1, blocking collectives, local(): largest = jnp.max(lax.all_to_all(copies, ('gx', 'gy'), 0, 0, tiled=True))  13 us
    concatenate x78, local copies, waits for them, and re-layouts, shifted(): return jnp.roll(values, -offset, along)  7.12 us
    unnamed x24, other arithmetic  4.17 us
    ppermute x6, starting transfers between devices, padded(): before = lax.ppermute(last, axis, up)  3.35 us
    ppermute x6, waiting for transfers between devices, padded(): before = lax.ppermute(last, axis, up)  2.55 us
  transfers between devices with their start and end apart: 12, of which 2 were waited for; matrix products, arithmetic and copies ran while one was open for 10% of the time, Pallas kernels for 0%

profile of v1, /device:TPU:0, one launch (start us, length us, event | category | flops | bytes accessed | tf_op | source)
XLA Modules:
  0.0 56.6 jit_solution(16891545140601127516)
XLA Ops:
  1.4 0.9 %constant_dynamic-update-slice_fusion.1 = f32[5,12,16,128]{3,2,1,0:T(8,128)S(1)} fusion(f32[5,12,16,128]{3,2,1,0:T(8,128)} %param.4), kind=kLoop, calls=%fused_computation.538 | loop fusion | bytes 196608
  2.3 1.0 %multiply_dynamic-update-slice_fusion.9 = f32[5,12,16,128]{3,2,1,0:T(8,128)S(1)} fusion(f32[5,12,16,128]{3,2,1,0:T(8,128)S(1)} %constant_dynamic-update-slice_fusion.1, f32[5,12,16,128]{3,2,1,0:T(8,128)} %param.4), kind=kLoop, calls=%fused_computation.533 | loop fusion | flops 73728 | bytes 393216
  3.7 3.0 %collective-permute-start.1 = (f32[5,3,16,128]{3,2,1,0:T(8,128)S(1)}, f32[5,3,16,128]{3,2,1,0:T(8,128)S(1)}, u32[]{:S(2)}, u32[]{:S(2)}) collective-permute-start(f32[5,3,16,128]{3,2,1,0:T(8,128)S(1)} %get-tuple-element.56), channel_id=1, source_target_pairs={{0,2},{2,4},{4,6},{6,8},{8,10},{10,12},{12,14},{14,16},{16,18},{18... | collective-permute-start | bytes 368648 | tf_op jit(solution)/shard_map/ppermute | solution.py:32
  6.7 4.1 %collective-permute-start = (f32[5,3,16,128]{3,2,1,0:T(8,128)S(1)}, f32[5,3,16,128]{3,2,1,0:T(8,128)S(1)}, u32[]{:S(2)}, u32[]{:S(2)}) collective-permute-start(f32[5,3,16,128]{3,2,1,0:T(8,128)S(1)} %get-tuple-element.55), channel_id=1, source_target_pairs={{2,0},{4,2},{6,4},{8,6},{10,8},{12,10},{14,12},{16,14},{18,16},{20... | collective-permute-start | bytes 368648 | tf_op jit(solution)/shard_map/ppermute | solution.py:33
  10.9 0.5 collective-permute-start.2
  11.9 0.1 slice_bitcast_fusion.174
  12.0 0.1 slice_bitcast_fusion.159
  12.1 0.1 slice_bitcast_fusion.158
  12.2 0.1 slice_bitcast_fusion.155
  12.4 0.1 slice_bitcast_fusion.154
  12.5 0.1 slice_bitcast_fusion.151
  12.6 0.1 slice_bitcast_fusion.150
  12.7 0.1 slice_bitcast_fusion.135
  12.9 0.1 slice_bitcast_fusion.134
  13.0 0.1 slice_bitcast_fusion.131
  13.1 0.1 slice_bitcast_fusion.130
  13.2 0.1 slice_bitcast_fusion.127
  13.4 0.1 slice_bitcast_fusion.126
  13.5 0.2 fusion.104
  13.7 0.2 fusion.110
  13.9 0.2 fusion.116
  14.2 0.2 fusion.122
  14.4 0.2 fusion.128
  15.4 0.7 %fusion.43 = f32[5,12,16,128]{3,2,1,0:T(8,128)S(1)} fusion(f32[5,12,16,128]{3,2,1,0:T(8,128)S(1)} %copy-done, f32[5,12,16,128]{3,2,1,0:T(8,128)S(1)} %fusion.128, f32[5,12,16,128]{3,2,1,0:T(8,128)S(1)} %bitcast_dynamic-update-slice_fusion.10, f32[5,12,16,128]{3,2,1,0:T(8,128)S(1)} %get-tuple-element.25, f32[5,3,16,128]{3,2,1,0:T(8,128)S(1)} %collective-permute-done.1, ...), kind=kLoop, calls=%fused_computation.91 | loop fusion | flops 4300800 | bytes 3084312 | tf_op jit(solution)/shard_map/add | solution.py:114
  16.5 0.1 slice_bitcast_fusion.121
  17.1 0.1 slice_bitcast_fusion.109
  17.2 0.1 slice_bitcast_fusion.106
  17.6 0.1 slice_bitcast_fusion.98
  17.7 0.1 slice_bitcast_fusion.97
  17.8 0.1 slice_bitcast_fusion.94
  18.2 0.1 slice_bitcast_fusion.85
  18.3 0.1 slice_bitcast_fusion.82
  18.8 0.1 slice_bitcast_fusion.73
  18.9 0.1 slice_bitcast_fusion.70
  19.0 0.1 slice_bitcast_fusion.69
  19.4 5.6 %collective-permute-start.4 = (f32[5,3,16,128]{3,2,1,0:T(8,128)S(1)}, f32[5,3,16,128]{3,2,1,0:T(8,128)S(1)}, u32[]{:S(2)}, u32[]{:S(2)}) collective-permute-start(f32[5,3,16,128]{3,2,1,0:T(8,128)S(1)} %get-tuple-element.45), channel_id=1, source_target_pairs={{2,0},{4,2},{6,4},{8,6},{10,8},{12,10},{14,12},{16,14},{18,16},{20... | collective-permute-start | bytes 368648 | tf_op jit(solution)/shard_map/ppermute | solution.py:33
  25.2 0.5 collective-permute-start.6
  25.7 0.2 fusion.134
  25.9 0.2 fusion.140
  26.1 0.2 fusion.146
  26.4 0.2 fusion.152
  26.6 0.2 fusion.158
  26.9 1.5 %collective-permute-done.5 = f32[5,3,16,128]{3,2,1,0:T(8,128)S(1)} collective-permute-done((f32[5,3,16,128]{3,2,1,0:T(8,128)S(1)}, f32[5,3,16,128]{3,2,1,0:T(8,128)S(1)}, u32[]{:S(2)}, u32[]{:S(2)}) %collective-permute-start.5) | collective-permute-done | bytes 122912 | tf_op jit(solution)/shard_map/ppermute | solution.py:32
  28.3 0.7 %fusion.28 = f32[5,12,16,128]{3,2,1,0:T(8,128)S(1)} fusion(f32[5,12,16,128]{3,2,1,0:T(8,128)S(1)} %fusion.43, f32[5,12,16,128]{3,2,1,0:T(8,128)S(1)} %fusion.158, f32[5,12,16,128]{3,2,1,0:T(8,128)S(1)} %bitcast_dynamic-update-slice_fusion.6, f32[5,12,16,128]{3,2,1,0:T(8,128)S(1)} %get-tuple-element.21, f32[5,3,16,128]{3,2,1,0:T(8,128)S(1)} %collective-permute-done.5, ...), kind=kLoop, calls=%fused_computation.76 | loop fusion | flops 4669440 | bytes 3575832 | tf_op jit(solution)/shard_map/add | solution.py:115
  29.7 0.1 slice_bitcast_fusion.53
  29.8 0.1 slice_bitcast_fusion.52
  30.1 0.1 slice_bitcast_fusion.45
  30.2 0.1 slice_bitcast_fusion.44
  30.7 0.1 slice_bitcast_fusion.33
  30.8 0.1 slice_bitcast_fusion.32
  30.9 0.1 slice_bitcast_fusion.29
  32.4 5.6 %collective-permute-start.8 = (f32[5,3,16,128]{3,2,1,0:T(8,128)S(1)}, f32[5,3,16,128]{3,2,1,0:T(8,128)S(1)}, u32[]{:S(2)}, u32[]{:S(2)}) collective-permute-start(f32[5,3,16,128]{3,2,1,0:T(8,128)S(1)} %get-tuple-element.35), channel_id=1, source_target_pairs={{2,0},{4,2},{6,4},{8,6},{10,8},{12,10},{14,12},{16,14},{18,16},{20... | collective-permute-start | bytes 368648 | tf_op jit(solution)/shard_map/ppermute | solution.py:33
  38.1 0.5 collective-permute-start.10
  38.6 0.2 fusion.164
  38.8 0.2 fusion.170
  39.1 0.2 fusion.176
  39.3 0.2 fusion.182
  39.5 0.2 fusion.188
  39.8 1.1 %collective-permute-done.9 = f32[5,3,16,128]{3,2,1,0:T(8,128)S(1)} collective-permute-done((f32[5,3,16,128]{3,2,1,0:T(8,128)S(1)}, f32[5,3,16,128]{3,2,1,0:T(8,128)S(1)}, u32[]{:S(2)}, u32[]{:S(2)}) %collective-permute-start.9) | collective-permute-done | bytes 122912 | tf_op jit(solution)/shard_map/ppermute | solution.py:32
  40.9 0.7 %fusion.11 = f32[5,12,16,128]{3,2,1,0:T(8,128)S(1)} fusion(f32[5,12,16,128]{3,2,1,0:T(8,128)S(1)} %fusion.28, f32[5,12,16,128]{3,2,1,0:T(8,128)S(1)} %fusion.188, f32[5,12,16,128]{3,2,1,0:T(8,128)S(1)} %bitcast_dynamic-update-slice_fusion.2, f32[5,12,16,128]{3,2,1,0:T(8,128)S(1)} %get-tuple-element.17, f32[5,3,16,128]{3,2,1,0:T(8,128)S(1)} %collective-permute-done.9, ...), kind=kLoop, calls=%fused_computation.59 | loop fusion | flops 4669440 | bytes 3575832 | tf_op jit(solution)/shard_map/add | solution.py:118
  41.6 0.7 %fusion.95 = f32[]{:T(128)} fusion(f32[5,12,16,128]{3,2,1,0:T(8,128)S(1)} %fusion.11, s32[12,16,128]{2,1,0:T(8,128)S(1)} %copy-done.2), kind=kLoop, calls=%fused_computation.157 | loop fusion | flops 712703 | bytes 589828 | tf_op jit(solution)/shard_map/reduce_max | solution.py:130
  42.3 0.7 %broadcast_in_dim.3 = f32[32,1,1]{2,1,0:T(1,128)S(1)} broadcast(f32[]{:T(128)} %fusion.95), dimensions={} | broadcast | bytes 132 | tf_op jit(solution)/shard_map/broadcast_in_dim | solution.py:130
  43.0 13.0 %all_to_all.6 = f32[32,1,1]{2,1,0:T(1,128)S(1)} all-to-all(f32[32,1,1]{2,1,0:T(1,128)S(1)} %broadcast_in_dim.3), channel_id=1, replica_groups=mesh['gx'=16,'gy'=2] {'gx','gy'}, dimensions={0} | all-to-all | bytes 256 | tf_op jit(solution)/shard_map/all_to_all | solution.py:131
  56.0 0.6 %reduce_max.19 = f32[]{:T(128)} reduce(f32[32,1,1]{2,1,0:T(1,128)S(1)} %all_to_all.6, f32[]{:T(128)} %constant.43.clone.1), dimensions={0,1,2}, to_apply=%region_1.2 | reduce | flops 31 | bytes 136 | tf_op jit(solution)/shard_map/reduce_max | solution.py:131
  (101 shorter events, 5.6 us)
Async XLA Ops:
  0.6 2.7 %copy-start = (f32[5,12,16,128]{3,2,1,0:T(8,128)S(1)}, f32[5,12,16,128]{3,2,1,0:T(8,128)}, u32[]{:S(2)}) copy-start(f32[5,12,16,128]{3,2,1,0:T(8,128)} %param.4) | copy-start | bytes 1474564
  2.3 1.1 %copy-start.2 = (s32[12,16,128]{2,1,0:T(8,128)S(1)}, s32[12,16,128]{2,1,0:T(8,128)}, u32[]{:S(2)}) copy-start(s32[12,16,128]{2,1,0:T(8,128)} %param.5) | copy-start | bytes 294916
  3.7 11.7 %collective-permute-start.1 = (f32[5,3,16,128]{3,2,1,0:T(8,128)S(1)}, f32[5,3,16,128]{3,2,1,0:T(8,128)S(1)}, u32[]{:S(2)}, u32[]{:S(2)}) collective-permute-start(f32[5,3,16,128]{3,2,1,0:T(8,128)S(1)} %get-tuple-element.56), channel_id=1, source_target_pairs={{0,2},{2,4},{4,6},{6,8},{8,10},{10,12},{12,14},{14,16},{16,18},{18... | collective-permute-start | bytes 368648 | tf_op jit(solution)/shard_map/ppermute | solution.py:32
  6.7 8.7 %collective-permute-start = (f32[5,3,16,128]{3,2,1,0:T(8,128)S(1)}, f32[5,3,16,128]{3,2,1,0:T(8,128)S(1)}, u32[]{:S(2)}, u32[]{:S(2)}) collective-permute-start(f32[5,3,16,128]{3,2,1,0:T(8,128)S(1)} %get-tuple-element.55), channel_id=1, source_target_pairs={{2,0},{4,2},{6,4},{8,6},{10,8},{12,10},{14,12},{16,14},{18,16},{20... | collective-permute-start | bytes 368648 | tf_op jit(solution)/shard_map/ppermute | solution.py:33
  10.8 4.6 %collective-permute-start.3 = (f32[5,12,3,128]{3,2,1,0:T(4,128)S(1)}, f32[5,12,3,128]{3,2,1,0:T(4,128)S(1)}, u32[]{:S(2)}, u32[]{:S(2)}) collective-permute-start(f32[5,12,3,128]{3,2,1,0:T(4,128)S(1)} %get-tuple-element.54), channel_id=1, source_target_pairs={{0,1},{1,0},{2,3},{3,2},{4,5},{5,4},{6,7},{7,6},{8,9},{9,8},{10,11... | collective-permute-start | bytes 276488 | tf_op jit(solution)/shard_map/ppermute | solution.py:32
  10.9 4.5 %collective-permute-start.2 = (f32[5,12,3,128]{3,2,1,0:T(4,128)S(1)}, f32[5,12,3,128]{3,2,1,0:T(4,128)S(1)}, u32[]{:S(2)}, u32[]{:S(2)}) collective-permute-start(f32[5,12,3,128]{3,2,1,0:T(4,128)S(1)} %get-tuple-element.53), channel_id=1, source_target_pairs={{1,0},{0,1},{3,2},{2,3},{5,4},{4,5},{7,6},{6,7},{9,8},{8,9},{11,10... | collective-permute-start | bytes 276488 | tf_op jit(solution)/shard_map/ppermute | solution.py:33
  19.4 9.0 %collective-permute-start.5 = (f32[5,3,16,128]{3,2,1,0:T(8,128)S(1)}, f32[5,3,16,128]{3,2,1,0:T(8,128)S(1)}, u32[]{:S(2)}, u32[]{:S(2)}) collective-permute-start(f32[5,3,16,128]{3,2,1,0:T(8,128)S(1)} %get-tuple-element.46), channel_id=1, source_target_pairs={{0,2},{2,4},{4,6},{6,8},{8,10},{10,12},{12,14},{14,16},{16,18},{18... | collective-permute-start | bytes 368648 | tf_op jit(solution)/shard_map/ppermute | solution.py:32
  19.4 8.9 %collective-permute-start.4 = (f32[5,3,16,128]{3,2,1,0:T(8,128)S(1)}, f32[5,3,16,128]{3,2,1,0:T(8,128)S(1)}, u32[]{:S(2)}, u32[]{:S(2)}) collective-permute-start(f32[5,3,16,128]{3,2,1,0:T(8,128)S(1)} %get-tuple-element.45), channel_id=1, source_target_pairs={{2,0},{4,2},{6,4},{8,6},{10,8},{12,10},{14,12},{16,14},{18,16},{20... | collective-permute-start | bytes 368648 | tf_op jit(solution)/shard_map/ppermute | solution.py:33
  25.1 1.7 %collective-permute-start.7 = (f32[5,12,3,128]{3,2,1,0:T(4,128)S(1)}, f32[5,12,3,128]{3,2,1,0:T(4,128)S(1)}, u32[]{:S(2)}, u32[]{:S(2)}) collective-permute-start(f32[5,12,3,128]{3,2,1,0:T(4,128)S(1)} %get-tuple-element.44), channel_id=1, source_target_pairs={{0,1},{1,0},{2,3},{3,2},{4,5},{5,4},{6,7},{7,6},{8,9},{9,8},{10,11... | collective-permute-start | bytes 276488 | tf_op jit(solution)/shard_map/ppermute | solution.py:32
  25.2 1.7 %collective-permute-start.6 = (f32[5,12,3,128]{3,2,1,0:T(4,128)S(1)}, f32[5,12,3,128]{3,2,1,0:T(4,128)S(1)}, u32[]{:S(2)}, u32[]{:S(2)}) collective-permute-start(f32[5,12,3,128]{3,2,1,0:T(4,128)S(1)} %get-tuple-element.43), channel_id=1, source_target_pairs={{1,0},{0,1},{3,2},{2,3},{5,4},{4,5},{7,6},{6,7},{9,8},{8,9},{11,10... | collective-permute-start | bytes 276488 | tf_op jit(solution)/shard_map/ppermute | solution.py:33
  32.3 8.5 %collective-permute-start.9 = (f32[5,3,16,128]{3,2,1,0:T(8,128)S(1)}, f32[5,3,16,128]{3,2,1,0:T(8,128)S(1)}, u32[]{:S(2)}, u32[]{:S(2)}) collective-permute-start(f32[5,3,16,128]{3,2,1,0:T(8,128)S(1)} %get-tuple-element.36), channel_id=1, source_target_pairs={{0,2},{2,4},{4,6},{6,8},{8,10},{10,12},{12,14},{14,16},{16,18},{18... | collective-permute-start | bytes 368648 | tf_op jit(solution)/shard_map/ppermute | solution.py:32
  32.4 8.5 %collective-permute-start.8 = (f32[5,3,16,128]{3,2,1,0:T(8,128)S(1)}, f32[5,3,16,128]{3,2,1,0:T(8,128)S(1)}, u32[]{:S(2)}, u32[]{:S(2)}) collective-permute-start(f32[5,3,16,128]{3,2,1,0:T(8,128)S(1)} %get-tuple-element.35), channel_id=1, source_target_pairs={{2,0},{4,2},{6,4},{8,6},{10,8},{12,10},{14,12},{16,14},{18,16},{20... | collective-permute-start | bytes 368648 | tf_op jit(solution)/shard_map/ppermute | solution.py:33
  38.0 1.7 %collective-permute-start.11 = (f32[5,12,3,128]{3,2,1,0:T(4,128)S(1)}, f32[5,12,3,128]{3,2,1,0:T(4,128)S(1)}, u32[]{:S(2)}, u32[]{:S(2)}) collective-permute-start(f32[5,12,3,128]{3,2,1,0:T(4,128)S(1)} %get-tuple-element.34), channel_id=1, source_target_pairs={{0,1},{1,0},{2,3},{3,2},{4,5},{5,4},{6,7},{7,6},{8,9},{9,8},{10,11... | collective-permute-start | bytes 276488 | tf_op jit(solution)/shard_map/ppermute | solution.py:32
  38.1 1.7 %collective-permute-start.10 = (f32[5,12,3,128]{3,2,1,0:T(4,128)S(1)}, f32[5,12,3,128]{3,2,1,0:T(4,128)S(1)}, u32[]{:S(2)}, u32[]{:S(2)}) collective-permute-start(f32[5,12,3,128]{3,2,1,0:T(4,128)S(1)} %get-tuple-element.33), channel_id=1, source_target_pairs={{1,0},{0,1},{3,2},{2,3},{5,4},{4,5},{7,6},{6,7},{9,8},{8,9},{11,10... | collective-permute-start | bytes 276488 | tf_op jit(solution)/shard_map/ppermute | solution.py:33
  41.6 15.0 %copy-start.1 = (f32[5,12,16,128]{3,2,1,0:T(8,128)}, f32[5,12,16,128]{3,2,1,0:T(8,128)S(1)}, u32[]{:S(2)}) copy-start(f32[5,12,16,128]{3,2,1,0:T(8,128)S(1)} %fusion.11) | copy-start | bytes 1474564

commit v2 on v0

v2 whole, which is shorter than its diff:
```python
import functools
import math

import jax
import jax.numpy as jnp
from jax import lax
from jax.experimental import pallas as pl
from jax.experimental.pallas import tpu as pltpu
from jax.sharding import PartitionSpec as P

PERIOD = 64


gamma_air = 1.4
gamma_water = 4.4
pinf_water = 3.0
cfl_number = 0.9
gravity = 1.0
shake_amp = 0.8
two_pi = 2.0 * math.pi
coef_one = 0.75
coef_two = -0.15
coef_three = 1.0 / 60.0
one_third = 1.0 / 3.0
two_thirds = 2.0 / 3.0

WIDTH = 3
TILE = 8
VMEM = pl.BlockSpec(memory_space=pltpu.VMEM)
SMEM = pl.BlockSpec(memory_space=pltpu.SMEM)


def point(state, phase):
    density, one, two, three, energy = state
    water_frac = phase.astype(jnp.float32)
    gamma_cell = gamma_air + (gamma_water - gamma_air) * water_frac
    pinf_cell = pinf_water * water_frac
    inverse = 1.0 / density
    velocity = (one * inverse, two * inverse, three * inverse)
    kinetic = 0.5 * (one * velocity[0] + two * velocity[1] + three * velocity[2])
    press_now = (gamma_cell - 1.0) * (energy - kinetic) - gamma_cell * pinf_cell
    return velocity, press_now, inverse, gamma_cell, pinf_cell


def flux(state, velocity, press_now, direction):
    speed = velocity[direction]
    pieces = [state[1 + direction]]
    for member in range(3):
        moment = state[1 + member] * speed
        pieces.append(moment + press_now if member == direction else moment)
    pieces.append((state[4] + press_now) * speed)
    return pieces


def plane(ref, index):
    return [ref[member, index] for member in range(5)]


def edge_fluxes(state_ref, phase_ref, last_ref, leading_ref):
    length = state_ref.shape[1]
    for target, start in ((last_ref, length - WIDTH), (leading_ref, 0)):
        for k in range(WIDTH):
            state = plane(state_ref, start + k)
            velocity, press_now, *_ = point(state, phase_ref[start + k])
            for member, piece in enumerate(flux(state, velocity, press_now, 0)):
                target[member, k] = piece


def edge_kernel(state_ref, phase_ref, last_ref, leading_ref):
    edge_fluxes(state_ref, phase_ref, last_ref, leading_ref)


def rows_kernel(state_ref, phase_ref, rows_ref):
    rows = state_ref.shape[2]
    below = lax.broadcasted_iota(jnp.int32, (TILE, state_ref.shape[3]), 0) < TILE // 2

    def body(index, carry):
        state = []
        for member in range(5):
            first = state_ref[member, index, 0:TILE]
            final = state_ref[member, index, rows - TILE : rows]
            state.append(jnp.where(below, first, final))
        phase = jnp.where(below, phase_ref[index, 0:TILE], phase_ref[index, rows - TILE : rows])
        velocity, press_now, *_ = point(state, phase)
        for member, piece in enumerate(flux(state, velocity, press_now, 1)):
            rows_ref[member, index] = piece
        return carry

    lax.fori_loop(0, state_ref.shape[1], body, 0, unroll=2)


def middle_kernel(weights, first, coefs, state_ref, phase_ref, start_ref, before_ref, after_ref, out_ref, xs, ys, zs):
    length, rows, lanes = phase_ref.shape
    blank = jnp.zeros((rows, lanes), jnp.float32)
    for member in range(5):
        for k in range(WIDTH):
            xs[member, k] = blank
            xs[member, WIDTH + length + k] = blank

    def fill(index, carry):
        state = plane(state_ref, index)
        velocity, press_now, *_ = point(state, phase_ref[index])
        for member, piece in enumerate(flux(state, velocity, press_now, 0)):
            xs[member, WIDTH + index] = piece
        for member, piece in enumerate(flux(state, velocity, press_now, 1)):
            ys[member, index, TILE : TILE + rows] = piece
            ys[member, index, 0:TILE] = before_ref[member, index]
            ys[member, index, TILE + rows : TILE + rows + TILE] = after_ref[member, index]
        for member, piece in enumerate(flux(state, velocity, press_now, 2)):
            zs[member, index] = piece
        return carry

    lax.fori_loop(0, length, fill, 0, unroll=2)
    keep, share = weights
    steps = [coefs[k] * share for k in range(3)]
    source = coefs[3] * share

    def update(index, carry):
        for member in range(5):
            third = zs[member, index]
            total = None
            for k in range(1, WIDTH + 1):
                ahead = xs[member, WIDTH + index + k] - xs[member, WIDTH + index - k]
                ahead = ahead + (
                    ys[member, index, TILE + k : TILE + k + rows] - ys[member, index, TILE - k : TILE - k + rows]
                )
                ahead = ahead + (pltpu.roll(third, lanes - k, 1) - pltpu.roll(third, k, 1))
                term = steps[k - 1] * ahead
                total = term if total is None else total + term
            value = state_ref[member, index]
            if first:
                value = value - total
            else:
                value = keep * start_ref[member, index] + (share * value - total)
            if member == 3:
                value = value + source * state_ref[0, index]
            if member == 4:
                value = value + source * state_ref[3, index]
            out_ref[member, index] = value
        return carry

    lax.fori_loop(0, length, update, 0)


def add_halo(share, coefs, partial_ref, left_ref, right_ref, out_ref):
    length = partial_ref.shape[1]
    steps = [coefs[k] * share for k in range(3)]
    for member in range(5):
        for near in range(WIDTH):
            left = partial_ref[member, near]
            right = partial_ref[member, length - 1 - near]
            for k in range(near + 1, WIDTH + 1):
                left = left + steps[k - 1] * left_ref[member, WIDTH + near - k]
                right = right - steps[k - 1] * right_ref[member, k - 1 - near]
            out_ref[member, near] = left
            out_ref[member, length - 1 - near] = right


def join_kernel(share, coefs, partial_ref, left_ref, right_ref, phase_ref, out_ref, last_ref, leading_ref):
    add_halo(share, coefs, partial_ref, left_ref, right_ref, out_ref)
    edge_fluxes(out_ref, phase_ref, last_ref, leading_ref)


def final_kernel(share, coefs, partial_ref, left_ref, right_ref, phase_ref, out_ref, peak_ref):
    length, rows, lanes = phase_ref.shape
    add_halo(share, coefs, partial_ref, left_ref, right_ref, out_ref)
    for index in range(WIDTH, length - WIDTH):
        for member in range(5):
            out_ref[member, index] = partial_ref[member, index]

    def body(index, largest):
        state = plane(out_ref, index)
        velocity, press_now, inverse, gamma_cell, pinf_cell = point(state, phase_ref[index])
        speed = jnp.abs(velocity[0]) + jnp.abs(velocity[1]) + jnp.abs(velocity[2])
        speed = speed + 3.0 * jnp.sqrt(gamma_cell * (press_now + pinf_cell) * inverse)
        return jnp.maximum(largest, speed)

    largest = lax.fori_loop(0, length, body, jnp.zeros((rows, lanes), jnp.float32), unroll=2)
    largest = jnp.max(largest, axis=0, keepdims=True)
    peak_ref[...] = jnp.broadcast_to(largest, peak_ref.shape)


def peak_kernel(peaks_ref, largest_ref):
    largest = jnp.max(jnp.max(peaks_ref[...], axis=0, keepdims=True), axis=1, keepdims=True)
    largest_ref[...] = largest


def shaped(*shape):
    return jax.ShapeDtypeStruct(shape, jnp.float32)


def call(kernel, outs, specs, args, *, flops, scratch=(), aliases=None):
    moved = 4 * sum(math.prod(o.shape) for o in outs)
    several = len(outs) > 1
    return pl.pallas_call(
        kernel,
        out_shape=list(outs) if several else outs[0],
        in_specs=specs,
        out_specs=[VMEM] * len(outs) if several else VMEM,
        scratch_shapes=list(scratch),
        input_output_aliases=aliases or {},
        cost_estimate=pl.CostEstimate(flops=flops, bytes_accessed=moved, transcendentals=0),
        compiler_params=pltpu.CompilerParams(vmem_limit_bytes=16 << 20),
    )(*args)


def local(fields, phase_map, lagged_speed, step_count):
    _, length, rows, lanes = fields.shape
    cells = length * rows * lanes
    time_step = cfl_number / lagged_speed[0]
    gravity_now = gravity * (
        1.0 + shake_amp * jnp.cos(two_pi * step_count[0].astype(jnp.float32) / PERIOD)
    )
    coefs = time_step * jnp.stack(
        [jnp.float32(coef_one), jnp.float32(coef_two), jnp.float32(coef_three), gravity_now]
    )
    along, across = lax.axis_size("gx"), lax.axis_size("gy")
    up = [(i, (i + 1) % along) for i in range(along)]
    down = [(j, i) for i, j in up]
    over = [(i, (i + 1) % across) for i in range(across)]
    back = [(j, i) for i, j in over]
    edge = shaped(5, WIDTH, rows, lanes)
    whole = shaped(5, length, rows, lanes)
    row_tile = shaped(5, length, TILE, lanes)

    state = fields
    last, leading = call(
        edge_kernel, [edge, edge], [VMEM, VMEM], [state, phase_map], flops=cells * 20
    )
    stages = ((0.0, 1.0), (0.75, 0.25), (one_third, two_thirds))
    for number, weights in enumerate(stages):
        left = lax.ppermute(last, "gx", up)
        right = lax.ppermute(leading, "gx", down)
        sent = call(rows_kernel, [row_tile], [VMEM, VMEM], [state, phase_map], flops=cells * 10)
        before = lax.ppermute(sent, "gy", over)
        after = before if across == 2 else lax.ppermute(sent, "gy", back)
        partial = call(
            functools.partial(middle_kernel, weights, number == 0),
            [whole],
            [SMEM] + [VMEM] * 5,
            [coefs, state, phase_map, fields, before, after],
            flops=cells * 2000,
            scratch=[
                pltpu.VMEM((5, length + 2 * WIDTH, rows, lanes), jnp.float32),
                pltpu.VMEM((5, length, rows + 2 * TILE, lanes), jnp.float32),
                pltpu.VMEM((5, length, rows, lanes), jnp.float32),
            ],
        )
        if number < 2:
            state, last, leading = call(
                functools.partial(join_kernel, weights[1]),
                [whole, edge, edge],
                [SMEM] + [VMEM] * 4,
                [coefs, partial, left, right, phase_map],
                flops=cells * 20,
                aliases={1: 0},
            )
        else:
            advanced, peak = call(
                functools.partial(final_kernel, weights[1]),
                [whole, shaped(along * across, lanes)],
                [SMEM] + [VMEM] * 4,
                [coefs, partial, left, right, phase_map],
                flops=cells * 50,
            )
    peaks = lax.all_to_all(peak, ("gx", "gy"), 0, 0, tiled=True)
    largest = call(peak_kernel, [shaped(1, 1)], [VMEM], [peaks], flops=1000)
    return (advanced, jnp.reshape(largest, (1,)))


def solution(mesh):
    return jax.shard_map(
        local,
        mesh=mesh,
        in_specs=(P(None, "gx", "gy", None), P("gx", "gy", None), P(), P()),
        out_specs=(P(None, "gx", "gy", None), P()),
        check_vma=False,
    )
```

time: 82.8 us -> 49.4 us (0.60)
  blocking collectives: 40.2 us -> 12.6 us
  Pallas kernels: 0 us -> 11.2 us
  other arithmetic: 8.27 us -> 0.08 us
  local copies, waits for them, and re-layouts: 8.25 us -> 1.93 us
  starting transfers between devices: 20.1 us -> 18.8 us
  between operations: 3.14 us -> 2.14 us
    pmax x1 -> x0, blocking collectives: 40.2 us -> none  [local(): largest = lax.pmax(jnp.max(local_speed), ('gx', 'gy'))]
    all_to_all x0 -> x1, blocking collectives: none -> 12.6 us  [local(): peaks = lax.all_to_all(peak, ('gx', 'gy'), 0, 0, tiled=True)]
    pallas_call x0 -> x11, Pallas kernels: none -> 11.2 us  [call(): pl.pallas_call(kernel, out_shape=list(outs) if several else outs[0], in_s...]
    concatenate x78 -> x0, local copies, waits for them, and re-layouts: 7.12 us -> none  [shifted(): return jnp.roll(values, -offset, along)]
    unnamed x24 -> x0, other arithmetic: 4.17 us -> none
    add x3 -> x0, other arithmetic: 2.19 us -> none  [the longest x1 0.74 us: local(): one_third * fields]
    ppermute x12 -> x9, starting transfers between devices: 20.1 us -> 18.8 us  [the longest x3 13.6 us: local(): right = lax.ppermute(leading, 'gx', down)]
    unnamed x9 -> x8, local copies, waits for them, and re-layouts: 0.94 us -> 1.93 us
  transfers between devices with their start and end apart: 12 -> 9, of which waited for: 2 -> 3; matrix products, arithmetic and copies ran while one was open for 7% -> 0% of each run, Pallas kernels for 0% -> 15%
where the time goes in v2:
time: 49.4 us; the launch traced here: 49.2 us
  starting transfers between devices  18.8 us (38%)
  blocking collectives  12.6 us (26%)
  Pallas kernels  11.2 us (23%)
  waiting for transfers between devices  2.52 us (5%)
  between operations  2.14 us (4%)
  local copies, waits for them, and re-layouts  1.93 us (4%)
    ppermute x3, starting transfers between devices, local(): right = lax.ppermute(leading, 'gx', down)  13.6 us
    all_to_all x1, blocking collectives, local(): peaks = lax.all_to_all(peak, ('gx', 'gy'), 0, 0, tiled=True)  12.6 us
    pallas_call x11, Pallas kernels, call(): pl.pallas_call(kernel, out_shape=list(outs) if several else outs[0], in_s...  11.2 us
    ppermute x3, starting transfers between devices, local(): left = lax.ppermute(last, 'gx', up)  4.27 us
    ppermute x3, waiting for transfers between devices, local(): left = lax.ppermute(last, 'gx', up)  2.51 us
    unnamed x8, local copies, waits for them, and re-layouts  1.93 us
  transfers between devices with their start and end apart: 9, of which 3 were waited for; matrix products, arithmetic and copies ran while one was open for 0% of the time, Pallas kernels for 15%

profile of v2, /device:TPU:0, one launch (start us, length us, event | category | flops | bytes accessed | tf_op | source)
XLA Modules:
  0.0 49.2 jit_solution(4740325991208302117)
XLA Ops:
  0.6 0.0 copy-start
  0.6 1.0 %copy-done = f32[5,12,16,128]{3,2,1,0:T(8,128)S(1)} copy-done((f32[5,12,16,128]{3,2,1,0:T(8,128)S(1)}, f32[5,12,16,128]{3,2,1,0:T(8,128)}, u32[]{:S(2)}) %copy-start) | copy-done | bytes 491544
  1.7 0.0 copy-start.2
  1.7 0.9 %copy-done.2 = s32[12,16,128]{2,1,0:T(8,128)S(1)} copy-done((s32[12,16,128]{2,1,0:T(8,128)S(1)}, s32[12,16,128]{2,1,0:T(8,128)}, u32[]{:S(2)}) %copy-start.2) | copy-done | bytes 98328
  2.6 0.1 shard_map.59
  2.7 0.6 %collective-permute-start = (f32[5,12,8,128]{3,2,1,0:T(8,128)S(1)}, f32[5,12,8,128]{3,2,1,0:T(8,128)S(1)}, u32[]{:S(2)}, u32[]{:S(2)}) collective-permute-start(f32[5,12,8,128]{3,2,1,0:T(8,128)S(1)} %shard_map.59), channel_id=1, source_target_pairs={{0,1},{1,0},{2,3},{3,2},{4,5},{5,4},{6,7},{7,6},{8,9},{9,8},{10,11... | collective-permute-start | bytes 737288 | tf_op jit(solution)/shard_map/ppermute | solution.py:235
  3.3 2.5 %collective-permute-start.1 = (f32[5,3,16,128]{3,2,1,0:T(8,128)S(1)}, f32[5,3,16,128]{3,2,1,0:T(8,128)S(1)}, u32[]{:S(2)}, u32[]{:S(2)}) collective-permute-start(f32[5,3,16,128]{3,2,1,0:T(8,128)S(1)} %get-tuple-element.12), channel_id=1, source_target_pairs={{0,2},{2,4},{4,6},{6,8},{8,10},{10,12},{12,14},{14,16},{16,18},{18... | collective-permute-start | bytes 368648 | tf_op jit(solution)/shard_map/ppermute | solution.py:232
  5.8 4.1 %collective-permute-start.2 = (f32[5,3,16,128]{3,2,1,0:T(8,128)S(1)}, f32[5,3,16,128]{3,2,1,0:T(8,128)S(1)}, u32[]{:S(2)}, u32[]{:S(2)}) collective-permute-start(f32[5,3,16,128]{3,2,1,0:T(8,128)S(1)} %get-tuple-element.13), channel_id=1, source_target_pairs={{2,0},{4,2},{6,4},{8,6},{10,8},{12,10},{14,12},{16,14},{18,16},{20... | collective-permute-start | bytes 368648 | tf_op jit(solution)/shard_map/ppermute | solution.py:233
  11.3 0.1 maximum_multiply_fusion.coefs
  11.4 0.0 copy-start.3
  11.4 0.0 collective-permute-done.before_ref.after_ref
  11.4 2.4 %shard_map.60.partial_ref = f32[5,12,16,128]{3,2,1,0:T(8,128)S(1)} custom-call(f32[4]{0:T(128)S(1)} %maximum_multiply_fusion.coefs, f32[5,12,16,128]{3,2,1,0:T(8,128)S(1)} %copy-done, s32[12,16,128]{2,1,0:T(8,128)S(1)} %copy-done.2, f32[5,12,16,128]{3,2,1,0:T(8,128)S(1)} %copy-done, f32[5,12,8,128]{3,2,1,0:T(8,128)S(1)} %collective-permute-done.before_ref.after_ref, ...), custom_call_target="tpu_custom_call" | custom-call | flops 49152000 | bytes 491520 | tf_op jit(solution)/shard_map/pallas_call | solution.py:195
  13.8 0.1 collective-permute-done.1.left_ref
  13.9 0.0 collective-permute-done.2.right_ref
  13.9 0.0 copy-done.3
  13.9 0.6 %shard_map.62 = (f32[5,12,16,128]{3,2,1,0:T(8,128)S(1)}, f32[5,3,16,128]{3,2,1,0:T(8,128)S(1)}, f32[5,3,16,128]{3,2,1,0:T(8,128)S(1)}) custom-call(f32[4]{0:T(128)S(1)} %maximum_multiply_fusion.coefs, f32[5,12,16,128]{3,2,1,0:T(8,128)S(1)} %shard_map.60.partial_ref, ...), custom_call_target="tpu_custom_call", output_to_operand_aliasing={{0}: (1, {})} | custom-call | flops 491520 | bytes 737280 | tf_op jit(solution)/shard_map/pallas_call | solution.py:195
  14.6 0.0 copy-start.1
  14.6 0.1 shard_map.63
  14.7 0.2 collective-permute-start.3
  14.9 1.1 %collective-permute-start.4 = (f32[5,3,16,128]{3,2,1,0:T(8,128)S(1)}, f32[5,3,16,128]{3,2,1,0:T(8,128)S(1)}, u32[]{:S(2)}, u32[]{:S(2)}) collective-permute-start(f32[5,3,16,128]{3,2,1,0:T(8,128)S(1)} %get-tuple-element.15), channel_id=1, source_target_pairs={{0,2},{2,4},{4,6},{6,8},{8,10},{10,12},{12,14},{14,16},{16,18},{18... | collective-permute-start | bytes 368648 | tf_op jit(solution)/shard_map/ppermute | solution.py:232
  16.1 4.5 %collective-permute-start.5 = (f32[5,3,16,128]{3,2,1,0:T(8,128)S(1)}, f32[5,3,16,128]{3,2,1,0:T(8,128)S(1)}, u32[]{:S(2)}, u32[]{:S(2)}) collective-permute-start(f32[5,3,16,128]{3,2,1,0:T(8,128)S(1)} %get-tuple-element.16), channel_id=1, source_target_pairs={{2,0},{4,2},{6,4},{8,6},{10,8},{12,10},{14,12},{16,14},{18,16},{20... | collective-permute-start | bytes 368648 | tf_op jit(solution)/shard_map/ppermute | solution.py:233
  20.6 0.0 collective-permute-done.3.before_ref.after_ref
  20.6 0.0 copy-done.1
  20.6 2.5 %shard_map.64.partial_ref = f32[5,12,16,128]{3,2,1,0:T(8,128)S(1)} custom-call(f32[4]{0:T(128)S(1)} %maximum_multiply_fusion.coefs, f32[5,12,16,128]{3,2,1,0:T(8,128)S(1)} %get-tuple-element.14.state_ref, s32[12,16,128]{2,1,0:T(8,128)S(1)} %copy-done.3, f32[5,12,16,128]{3,2,1,0:T(8,128)S(1)} %copy-done.1, ...), custom_call_target="tpu_custom_call" | custom-call | flops 49152000 | bytes 491520 | tf_op jit(solution)/shard_map/pallas_call | solution.py:195
  23.0 1.2 %collective-permute-done.4.left_ref = f32[5,3,16,128]{3,2,1,0:T(8,128)S(1)} collective-permute-done((f32[5,3,16,128]{3,2,1,0:T(8,128)S(1)}, f32[5,3,16,128]{3,2,1,0:T(8,128)S(1)}, u32[]{:S(2)}, u32[]{:S(2)}) %collective-permute-start.4) | collective-permute-done | bytes 122912 | tf_op jit(solution)/shard_map/ppermute | solution.py:232
  24.2 0.0 collective-permute-done.5.right_ref
  24.2 0.6 %shard_map.65 = (f32[5,12,16,128]{3,2,1,0:T(8,128)S(1)}, f32[5,3,16,128]{3,2,1,0:T(8,128)S(1)}, f32[5,3,16,128]{3,2,1,0:T(8,128)S(1)}) custom-call(f32[4]{0:T(128)S(1)} %maximum_multiply_fusion.coefs, f32[5,12,16,128]{3,2,1,0:T(8,128)S(1)} %shard_map.64.partial_ref, ...), custom_call_target="tpu_custom_call", output_to_operand_aliasing={{0}: (1, {})} | custom-call | flops 491520 | bytes 737280 | tf_op jit(solution)/shard_map/pallas_call | solution.py:195
  24.9 0.1 shard_map.66
  25.0 0.1 collective-permute-start.6
  25.1 0.6 %collective-permute-start.7 = (f32[5,3,16,128]{3,2,1,0:T(8,128)S(1)}, f32[5,3,16,128]{3,2,1,0:T(8,128)S(1)}, u32[]{:S(2)}, u32[]{:S(2)}) collective-permute-start(f32[5,3,16,128]{3,2,1,0:T(8,128)S(1)} %get-tuple-element.18), channel_id=1, source_target_pairs={{0,2},{2,4},{4,6},{6,8},{8,10},{10,12},{12,14},{14,16},{16,18},{18... | collective-permute-start | bytes 368648 | tf_op jit(solution)/shard_map/ppermute | solution.py:232
  25.7 5.1 %collective-permute-start.8 = (f32[5,3,16,128]{3,2,1,0:T(8,128)S(1)}, f32[5,3,16,128]{3,2,1,0:T(8,128)S(1)}, u32[]{:S(2)}, u32[]{:S(2)}) collective-permute-start(f32[5,3,16,128]{3,2,1,0:T(8,128)S(1)} %get-tuple-element.19), channel_id=1, source_target_pairs={{2,0},{4,2},{6,4},{8,6},{10,8},{12,10},{14,12},{16,14},{18,16},{20... | collective-permute-start | bytes 368648 | tf_op jit(solution)/shard_map/ppermute | solution.py:233
  30.7 0.0 collective-permute-done.6.before_ref.after_ref
  30.7 2.5 %shard_map.67.partial_ref = f32[5,12,16,128]{3,2,1,0:T(8,128)S(1)} custom-call(f32[4]{0:T(128)S(1)} %maximum_multiply_fusion.coefs, f32[5,12,16,128]{3,2,1,0:T(8,128)S(1)} %get-tuple-element.17.state_ref, s32[12,16,128]{2,1,0:T(8,128)S(1)} %copy-done.3, f32[5,12,16,128]{3,2,1,0:T(8,128)S(1)} %copy-done.1, ...), custom_call_target="tpu_custom_call" | custom-call | flops 49152000 | bytes 491520 | tf_op jit(solution)/shard_map/pallas_call | solution.py:195
  33.2 1.3 %collective-permute-done.7.left_ref = f32[5,3,16,128]{3,2,1,0:T(8,128)S(1)} collective-permute-done((f32[5,3,16,128]{3,2,1,0:T(8,128)S(1)}, f32[5,3,16,128]{3,2,1,0:T(8,128)S(1)}, u32[]{:S(2)}, u32[]{:S(2)}) %collective-permute-start.7) | collective-permute-done | bytes 122912 | tf_op jit(solution)/shard_map/ppermute | solution.py:232
  34.5 0.0 collective-permute-done.8.right_ref
  34.5 1.5 %shard_map.68 = (f32[5,12,16,128]{3,2,1,0:T(8,128)}, f32[32,128]{1,0:T(8,128)S(1)}) custom-call(f32[4]{0:T(128)S(1)} %maximum_multiply_fusion.coefs, f32[5,12,16,128]{3,2,1,0:T(8,128)S(1)} %shard_map.67.partial_ref, f32[5,3,16,128]{3,2,1,0:T(8,128)S(1)} %collective-permute-done.7.left_ref, f32[5,3,16,128]{3,2,1,0:T(8,128)S(1)} %collective-permute-done.8.right_ref, ...), custom_call_target="tpu_custom_call" | custom-call | flops 1228800 | bytes 507904 | tf_op jit(solution)/shard_map/pallas_call | solution.py:195
  36.0 12.6 %all_to_all.11 = f32[32,1,128]{2,1,0:T(1,128)S(1)} all-to-all(f32[32,1,128]{2,1,0:T(1,128)S(1)} %bitcast.7), channel_id=1, replica_groups=mesh['gx'=16,'gy'=2] {'gx','gy'}, dimensions={0} | all-to-all | bytes 32768 | tf_op jit(solution)/shard_map/all_to_all | solution.py:266
  48.6 0.6 %shard_map.69 = f32[1,1]{1,0:T(1,128)} custom-call(f32[32,128]{1,0:T(8,128)S(1)} %bitcast.6), custom_call_target="tpu_custom_call" | custom-call | flops 1000 | bytes 4 | tf_op jit(solution)/shard_map/pallas_call | solution.py:195
  (1 shorter events, 0.0 us)
Async XLA Ops:
  0.6 1.0 %copy-start = (f32[5,12,16,128]{3,2,1,0:T(8,128)S(1)}, f32[5,12,16,128]{3,2,1,0:T(8,128)}, u32[]{:S(2)}) copy-start(f32[5,12,16,128]{3,2,1,0:T(8,128)} %start_ref.5) | copy-start | bytes 1474564
  1.7 0.9 %copy-start.2 = (s32[12,16,128]{2,1,0:T(8,128)S(1)}, s32[12,16,128]{2,1,0:T(8,128)}, u32[]{:S(2)}) copy-start(s32[12,16,128]{2,1,0:T(8,128)} %phase_ref.19) | copy-start | bytes 294916
  2.7 8.7 %collective-permute-start = (f32[5,12,8,128]{3,2,1,0:T(8,128)S(1)}, f32[5,12,8,128]{3,2,1,0:T(8,128)S(1)}, u32[]{:S(2)}, u32[]{:S(2)}) collective-permute-start(f32[5,12,8,128]{3,2,1,0:T(8,128)S(1)} %shard_map.59), channel_id=1, source_target_pairs={{0,1},{1,0},{2,3},{3,2},{4,5},{5,4},{6,7},{7,6},{8,9},{9,8},{10,11... | collective-permute-start | bytes 737288 | tf_op jit(solution)/shard_map/ppermute | solution.py:235
  3.3 10.6 %collective-permute-start.1 = (f32[5,3,16,128]{3,2,1,0:T(8,128)S(1)}, f32[5,3,16,128]{3,2,1,0:T(8,128)S(1)}, u32[]{:S(2)}, u32[]{:S(2)}) collective-permute-start(f32[5,3,16,128]{3,2,1,0:T(8,128)S(1)} %get-tuple-element.12), channel_id=1, source_target_pairs={{0,2},{2,4},{4,6},{6,8},{8,10},{10,12},{12,14},{14,16},{16,18},{18... | collective-permute-start | bytes 368648 | tf_op jit(solution)/shard_map/ppermute | solution.py:232
  5.8 8.1 %collective-permute-start.2 = (f32[5,3,16,128]{3,2,1,0:T(8,128)S(1)}, f32[5,3,16,128]{3,2,1,0:T(8,128)S(1)}, u32[]{:S(2)}, u32[]{:S(2)}) collective-permute-start(f32[5,3,16,128]{3,2,1,0:T(8,128)S(1)} %get-tuple-element.13), channel_id=1, source_target_pairs={{2,0},{4,2},{6,4},{8,6},{10,8},{12,10},{14,12},{16,14},{18,16},{20... | collective-permute-start | bytes 368648 | tf_op jit(solution)/shard_map/ppermute | solution.py:233
  11.4 2.5 %copy-start.3 = (s32[12,16,128]{2,1,0:T(8,128)S(1)}, s32[12,16,128]{2,1,0:T(8,128)}, u32[]{:S(2)}) copy-start(s32[12,16,128]{2,1,0:T(8,128)} %phase_ref.19) | copy-start | bytes 294916
  14.6 6.0 %copy-start.1 = (f32[5,12,16,128]{3,2,1,0:T(8,128)S(1)}, f32[5,12,16,128]{3,2,1,0:T(8,128)}, u32[]{:S(2)}) copy-start(f32[5,12,16,128]{3,2,1,0:T(8,128)} %start_ref.5) | copy-start | bytes 1474564
  14.7 5.9 %collective-permute-start.3 = (f32[5,12,8,128]{3,2,1,0:T(8,128)S(1)}, f32[5,12,8,128]{3,2,1,0:T(8,128)S(1)}, u32[]{:S(2)}, u32[]{:S(2)}) collective-permute-start(f32[5,12,8,128]{3,2,1,0:T(8,128)S(1)} %shard_map.63), channel_id=1, source_target_pairs={{0,1},{1,0},{2,3},{3,2},{4,5},{5,4},{6,7},{7,6},{8,9},{9,8},{10,11... | collective-permute-start | bytes 737288 | tf_op jit(solution)/shard_map/ppermute | solution.py:235
  14.9 9.3 %collective-permute-start.4 = (f32[5,3,16,128]{3,2,1,0:T(8,128)S(1)}, f32[5,3,16,128]{3,2,1,0:T(8,128)S(1)}, u32[]{:S(2)}, u32[]{:S(2)}) collective-permute-start(f32[5,3,16,128]{3,2,1,0:T(8,128)S(1)} %get-tuple-element.15), channel_id=1, source_target_pairs={{0,2},{2,4},{4,6},{6,8},{8,10},{10,12},{12,14},{14,16},{16,18},{18... | collective-permute-start | bytes 368648 | tf_op jit(solution)/shard_map/ppermute | solution.py:232
  16.1 8.1 %collective-permute-start.5 = (f32[5,3,16,128]{3,2,1,0:T(8,128)S(1)}, f32[5,3,16,128]{3,2,1,0:T(8,128)S(1)}, u32[]{:S(2)}, u32[]{:S(2)}) collective-permute-start(f32[5,3,16,128]{3,2,1,0:T(8,128)S(1)} %get-tuple-element.16), channel_id=1, source_target_pairs={{2,0},{4,2},{6,4},{8,6},{10,8},{12,10},{14,12},{16,14},{18,16},{20... | collective-permute-start | bytes 368648 | tf_op jit(solution)/shard_map/ppermute | solution.py:233
  25.0 5.8 %collective-permute-start.6 = (f32[5,12,8,128]{3,2,1,0:T(8,128)S(1)}, f32[5,12,8,128]{3,2,1,0:T(8,128)S(1)}, u32[]{:S(2)}, u32[]{:S(2)}) collective-permute-start(f32[5,12,8,128]{3,2,1,0:T(8,128)S(1)} %shard_map.66), channel_id=1, source_target_pairs={{0,1},{1,0},{2,3},{3,2},{4,5},{5,4},{6,7},{7,6},{8,9},{9,8},{10,11... | collective-permute-start | bytes 737288 | tf_op jit(solution)/shard_map/ppermute | solution.py:235
  25.1 9.4 %collective-permute-start.7 = (f32[5,3,16,128]{3,2,1,0:T(8,128)S(1)}, f32[5,3,16,128]{3,2,1,0:T(8,128)S(1)}, u32[]{:S(2)}, u32[]{:S(2)}) collective-permute-start(f32[5,3,16,128]{3,2,1,0:T(8,128)S(1)} %get-tuple-element.18), channel_id=1, source_target_pairs={{0,2},{2,4},{4,6},{6,8},{8,10},{10,12},{12,14},{14,16},{16,18},{18... | collective-permute-start | bytes 368648 | tf_op jit(solution)/shard_map/ppermute | solution.py:232
  25.7 8.8 %collective-permute-start.8 = (f32[5,3,16,128]{3,2,1,0:T(8,128)S(1)}, f32[5,3,16,128]{3,2,1,0:T(8,128)S(1)}, u32[]{:S(2)}, u32[]{:S(2)}) collective-permute-start(f32[5,3,16,128]{3,2,1,0:T(8,128)S(1)} %get-tuple-element.19), channel_id=1, source_target_pairs={{2,0},{4,2},{6,4},{8,6},{10,8},{12,10},{14,12},{16,14},{18,16},{20... | collective-permute-start | bytes 368648 | tf_op jit(solution)/shard_map/ppermute | solution.py:233

commit v3 on v2

--- a/solution.py
+++ b/solution.py
@@ -7,6 +7,7 @@
 from jax.experimental import pallas as pl
 from jax.experimental.pallas import tpu as pltpu
 from jax.sharding import PartitionSpec as P
+
 
 PERIOD = 64
 
@@ -28,6 +29,7 @@
 TILE = 8
 VMEM = pl.BlockSpec(memory_space=pltpu.VMEM)
 SMEM = pl.BlockSpec(memory_space=pltpu.SMEM)
+HBM = pl.BlockSpec(memory_space=pltpu.HBM)
 
 
 def point(state, phase):
@@ -56,18 +58,24 @@
     return [ref[member, index] for member in range(5)]
 
 
-def edge_fluxes(state_ref, phase_ref, last_ref, leading_ref):
+def edge_kernel(state_ref, phase_ref, last_ref, leading_ref, planes, phases, semaphores):
     length = state_ref.shape[1]
-    for target, start in ((last_ref, length - WIDTH), (leading_ref, 0)):
+    sides = ((last_ref, length - WIDTH), (leading_ref, 0))
+    copies = []
+    for side, (_, start) in enumerate(sides):
+        near = pl.ds(start, WIDTH)
+        copies.append(pltpu.make_async_copy(state_ref.at[:, near], planes.at[side], semaphores.at[2 * side]))
+        copies.append(pltpu.make_async_copy(phase_ref.at[near], phases.at[side], semaphores.at[2 * side + 1]))
+    for copy in copies:
+        copy.start()
+    for side, (target, _) in enumerate(sides):
+        copies[2 * side].wait()
+        copies[2 * side + 1].wait()
         for k in range(WIDTH):
-            state = plane(state_ref, start + k)
-            velocity, press_now, *_ = point(state, phase_ref[start + k])
+            state = [planes[side, member, k] for member in range(5)]
+            velocity, press_now, *_ = point(state, phases[side, k])
             for member, piece in enumerate(flux(state, velocity, press_now, 0)):
                 target[member, k] = piece
-
-
-def edge_kernel(state_ref, phase_ref, last_ref, leading_ref):
-    edge_fluxes(state_ref, phase_ref, last_ref, leading_ref)
 
 
 def rows_kernel(state_ref, phase_ref, rows_ref):
@@ -89,8 +97,9 @@
     lax.fori_loop(0, state_ref.shape[1], body, 0, unroll=2)
 
 
-def middle_kernel(weights, first, coefs, state_ref, phase_ref, start_ref, before_ref, after_ref, out_ref, xs, ys, zs):
+def middle_kernel(weights, first, final, coefs, state_ref, phase_ref, start_ref, before_ref, after_ref, out_ref, *rest):
     length, rows, lanes = phase_ref.shape
+    xs, ys, zs = rest[-3:]
     blank = jnp.zeros((rows, lanes), jnp.float32)
     for member in range(5):
         for k in range(WIDTH):
@@ -140,44 +149,64 @@
         return carry
 
     lax.fori_loop(0, length, update, 0)
-
-
-def add_halo(share, coefs, partial_ref, left_ref, right_ref, out_ref):
+    if final:
+
+        def fastest(index, largest):
+            return jnp.maximum(largest, wave_speed(plane(out_ref, index), phase_ref[index]))
+
+        rest[0][...] = lax.fori_loop(WIDTH, length - WIDTH, fastest, blank)
+
+
+def with_halo(share, coefs, partial_ref, left_ref, right_ref):
     length = partial_ref.shape[1]
     steps = [coefs[k] * share for k in range(3)]
-    for member in range(5):
-        for near in range(WIDTH):
-            left = partial_ref[member, near]
-            right = partial_ref[member, length - 1 - near]
-            for k in range(near + 1, WIDTH + 1):
-                left = left + steps[k - 1] * left_ref[member, WIDTH + near - k]
-                right = right - steps[k - 1] * right_ref[member, k - 1 - near]
-            out_ref[member, near] = left
-            out_ref[member, length - 1 - near] = right
+    for near in range(WIDTH):
+        left = plane(partial_ref, near)
+        right = plane(partial_ref, length - 1 - near)
+        for k in range(near + 1, WIDTH + 1):
+            left = [v + steps[k - 1] * left_ref[m, WIDTH + near - k] for m, v in enumerate(left)]
+            right = [v - steps[k - 1] * right_ref[m, k - 1 - near] for m, v in enumerate(right)]
+        yield near, 0, near, left
+        yield length - 1 - near, 1, WIDTH - 1 - near, right
 
 
 def join_kernel(share, coefs, partial_ref, left_ref, right_ref, phase_ref, out_ref, last_ref, leading_ref):
-    add_halo(share, coefs, partial_ref, left_ref, right_ref, out_ref)
-    edge_fluxes(out_ref, phase_ref, last_ref, leading_ref)
-
-
-def final_kernel(share, coefs, partial_ref, left_ref, right_ref, phase_ref, out_ref, peak_ref):
-    length, rows, lanes = phase_ref.shape
-    add_halo(share, coefs, partial_ref, left_ref, right_ref, out_ref)
-    for index in range(WIDTH, length - WIDTH):
+    for index, side, place, state in with_halo(share, coefs, partial_ref, left_ref, right_ref):
+        velocity, press_now, *_ = point(state, phase_ref[index])
+        target = last_ref if side else leading_ref
+        for member, piece in enumerate(flux(state, velocity, press_now, 0)):
+            target[member, place] = piece
         for member in range(5):
-            out_ref[member, index] = partial_ref[member, index]
-
-    def body(index, largest):
-        state = plane(out_ref, index)
-        velocity, press_now, inverse, gamma_cell, pinf_cell = point(state, phase_ref[index])
-        speed = jnp.abs(velocity[0]) + jnp.abs(velocity[1]) + jnp.abs(velocity[2])
-        speed = speed + 3.0 * jnp.sqrt(gamma_cell * (press_now + pinf_cell) * inverse)
-        return jnp.maximum(largest, speed)
-
-    largest = lax.fori_loop(0, length, body, jnp.zeros((rows, lanes), jnp.float32), unroll=2)
+            out_ref[member, index] = state[member]
+
+
+def wave_speed(state, phase):
+    velocity, press_now, inverse, gamma_cell, pinf_cell = point(state, phase)
+    speed = jnp.abs(velocity[0]) + jnp.abs(velocity[1]) + jnp.abs(velocity[2])
+    return speed + 3.0 * jnp.sqrt(gamma_cell * (press_now + pinf_cell) * inverse)
+
+
+def final_kernel(
+    share, coefs, partial_ref, left_ref, right_ref, phase_ref, inner_ref, out_ref, peak_ref, edges, semaphores
+):
+    length = partial_ref.shape[1]
+    inner = pl.ds(WIDTH, length - 2 * WIDTH)
+    copies = [pltpu.make_async_copy(partial_ref.at[:, inner], out_ref.at[:, inner], semaphores.at[0])]
+    copies[0].start()
+    largest = inner_ref[...]
+    for index, side, place, state in with_halo(share, coefs, partial_ref, left_ref, right_ref):
+        for member in range(5):
+            edges[side, member, place] = state[member]
+        largest = jnp.maximum(largest, wave_speed(state, phase_ref[index]))
+    for side, start in enumerate((0, length - WIDTH)):
+        copies.append(
+            pltpu.make_async_copy(edges.at[side], out_ref.at[:, pl.ds(start, WIDTH)], semaphores.at[1 + side])
+        )
+        copies[-1].start()
     largest = jnp.max(largest, axis=0, keepdims=True)
     peak_ref[...] = jnp.broadcast_to(largest, peak_ref.shape)
+    for copy in copies:
+        copy.wait()
 
 
 def peak_kernel(peaks_ref, largest_ref):
@@ -189,14 +218,13 @@
     return jax.ShapeDtypeStruct(shape, jnp.float32)
 
 
-def call(kernel, outs, specs, args, *, flops, scratch=(), aliases=None):
+def call(kernel, outs, specs, args, *, flops, scratch=(), aliases=None, places=None):
     moved = 4 * sum(math.prod(o.shape) for o in outs)
-    several = len(outs) > 1
     return pl.pallas_call(
         kernel,
-        out_shape=list(outs) if several else outs[0],
+        out_shape=list(outs),
         in_specs=specs,
-        out_specs=[VMEM] * len(outs) if several else VMEM,
+        out_specs=places or [VMEM] * len(outs),
         scratch_shapes=list(scratch),
         input_output_aliases=aliases or {},
         cost_estimate=pl.CostEstimate(flops=flops, bytes_accessed=moved, transcendentals=0),
@@ -225,18 +253,28 @@
 
     state = fields
     last, leading = call(
-        edge_kernel, [edge, edge], [VMEM, VMEM], [state, phase_map], flops=cells * 20
+        edge_kernel,
+        [edge, edge],
+        [HBM, HBM],
+        [pltpu.with_memory_space_constraint(array, pltpu.HBM) for array in (state, phase_map)],
+        flops=cells * 20,
+        scratch=[
+            pltpu.VMEM((2, 5, WIDTH, rows, lanes), jnp.float32),
+            pltpu.VMEM((2, WIDTH, rows, lanes), jnp.int32),
+            pltpu.SemaphoreType.DMA((4,)),
+        ],
     )
     stages = ((0.0, 1.0), (0.75, 0.25), (one_third, two_thirds))
     for number, weights in enumerate(stages):
         left = lax.ppermute(last, "gx", up)
         right = lax.ppermute(leading, "gx", down)
-        sent = call(rows_kernel, [row_tile], [VMEM, VMEM], [state, phase_map], flops=cells * 10)
+        (sent,) = call(rows_kernel, [row_tile], [VMEM, VMEM], [state, phase_map], flops=cells * 10)
         before = lax.ppermute(sent, "gy", over)
         after = before if across == 2 else lax.ppermute(sent, "gy", back)
-        partial = call(
-            functools.partial(middle_kernel, weights, number == 0),
-            [whole],
+        final = number == 2
+        partial, *inner = call(
+            functools.partial(middle_kernel, weights, number == 0, final),
+            [whole, shaped(rows, lanes)] if final else [whole],
             [SMEM] + [VMEM] * 5,
             [coefs, state, phase_map, fields, before, after],
             flops=cells * 2000,
@@ -246,7 +284,7 @@
                 pltpu.VMEM((5, length, rows, lanes), jnp.float32),
             ],
         )
-        if number < 2:
+        if not final:
             state, last, leading = call(
                 functools.partial(join_kernel, weights[1]),
                 [whole, edge, edge],
@@ -259,12 +297,17 @@
             advanced, peak = call(
                 functools.partial(final_kernel, weights[1]),
                 [whole, shaped(along * across, lanes)],
-                [SMEM] + [VMEM] * 4,
-                [coefs, partial, left, right, phase_map],
+                [SMEM] + [VMEM] * 5,
+                [coefs, partial, left, right, phase_map, *inner],
                 flops=cells * 50,
+                places=[HBM, VMEM],
+                scratch=[
+                    pltpu.VMEM((2, 5, WIDTH, rows, lanes), jnp.float32),
+                    pltpu.SemaphoreType.DMA((3,)),
+                ],
             )
     peaks = lax.all_to_all(peak, ("gx", "gy"), 0, 0, tiled=True)
-    largest = call(peak_kernel, [shaped(1, 1)], [VMEM], [peaks], flops=1000)
+    (largest,) = call(peak_kernel, [shaped(1, 1)], [VMEM], [peaks], flops=1000)
     return (advanced, jnp.reshape(largest, (1,)))
 
 

time: 49.4 us -> 50.3 us (1.018)
  Pallas kernels: 11.2 us -> 12.2 us
    pallas_call x11, Pallas kernels: 11.2 us -> 12.2 us  [call(): pl.pallas_call(kernel, out_shape=list(outs), in_specs=specs, out_specs=pl...]
  transfers between devices with their start and end apart: 9 -> 9, of which waited for: 3 -> 2; matrix products, arithmetic and copies ran while one was open for 0% -> 0% of each run, Pallas kernels for 15% -> 17%
where the time goes in v3:
time: 50.3 us; the launch traced here: 50.1 us
  starting transfers between devices  18.8 us (37%)
  blocking collectives  12.6 us (25%)
  Pallas kernels  12.2 us (24%)
  waiting for transfers between devices  2.29 us (5%)
  between operations  2.17 us (4%)
  local copies, waits for them, and re-layouts  1.93 us (4%)
    ppermute x3, starting transfers between devices, local(): right = lax.ppermute(leading, 'gx', down)  13.7 us
    all_to_all x1, blocking collectives, local(): peaks = lax.all_to_all(peak, ('gx', 'gy'), 0, 0, tiled=True)  12.6 us
    pallas_call x11, Pallas kernels, call(): pl.pallas_call(kernel, out_shape=list(outs), in_specs=specs, out_specs=pl...  12.2 us
    ppermute x3, starting transfers between devices, local(): left = lax.ppermute(last, 'gx', up)  4.28 us
    ppermute x3, waiting for transfers between devices, local(): left = lax.ppermute(last, 'gx', up)  2.28 us
    unnamed x8, local copies, waits for them, and re-layouts  1.93 us
  transfers between devices with their start and end apart: 9, of which 2 were waited for; matrix products, arithmetic and copies ran while one was open for 0% of the time, Pallas kernels for 17%

profile of v3, /device:TPU:0, one launch (start us, length us, event | category | flops | bytes accessed | tf_op | source)
XLA Modules:
  0.0 50.1 jit_solution(8125945766704522306)
XLA Ops:
  0.6 0.0 copy-start
  0.6 1.0 %copy-done = f32[5,12,16,128]{3,2,1,0:T(8,128)S(1)} copy-done((f32[5,12,16,128]{3,2,1,0:T(8,128)S(1)}, f32[5,12,16,128]{3,2,1,0:T(8,128)}, u32[]{:S(2)}) %copy-start) | copy-done | bytes 491544
  1.7 0.0 copy-start.2
  1.7 0.9 %copy-done.2 = s32[12,16,128]{2,1,0:T(8,128)S(1)} copy-done((s32[12,16,128]{2,1,0:T(8,128)S(1)}, s32[12,16,128]{2,1,0:T(8,128)}, u32[]{:S(2)}) %copy-start.2) | copy-done | bytes 98328
  2.6 0.1 shard_map.59
  2.7 0.0 copy-start.1
  2.7 0.0 copy-start.3
  2.7 0.6 %collective-permute-start = (f32[5,12,8,128]{3,2,1,0:T(8,128)S(1)}, f32[5,12,8,128]{3,2,1,0:T(8,128)S(1)}, u32[]{:S(2)}, u32[]{:S(2)}) collective-permute-start(f32[5,12,8,128]{3,2,1,0:T(8,128)S(1)} %shard_map.59), channel_id=1, source_target_pairs={{0,1},{1,0},{2,3},{3,2},{4,5},{5,4},{6,7},{7,6},{8,9},{9,8},{10,11... | collective-permute-start | bytes 737288 | tf_op jit(solution)/shard_map/ppermute | solution.py:272
  3.3 1.0 %shard_map.61 = (f32[5,3,16,128]{3,2,1,0:T(8,128)S(1)}, f32[5,3,16,128]{3,2,1,0:T(8,128)S(1)}) custom-call(f32[5,12,16,128]{3,2,1,0:T(8,128)} %start_ref.5, s32[12,16,128]{2,1,0:T(8,128)} %phase_ref.19), custom_call_target="tpu_custom_call" | custom-call | flops 491520 | bytes 245760 | tf_op jit(solution)/shard_map/pallas_call | solution.py:223
  4.3 2.6 %collective-permute-start.1 = (f32[5,3,16,128]{3,2,1,0:T(8,128)S(1)}, f32[5,3,16,128]{3,2,1,0:T(8,128)S(1)}, u32[]{:S(2)}, u32[]{:S(2)}) collective-permute-start(f32[5,3,16,128]{3,2,1,0:T(8,128)S(1)} %get-tuple-element.14), channel_id=1, source_target_pairs={{0,2},{2,4},{4,6},{6,8},{8,10},{10,12},{12,14},{14,16},{16,18},{18... | collective-permute-start | bytes 368648 | tf_op jit(solution)/shard_map/ppermute | solution.py:269
  6.9 4.1 %collective-permute-start.2 = (f32[5,3,16,128]{3,2,1,0:T(8,128)S(1)}, f32[5,3,16,128]{3,2,1,0:T(8,128)S(1)}, u32[]{:S(2)}, u32[]{:S(2)}) collective-permute-start(f32[5,3,16,128]{3,2,1,0:T(8,128)S(1)} %get-tuple-element.15), channel_id=1, source_target_pairs={{2,0},{4,2},{6,4},{8,6},{10,8},{12,10},{14,12},{16,14},{18,16},{20... | collective-permute-start | bytes 368648 | tf_op jit(solution)/shard_map/ppermute | solution.py:270
  12.4 0.1 maximum_multiply_fusion.coefs
  12.5 0.0 collective-permute-done.before_ref.after_ref
  12.5 0.0 copy-done.1
  12.5 0.0 copy-done.3
  12.5 2.4 %shard_map.60.partial_ref = f32[5,12,16,128]{3,2,1,0:T(8,128)S(1)} custom-call(f32[4]{0:T(128)S(1)} %maximum_multiply_fusion.coefs, f32[5,12,16,128]{3,2,1,0:T(8,128)S(1)} %copy-done.1, s32[12,16,128]{2,1,0:T(8,128)S(1)} %copy-done.3, f32[5,12,16,128]{3,2,1,0:T(8,128)S(1)} %copy-done.1, f32[5,12,8,128]{3,2,1,0:T(8,128)S(1)} %collective-permute-done.before_ref.after_ref, ...), custom_call_target="tpu_custom_call" | custom-call | flops 49152000 | bytes 491520 | tf_op jit(solution)/shard_map/pallas_call | solution.py:223
  14.9 0.0 collective-permute-done.1.left_ref
  14.9 0.0 collective-permute-done.2.right_ref
  14.9 0.7 %shard_map.62 = (f32[5,12,16,128]{3,2,1,0:T(8,128)S(1)}, f32[5,3,16,128]{3,2,1,0:T(8,128)S(1)}, f32[5,3,16,128]{3,2,1,0:T(8,128)S(1)}) custom-call(f32[4]{0:T(128)S(1)} %maximum_multiply_fusion.coefs, f32[5,12,16,128]{3,2,1,0:T(8,128)S(1)} %shard_map.60.partial_ref, ...), custom_call_target="tpu_custom_call", output_to_operand_aliasing={{0}: (1, {})} | custom-call | flops 491520 | bytes 737280 | tf_op jit(solution)/shard_map/pallas_call | solution.py:223
  15.6 0.1 shard_map.63
  15.8 0.2 collective-permute-start.3
  16.0 1.1 %collective-permute-start.4 = (f32[5,3,16,128]{3,2,1,0:T(8,128)S(1)}, f32[5,3,16,128]{3,2,1,0:T(8,128)S(1)}, u32[]{:S(2)}, u32[]{:S(2)}) collective-permute-start(f32[5,3,16,128]{3,2,1,0:T(8,128)S(1)} %get-tuple-element.17), channel_id=1, source_target_pairs={{0,2},{2,4},{4,6},{6,8},{8,10},{10,12},{12,14},{14,16},{16,18},{18... | collective-permute-start | bytes 368648 | tf_op jit(solution)/shard_map/ppermute | solution.py:269
  17.1 4.5 %collective-permute-start.5 = (f32[5,3,16,128]{3,2,1,0:T(8,128)S(1)}, f32[5,3,16,128]{3,2,1,0:T(8,128)S(1)}, u32[]{:S(2)}, u32[]{:S(2)}) collective-permute-start(f32[5,3,16,128]{3,2,1,0:T(8,128)S(1)} %get-tuple-element.18), channel_id=1, source_target_pairs={{2,0},{4,2},{6,4},{8,6},{10,8},{12,10},{14,12},{16,14},{18,16},{20... | collective-permute-start | bytes 368648 | tf_op jit(solution)/shard_map/ppermute | solution.py:270
  21.6 0.0 collective-permute-done.3.before_ref.after_ref
  21.6 2.5 %shard_map.64.partial_ref = f32[5,12,16,128]{3,2,1,0:T(8,128)S(1)} custom-call(f32[4]{0:T(128)S(1)} %maximum_multiply_fusion.coefs, f32[5,12,16,128]{3,2,1,0:T(8,128)S(1)} %get-tuple-element.16.state_ref, s32[12,16,128]{2,1,0:T(8,128)S(1)} %copy-done.3, f32[5,12,16,128]{3,2,1,0:T(8,128)S(1)} %copy-done.1, ...), custom_call_target="tpu_custom_call" | custom-call | flops 49152000 | bytes 491520 | tf_op jit(solution)/shard_map/pallas_call | solution.py:223
  24.1 1.2 %collective-permute-done.4.left_ref = f32[5,3,16,128]{3,2,1,0:T(8,128)S(1)} collective-permute-done((f32[5,3,16,128]{3,2,1,0:T(8,128)S(1)}, f32[5,3,16,128]{3,2,1,0:T(8,128)S(1)}, u32[]{:S(2)}, u32[]{:S(2)}) %collective-permute-start.4) | collective-permute-done | bytes 122912 | tf_op jit(solution)/shard_map/ppermute | solution.py:269
  25.3 0.0 collective-permute-done.5.right_ref
  25.3 0.7 %shard_map.65 = (f32[5,12,16,128]{3,2,1,0:T(8,128)S(1)}, f32[5,3,16,128]{3,2,1,0:T(8,128)S(1)}, f32[5,3,16,128]{3,2,1,0:T(8,128)S(1)}) custom-call(f32[4]{0:T(128)S(1)} %maximum_multiply_fusion.coefs, f32[5,12,16,128]{3,2,1,0:T(8,128)S(1)} %shard_map.64.partial_ref, ...), custom_call_target="tpu_custom_call", output_to_operand_aliasing={{0}: (1, {})} | custom-call | flops 491520 | bytes 737280 | tf_op jit(solution)/shard_map/pallas_call | solution.py:223
  25.9 0.1 shard_map.66
  26.1 0.1 collective-permute-start.6
  26.1 0.6 %collective-permute-start.7 = (f32[5,3,16,128]{3,2,1,0:T(8,128)S(1)}, f32[5,3,16,128]{3,2,1,0:T(8,128)S(1)}, u32[]{:S(2)}, u32[]{:S(2)}) collective-permute-start(f32[5,3,16,128]{3,2,1,0:T(8,128)S(1)} %get-tuple-element.21), channel_id=1, source_target_pairs={{0,2},{2,4},{4,6},{6,8},{8,10},{10,12},{12,14},{14,16},{16,18},{18... | collective-permute-start | bytes 368648 | tf_op jit(solution)/shard_map/ppermute | solution.py:269
  26.7 5.1 %collective-permute-start.8 = (f32[5,3,16,128]{3,2,1,0:T(8,128)S(1)}, f32[5,3,16,128]{3,2,1,0:T(8,128)S(1)}, u32[]{:S(2)}, u32[]{:S(2)}) collective-permute-start(f32[5,3,16,128]{3,2,1,0:T(8,128)S(1)} %get-tuple-element.22), channel_id=1, source_target_pairs={{2,0},{4,2},{6,4},{8,6},{10,8},{12,10},{14,12},{16,14},{18,16},{20... | collective-permute-start | bytes 368648 | tf_op jit(solution)/shard_map/ppermute | solution.py:270
  31.8 0.0 collective-permute-done.6.before_ref.after_ref
  31.8 2.6 %shard_map.67 = (f32[5,12,16,128]{3,2,1,0:T(8,128)S(1)}, f32[16,128]{1,0:T(8,128)S(1)}) custom-call(f32[4]{0:T(128)S(1)} %maximum_multiply_fusion.coefs, f32[5,12,16,128]{3,2,1,0:T(8,128)S(1)} %get-tuple-element.19.state_ref, s32[12,16,128]{2,1,0:T(8,128)S(1)} %copy-done.3, f32[5,12,16,128]{3,2,1,0:T(8,128)S(1)} %copy-done.1, ...), custom_call_target="tpu_custom_call" | custom-call | flops 49152000 | bytes 499712 | tf_op jit(solution)/shard_map/pallas_call | solution.py:223
  34.5 1.1 %collective-permute-done.7.left_ref = f32[5,3,16,128]{3,2,1,0:T(8,128)S(1)} collective-permute-done((f32[5,3,16,128]{3,2,1,0:T(8,128)S(1)}, f32[5,3,16,128]{3,2,1,0:T(8,128)S(1)}, u32[]{:S(2)}, u32[]{:S(2)}) %collective-permute-start.7) | collective-permute-done | bytes 122912 | tf_op jit(solution)/shard_map/ppermute | solution.py:269
  35.6 0.0 collective-permute-done.8.right_ref
  35.6 1.3 %shard_map.68 = (f32[5,12,16,128]{3,2,1,0:T(8,128)}, f32[32,128]{1,0:T(8,128)S(1)}) custom-call(f32[4]{0:T(128)S(1)} %maximum_multiply_fusion.coefs, f32[5,12,16,128]{3,2,1,0:T(8,128)S(1)} %get-tuple-element.20.partial_ref, f32[5,3,16,128]{3,2,1,0:T(8,128)S(1)} %collective-permute-done.7.left_ref, f32[5,3,16,128]{3,2,1,0:T(8,128)S(1)} %collective-permute-done.8.right_ref, ...), custom_call_target="tpu_custom_call" | custom-call | flops 1228800 | bytes 507904 | tf_op jit(solution)/shard_map/pallas_call | solution.py:223
  36.9 12.6 %all_to_all.11 = f32[32,1,128]{2,1,0:T(1,128)S(1)} all-to-all(f32[32,1,128]{2,1,0:T(1,128)S(1)} %bitcast.7), channel_id=1, replica_groups=mesh['gx'=16,'gy'=2] {'gx','gy'}, dimensions={0} | all-to-all | bytes 32768 | tf_op jit(solution)/shard_map/all_to_all | solution.py:309
  49.5 0.6 %shard_map.69 = f32[1,1]{1,0:T(1,128)} custom-call(f32[32,128]{1,0:T(8,128)S(1)} %bitcast.6), custom_call_target="tpu_custom_call" | custom-call | flops 1000 | bytes 4 | tf_op jit(solution)/shard_map/pallas_call | solution.py:223
Async XLA Ops:
  0.6 1.0 %copy-start = (f32[5,12,16,128]{3,2,1,0:T(8,128)S(1)}, f32[5,12,16,128]{3,2,1,0:T(8,128)}, u32[]{:S(2)}) copy-start(f32[5,12,16,128]{3,2,1,0:T(8,128)} %start_ref.5) | copy-start | bytes 1474564
  1.7 0.9 %copy-start.2 = (s32[12,16,128]{2,1,0:T(8,128)S(1)}, s32[12,16,128]{2,1,0:T(8,128)}, u32[]{:S(2)}) copy-start(s32[12,16,128]{2,1,0:T(8,128)} %phase_ref.19) | copy-start | bytes 294916
  2.7 9.8 %copy-start.1 = (f32[5,12,16,128]{3,2,1,0:T(8,128)S(1)}, f32[5,12,16,128]{3,2,1,0:T(8,128)}, u32[]{:S(2)}) copy-start(f32[5,12,16,128]{3,2,1,0:T(8,128)} %start_ref.5) | copy-start | bytes 1474564
  2.7 9.8 %copy-start.3 = (s32[12,16,128]{2,1,0:T(8,128)S(1)}, s32[12,16,128]{2,1,0:T(8,128)}, u32[]{:S(2)}) copy-start(s32[12,16,128]{2,1,0:T(8,128)} %phase_ref.19) | copy-start | bytes 294916
  2.7 9.8 %collective-permute-start = (f32[5,12,8,128]{3,2,1,0:T(8,128)S(1)}, f32[5,12,8,128]{3,2,1,0:T(8,128)S(1)}, u32[]{:S(2)}, u32[]{:S(2)}) collective-permute-start(f32[5,12,8,128]{3,2,1,0:T(8,128)S(1)} %shard_map.59), channel_id=1, source_target_pairs={{0,1},{1,0},{2,3},{3,2},{4,5},{5,4},{6,7},{7,6},{8,9},{9,8},{10,11... | collective-permute-start | bytes 737288 | tf_op jit(solution)/shard_map/ppermute | solution.py:272
  4.3 10.6 %collective-permute-start.1 = (f32[5,3,16,128]{3,2,1,0:T(8,128)S(1)}, f32[5,3,16,128]{3,2,1,0:T(8,128)S(1)}, u32[]{:S(2)}, u32[]{:S(2)}) collective-permute-start(f32[5,3,16,128]{3,2,1,0:T(8,128)S(1)} %get-tuple-element.14), channel_id=1, source_target_pairs={{0,2},{2,4},{4,6},{6,8},{8,10},{10,12},{12,14},{14,16},{16,18},{18... | collective-permute-start | bytes 368648 | tf_op jit(solution)/shard_map/ppermute | solution.py:269
  6.9 8.0 %collective-permute-start.2 = (f32[5,3,16,128]{3,2,1,0:T(8,128)S(1)}, f32[5,3,16,128]{3,2,1,0:T(8,128)S(1)}, u32[]{:S(2)}, u32[]{:S(2)}) collective-permute-start(f32[5,3,16,128]{3,2,1,0:T(8,128)S(1)} %get-tuple-element.15), channel_id=1, source_target_pairs={{2,0},{4,2},{6,4},{8,6},{10,8},{12,10},{14,12},{16,14},{18,16},{20... | collective-permute-start | bytes 368648 | tf_op jit(solution)/shard_map/ppermute | solution.py:270
  15.8 5.9 %collective-permute-start.3 = (f32[5,12,8,128]{3,2,1,0:T(8,128)S(1)}, f32[5,12,8,128]{3,2,1,0:T(8,128)S(1)}, u32[]{:S(2)}, u32[]{:S(2)}) collective-permute-start(f32[5,12,8,128]{3,2,1,0:T(8,128)S(1)} %shard_map.63), channel_id=1, source_target_pairs={{0,1},{1,0},{2,3},{3,2},{4,5},{5,4},{6,7},{7,6},{8,9},{9,8},{10,11... | collective-permute-start | bytes 737288 | tf_op jit(solution)/shard_map/ppermute | solution.py:272
  16.0 9.3 %collective-permute-start.4 = (f32[5,3,16,128]{3,2,1,0:T(8,128)S(1)}, f32[5,3,16,128]{3,2,1,0:T(8,128)S(1)}, u32[]{:S(2)}, u32[]{:S(2)}) collective-permute-start(f32[5,3,16,128]{3,2,1,0:T(8,128)S(1)} %get-tuple-element.17), channel_id=1, source_target_pairs={{0,2},{2,4},{4,6},{6,8},{8,10},{10,12},{12,14},{14,16},{16,18},{18... | collective-permute-start | bytes 368648 | tf_op jit(solution)/shard_map/ppermute | solution.py:269
  17.1 8.2 %collective-permute-start.5 = (f32[5,3,16,128]{3,2,1,0:T(8,128)S(1)}, f32[5,3,16,128]{3,2,1,0:T(8,128)S(1)}, u32[]{:S(2)}, u32[]{:S(2)}) collective-permute-start(f32[5,3,16,128]{3,2,1,0:T(8,128)S(1)} %get-tuple-element.18), channel_id=1, source_target_pairs={{2,0},{4,2},{6,4},{8,6},{10,8},{12,10},{14,12},{16,14},{18,16},{20... | collective-permute-start | bytes 368648 | tf_op jit(solution)/shard_map/ppermute | solution.py:270
  26.1 5.8 %collective-permute-start.6 = (f32[5,12,8,128]{3,2,1,0:T(8,128)S(1)}, f32[5,12,8,128]{3,2,1,0:T(8,128)S(1)}, u32[]{:S(2)}, u32[]{:S(2)}) collective-permute-start(f32[5,12,8,128]{3,2,1,0:T(8,128)S(1)} %shard_map.66), channel_id=1, source_target_pairs={{0,1},{1,0},{2,3},{3,2},{4,5},{5,4},{6,7},{7,6},{8,9},{9,8},{10,11... | collective-permute-start | bytes 737288 | tf_op jit(solution)/shard_map/ppermute | solution.py:272
  26.1 9.4 %collective-permute-start.7 = (f32[5,3,16,128]{3,2,1,0:T(8,128)S(1)}, f32[5,3,16,128]{3,2,1,0:T(8,128)S(1)}, u32[]{:S(2)}, u32[]{:S(2)}) collective-permute-start(f32[5,3,16,128]{3,2,1,0:T(8,128)S(1)} %get-tuple-element.21), channel_id=1, source_target_pairs={{0,2},{2,4},{4,6},{6,8},{8,10},{10,12},{12,14},{14,16},{16,18},{18... | collective-permute-start | bytes 368648 | tf_op jit(solution)/shard_map/ppermute | solution.py:269
  26.7 8.9 %collective-permute-start.8 = (f32[5,3,16,128]{3,2,1,0:T(8,128)S(1)}, f32[5,3,16,128]{3,2,1,0:T(8,128)S(1)}, u32[]{:S(2)}, u32[]{:S(2)}) collective-permute-start(f32[5,3,16,128]{3,2,1,0:T(8,128)S(1)} %get-tuple-element.22), channel_id=1, source_target_pairs={{2,0},{4,2},{6,4},{8,6},{10,8},{12,10},{14,12},{16,14},{18,16},{20... | collective-permute-start | bytes 368648 | tf_op jit(solution)/shard_map/ppermute | solution.py:270

commit v4 on v3

--- a/solution.py
+++ b/solution.py
@@ -28,7 +28,6 @@
 WIDTH = 3
 TILE = 8
 VMEM = pl.BlockSpec(memory_space=pltpu.VMEM)
-SMEM = pl.BlockSpec(memory_space=pltpu.SMEM)
 HBM = pl.BlockSpec(memory_space=pltpu.HBM)
 
 
@@ -242,6 +241,7 @@
     coefs = time_step * jnp.stack(
         [jnp.float32(coef_one), jnp.float32(coef_two), jnp.float32(coef_three), gravity_now]
     )
+    coefs = jnp.broadcast_to(coefs[:, None, None], (4, rows, lanes))
     along, across = lax.axis_size("gx"), lax.axis_size("gy")
     up = [(i, (i + 1) % along) for i in range(along)]
     down = [(j, i) for i, j in up]
@@ -275,7 +275,7 @@
         partial, *inner = call(
             functools.partial(middle_kernel, weights, number == 0, final),
             [whole, shaped(rows, lanes)] if final else [whole],
-            [SMEM] + [VMEM] * 5,
+            [VMEM] * 6,
             [coefs, state, phase_map, fields, before, after],
             flops=cells * 2000,
             scratch=[
@@ -288,7 +288,7 @@
             state, last, leading = call(
                 functools.partial(join_kernel, weights[1]),
                 [whole, edge, edge],
-                [SMEM] + [VMEM] * 4,
+                [VMEM] * 5,
                 [coefs, partial, left, right, phase_map],
                 flops=cells * 20,
                 aliases={1: 0},
@@ -297,7 +297,7 @@
             advanced, peak = call(
                 functools.partial(final_kernel, weights[1]),
                 [whole, shaped(along * across, lanes)],
-                [SMEM] + [VMEM] * 5,
+                [VMEM] * 6,
                 [coefs, partial, left, right, phase_map, *inner],
                 flops=cells * 50,
                 places=[HBM, VMEM],

time: 50.3 us -> 48.7 us (0.968)
  Pallas kernels: 12.2 us -> 9.07 us
  waiting for transfers between devices: 2.29 us -> 3.92 us
    pallas_call x11, Pallas kernels: 12.2 us -> 9.07 us  [call(): pl.pallas_call(kernel, out_shape=list(outs), in_specs=specs, out_specs=pl...]
    ppermute x3, waiting for transfers between devices: 2.28 us -> 3.9 us  [local(): left = lax.ppermute(last, 'gx', up)]
  transfers between devices with their start and end apart: 9 -> 9, of which waited for: 2 -> 3; matrix products, arithmetic and copies ran while one was open for 0% -> 0% of each run, Pallas kernels for 17% -> 15%
where the time goes in v4:
time: 48.7 us; the launch traced here: 48.5 us
  starting transfers between devices  18.7 us (38%)
  blocking collectives  12.6 us (26%)
  Pallas kernels  9.07 us (19%)
  waiting for transfers between devices  3.92 us (8%)
  between operations  2.16 us (4%)
  local copies, waits for them, and re-layouts  2 us (4%)
    ppermute x3, starting transfers between devices, local(): right = lax.ppermute(leading, 'gx', down)  13.5 us
    all_to_all x1, blocking collectives, local(): peaks = lax.all_to_all(peak, ('gx', 'gy'), 0, 0, tiled=True)  12.6 us
    pallas_call x11, Pallas kernels, call(): pl.pallas_call(kernel, out_shape=list(outs), in_specs=specs, out_specs=pl...  9.07 us
    ppermute x3, starting transfers between devices, local(): left = lax.ppermute(last, 'gx', up)  4.45 us
    ppermute x3, waiting for transfers between devices, local(): left = lax.ppermute(last, 'gx', up)  3.9 us
    unnamed x8, local copies, waits for them, and re-layouts  1.93 us
  transfers between devices with their start and end apart: 9, of which 3 were waited for; matrix products, arithmetic and copies ran while one was open for 0% of the time, Pallas kernels for 15%

profile of v4, /device:TPU:0, one launch (start us, length us, event | category | flops | bytes accessed | tf_op | source)
XLA Modules:
  0.0 48.5 jit_solution(13740037296281185078)
XLA Ops:
  0.6 0.0 copy-start
  0.6 1.0 %copy-done = f32[5,12,16,128]{3,2,1,0:T(8,128)S(1)} copy-done((f32[5,12,16,128]{3,2,1,0:T(8,128)S(1)}, f32[5,12,16,128]{3,2,1,0:T(8,128)}, u32[]{:S(2)}) %copy-start) | copy-done | bytes 491544
  1.7 0.0 copy-start.2
  1.7 0.9 %copy-done.2 = s32[12,16,128]{2,1,0:T(8,128)S(1)} copy-done((s32[12,16,128]{2,1,0:T(8,128)S(1)}, s32[12,16,128]{2,1,0:T(8,128)}, u32[]{:S(2)}) %copy-start.2) | copy-done | bytes 98328
  2.6 0.1 shard_map.59
  2.7 0.0 copy-start.1
  2.7 0.6 %collective-permute-start = (f32[5,12,8,128]{3,2,1,0:T(8,128)S(1)}, f32[5,12,8,128]{3,2,1,0:T(8,128)S(1)}, u32[]{:S(2)}, u32[]{:S(2)}) collective-permute-start(f32[5,12,8,128]{3,2,1,0:T(8,128)S(1)} %shard_map.59), channel_id=1, source_target_pairs={{0,1},{1,0},{2,3},{3,2},{4,5},{5,4},{6,7},{7,6},{8,9},{9,8},{10,11... | collective-permute-start | bytes 737288 | tf_op jit(solution)/shard_map/ppermute | solution.py:272
  3.2 0.0 copy-start.3
  3.3 1.1 %shard_map.61 = (f32[5,3,16,128]{3,2,1,0:T(8,128)S(1)}, f32[5,3,16,128]{3,2,1,0:T(8,128)S(1)}) custom-call(f32[5,12,16,128]{3,2,1,0:T(8,128)} %start_ref.5, s32[12,16,128]{2,1,0:T(8,128)} %phase_ref.19), custom_call_target="tpu_custom_call" | custom-call | flops 491520 | bytes 245760 | tf_op jit(solution)/shard_map/pallas_call | solution.py:222
  4.3 2.6 %collective-permute-start.1 = (f32[5,3,16,128]{3,2,1,0:T(8,128)S(1)}, f32[5,3,16,128]{3,2,1,0:T(8,128)S(1)}, u32[]{:S(2)}, u32[]{:S(2)}) collective-permute-start(f32[5,3,16,128]{3,2,1,0:T(8,128)S(1)} %get-tuple-element.14), channel_id=1, source_target_pairs={{0,2},{2,4},{4,6},{6,8},{8,10},{10,12},{12,14},{14,16},{16,18},{18... | collective-permute-start | bytes 368648 | tf_op jit(solution)/shard_map/ppermute | solution.py:269
  6.9 4.1 %collective-permute-start.2 = (f32[5,3,16,128]{3,2,1,0:T(8,128)S(1)}, f32[5,3,16,128]{3,2,1,0:T(8,128)S(1)}, u32[]{:S(2)}, u32[]{:S(2)}) collective-permute-start(f32[5,3,16,128]{3,2,1,0:T(8,128)S(1)} %get-tuple-element.15), channel_id=1, source_target_pairs={{2,0},{4,2},{6,4},{8,6},{10,8},{12,10},{14,12},{16,14},{18,16},{20... | collective-permute-start | bytes 368648 | tf_op jit(solution)/shard_map/ppermute | solution.py:270
  12.4 0.1 maximum_multiply_fusion
  12.5 0.0 collective-permute-done.before_ref.after_ref
  12.5 0.1 broadcast_in_dim.2.coefs
  12.5 0.0 copy-done.1
  12.5 0.0 copy-done.3
  12.5 1.9 %shard_map.60.partial_ref = f32[5,12,16,128]{3,2,1,0:T(8,128)S(1)} custom-call(f32[4,16,128]{2,1,0:T(8,128)S(1)} %broadcast_in_dim.2.coefs, f32[5,12,16,128]{3,2,1,0:T(8,128)S(1)} %copy-done.1, s32[12,16,128]{2,1,0:T(8,128)S(1)} %copy-done.3, f32[5,12,16,128]{3,2,1,0:T(8,128)S(1)} %copy-done.1, ...), custom_call_target="tpu_custom_call" | custom-call | flops 49152000 | bytes 491520 | tf_op jit(solution)/shard_map/pallas_call | solution.py:222
  14.4 0.5 %collective-permute-done.1.left_ref = f32[5,3,16,128]{3,2,1,0:T(8,128)S(1)} collective-permute-done((f32[5,3,16,128]{3,2,1,0:T(8,128)S(1)}, f32[5,3,16,128]{3,2,1,0:T(8,128)S(1)}, u32[]{:S(2)}, u32[]{:S(2)}) %collective-permute-start.1) | collective-permute-done | bytes 122912 | tf_op jit(solution)/shard_map/ppermute | solution.py:269
  15.0 0.0 collective-permute-done.2.right_ref
  15.0 0.1 shard_map.62
  15.1 0.1 shard_map.63
  15.2 0.1 collective-permute-start.3
  15.3 1.3 %collective-permute-start.4 = (f32[5,3,16,128]{3,2,1,0:T(8,128)S(1)}, f32[5,3,16,128]{3,2,1,0:T(8,128)S(1)}, u32[]{:S(2)}, u32[]{:S(2)}) collective-permute-start(f32[5,3,16,128]{3,2,1,0:T(8,128)S(1)} %get-tuple-element.17), channel_id=1, source_target_pairs={{0,2},{2,4},{4,6},{6,8},{8,10},{10,12},{12,14},{14,16},{16,18},{18... | collective-permute-start | bytes 368648 | tf_op jit(solution)/shard_map/ppermute | solution.py:269
  16.6 4.4 %collective-permute-start.5 = (f32[5,3,16,128]{3,2,1,0:T(8,128)S(1)}, f32[5,3,16,128]{3,2,1,0:T(8,128)S(1)}, u32[]{:S(2)}, u32[]{:S(2)}) collective-permute-start(f32[5,3,16,128]{3,2,1,0:T(8,128)S(1)} %get-tuple-element.18), channel_id=1, source_target_pairs={{2,0},{4,2},{6,4},{8,6},{10,8},{12,10},{14,12},{16,14},{18,16},{20... | collective-permute-start | bytes 368648 | tf_op jit(solution)/shard_map/ppermute | solution.py:270
  21.0 0.0 collective-permute-done.3.before_ref.after_ref
  21.0 1.9 %shard_map.64.partial_ref = f32[5,12,16,128]{3,2,1,0:T(8,128)S(1)} custom-call(f32[4,16,128]{2,1,0:T(8,128)S(1)} %broadcast_in_dim.2.coefs, f32[5,12,16,128]{3,2,1,0:T(8,128)S(1)} %get-tuple-element.16.state_ref, s32[12,16,128]{2,1,0:T(8,128)S(1)} %copy-done.3, f32[5,12,16,128]{3,2,1,0:T(8,128)S(1)} %copy-done.1, ...), custom_call_target="tpu_custom_call" | custom-call | flops 49152000 | bytes 491520 | tf_op jit(solution)/shard_map/pallas_call | solution.py:222
  22.9 1.8 %collective-permute-done.4.left_ref = f32[5,3,16,128]{3,2,1,0:T(8,128)S(1)} collective-permute-done((f32[5,3,16,128]{3,2,1,0:T(8,128)S(1)}, f32[5,3,16,128]{3,2,1,0:T(8,128)S(1)}, u32[]{:S(2)}, u32[]{:S(2)}) %collective-permute-start.4) | collective-permute-done | bytes 122912 | tf_op jit(solution)/shard_map/ppermute | solution.py:269
  24.7 0.0 collective-permute-done.5.right_ref
  24.7 0.1 shard_map.65
  24.9 0.1 shard_map.66
  25.0 0.1 collective-permute-start.6
  25.1 0.6 %collective-permute-start.7 = (f32[5,3,16,128]{3,2,1,0:T(8,128)S(1)}, f32[5,3,16,128]{3,2,1,0:T(8,128)S(1)}, u32[]{:S(2)}, u32[]{:S(2)}) collective-permute-start(f32[5,3,16,128]{3,2,1,0:T(8,128)S(1)} %get-tuple-element.21), channel_id=1, source_target_pairs={{0,2},{2,4},{4,6},{6,8},{8,10},{10,12},{12,14},{14,16},{16,18},{18... | collective-permute-start | bytes 368648 | tf_op jit(solution)/shard_map/ppermute | solution.py:269
  25.7 5.1 %collective-permute-start.8 = (f32[5,3,16,128]{3,2,1,0:T(8,128)S(1)}, f32[5,3,16,128]{3,2,1,0:T(8,128)S(1)}, u32[]{:S(2)}, u32[]{:S(2)}) collective-permute-start(f32[5,3,16,128]{3,2,1,0:T(8,128)S(1)} %get-tuple-element.22), channel_id=1, source_target_pairs={{2,0},{4,2},{6,4},{8,6},{10,8},{12,10},{14,12},{16,14},{18,16},{20... | collective-permute-start | bytes 368648 | tf_op jit(solution)/shard_map/ppermute | solution.py:270
  30.7 0.0 collective-permute-done.6.before_ref.after_ref
  30.7 2.1 %shard_map.67 = (f32[5,12,16,128]{3,2,1,0:T(8,128)S(1)}, f32[16,128]{1,0:T(8,128)S(1)}) custom-call(f32[4,16,128]{2,1,0:T(8,128)S(1)} %broadcast_in_dim.2.coefs, f32[5,12,16,128]{3,2,1,0:T(8,128)S(1)} %get-tuple-element.19.state_ref, s32[12,16,128]{2,1,0:T(8,128)S(1)} %copy-done.3, f32[5,12,16,128]{3,2,1,0:T(8,128)S(1)} %copy-done.1, ...), custom_call_target="tpu_custom_call" | custom-call | flops 49152000 | bytes 499712 | tf_op jit(solution)/shard_map/pallas_call | solution.py:222
  32.9 1.6 %collective-permute-done.7.left_ref = f32[5,3,16,128]{3,2,1,0:T(8,128)S(1)} collective-permute-done((f32[5,3,16,128]{3,2,1,0:T(8,128)S(1)}, f32[5,3,16,128]{3,2,1,0:T(8,128)S(1)}, u32[]{:S(2)}, u32[]{:S(2)}) %collective-permute-start.7) | collective-permute-done | bytes 122912 | tf_op jit(solution)/shard_map/ppermute | solution.py:269
  34.5 0.0 collective-permute-done.8.right_ref
  34.5 0.8 %shard_map.68 = (f32[5,12,16,128]{3,2,1,0:T(8,128)}, f32[32,128]{1,0:T(8,128)S(1)}) custom-call(f32[4,16,128]{2,1,0:T(8,128)S(1)} %broadcast_in_dim.2.coefs, f32[5,12,16,128]{3,2,1,0:T(8,128)S(1)} %get-tuple-element.20.partial_ref, f32[5,3,16,128]{3,2,1,0:T(8,128)S(1)} %collective-permute-done.7.left_ref, ...), custom_call_target="tpu_custom_call" | custom-call | flops 1228800 | bytes 507904 | tf_op jit(solution)/shard_map/pallas_call | solution.py:222
  35.3 12.6 %all_to_all.11 = f32[32,1,128]{2,1,0:T(1,128)S(1)} all-to-all(f32[32,1,128]{2,1,0:T(1,128)S(1)} %bitcast.7), channel_id=1, replica_groups=mesh['gx'=16,'gy'=2] {'gx','gy'}, dimensions={0} | all-to-all | bytes 32768 | tf_op jit(solution)/shard_map/all_to_all | solution.py:309
  47.9 0.6 %shard_map.69 = f32[1,1]{1,0:T(1,128)} custom-call(f32[32,128]{1,0:T(8,128)S(1)} %bitcast.6), custom_call_target="tpu_custom_call" | custom-call | flops 1000 | bytes 4 | tf_op jit(solution)/shard_map/pallas_call | solution.py:222
Async XLA Ops:
  0.6 1.0 %copy-start = (f32[5,12,16,128]{3,2,1,0:T(8,128)S(1)}, f32[5,12,16,128]{3,2,1,0:T(8,128)}, u32[]{:S(2)}) copy-start(f32[5,12,16,128]{3,2,1,0:T(8,128)} %start_ref.5) | copy-start | bytes 1474564
  1.7 0.9 %copy-start.2 = (s32[12,16,128]{2,1,0:T(8,128)S(1)}, s32[12,16,128]{2,1,0:T(8,128)}, u32[]{:S(2)}) copy-start(s32[12,16,128]{2,1,0:T(8,128)} %phase_ref.19) | copy-start | bytes 294916
  2.7 9.9 %copy-start.1 = (f32[5,12,16,128]{3,2,1,0:T(8,128)S(1)}, f32[5,12,16,128]{3,2,1,0:T(8,128)}, u32[]{:S(2)}) copy-start(f32[5,12,16,128]{3,2,1,0:T(8,128)} %start_ref.5) | copy-start | bytes 1474564
  2.7 9.8 %collective-permute-start = (f32[5,12,8,128]{3,2,1,0:T(8,128)S(1)}, f32[5,12,8,128]{3,2,1,0:T(8,128)S(1)}, u32[]{:S(2)}, u32[]{:S(2)}) collective-permute-start(f32[5,12,8,128]{3,2,1,0:T(8,128)S(1)} %shard_map.59), channel_id=1, source_target_pairs={{0,1},{1,0},{2,3},{3,2},{4,5},{5,4},{6,7},{7,6},{8,9},{9,8},{10,11... | collective-permute-start | bytes 737288 | tf_op jit(solution)/shard_map/ppermute | solution.py:272
  3.2 9.3 %copy-start.3 = (s32[12,16,128]{2,1,0:T(8,128)S(1)}, s32[12,16,128]{2,1,0:T(8,128)}, u32[]{:S(2)}) copy-start(s32[12,16,128]{2,1,0:T(8,128)} %phase_ref.19) | copy-start | bytes 294916
  4.3 10.6 %collective-permute-start.1 = (f32[5,3,16,128]{3,2,1,0:T(8,128)S(1)}, f32[5,3,16,128]{3,2,1,0:T(8,128)S(1)}, u32[]{:S(2)}, u32[]{:S(2)}) collective-permute-start(f32[5,3,16,128]{3,2,1,0:T(8,128)S(1)} %get-tuple-element.14), channel_id=1, source_target_pairs={{0,2},{2,4},{4,6},{6,8},{8,10},{10,12},{12,14},{14,16},{16,18},{18... | collective-permute-start | bytes 368648 | tf_op jit(solution)/shard_map/ppermute | solution.py:269
  6.9 8.1 %collective-permute-start.2 = (f32[5,3,16,128]{3,2,1,0:T(8,128)S(1)}, f32[5,3,16,128]{3,2,1,0:T(8,128)S(1)}, u32[]{:S(2)}, u32[]{:S(2)}) collective-permute-start(f32[5,3,16,128]{3,2,1,0:T(8,128)S(1)} %get-tuple-element.15), channel_id=1, source_target_pairs={{2,0},{4,2},{6,4},{8,6},{10,8},{12,10},{14,12},{16,14},{18,16},{20... | collective-permute-start | bytes 368648 | tf_op jit(solution)/shard_map/ppermute | solution.py:270
  15.2 5.8 %collective-permute-start.3 = (f32[5,12,8,128]{3,2,1,0:T(8,128)S(1)}, f32[5,12,8,128]{3,2,1,0:T(8,128)S(1)}, u32[]{:S(2)}, u32[]{:S(2)}) collective-permute-start(f32[5,12,8,128]{3,2,1,0:T(8,128)S(1)} %shard_map.63), channel_id=1, source_target_pairs={{0,1},{1,0},{2,3},{3,2},{4,5},{5,4},{6,7},{7,6},{8,9},{9,8},{10,11... | collective-permute-start | bytes 737288 | tf_op jit(solution)/shard_map/ppermute | solution.py:272
  15.3 9.4 %collective-permute-start.4 = (f32[5,3,16,128]{3,2,1,0:T(8,128)S(1)}, f32[5,3,16,128]{3,2,1,0:T(8,128)S(1)}, u32[]{:S(2)}, u32[]{:S(2)}) collective-permute-start(f32[5,3,16,128]{3,2,1,0:T(8,128)S(1)} %get-tuple-element.17), channel_id=1, source_target_pairs={{0,2},{2,4},{4,6},{6,8},{8,10},{10,12},{12,14},{14,16},{16,18},{18... | collective-permute-start | bytes 368648 | tf_op jit(solution)/shard_map/ppermute | solution.py:269
  16.6 8.1 %collective-permute-start.5 = (f32[5,3,16,128]{3,2,1,0:T(8,128)S(1)}, f32[5,3,16,128]{3,2,1,0:T(8,128)S(1)}, u32[]{:S(2)}, u32[]{:S(2)}) collective-permute-start(f32[5,3,16,128]{3,2,1,0:T(8,128)S(1)} %get-tuple-element.18), channel_id=1, source_target_pairs={{2,0},{4,2},{6,4},{8,6},{10,8},{12,10},{14,12},{16,14},{18,16},{20... | collective-permute-start | bytes 368648 | tf_op jit(solution)/shard_map/ppermute | solution.py:270
  25.0 5.8 %collective-permute-start.6 = (f32[5,12,8,128]{3,2,1,0:T(8,128)S(1)}, f32[5,12,8,128]{3,2,1,0:T(8,128)S(1)}, u32[]{:S(2)}, u32[]{:S(2)}) collective-permute-start(f32[5,12,8,128]{3,2,1,0:T(8,128)S(1)} %shard_map.66), channel_id=1, source_target_pairs={{0,1},{1,0},{2,3},{3,2},{4,5},{5,4},{6,7},{7,6},{8,9},{9,8},{10,11... | collective-permute-start | bytes 737288 | tf_op jit(solution)/shard_map/ppermute | solution.py:272
  25.1 9.4 %collective-permute-start.7 = (f32[5,3,16,128]{3,2,1,0:T(8,128)S(1)}, f32[5,3,16,128]{3,2,1,0:T(8,128)S(1)}, u32[]{:S(2)}, u32[]{:S(2)}) collective-permute-start(f32[5,3,16,128]{3,2,1,0:T(8,128)S(1)} %get-tuple-element.21), channel_id=1, source_target_pairs={{0,2},{2,4},{4,6},{6,8},{8,10},{10,12},{12,14},{14,16},{16,18},{18... | collective-permute-start | bytes 368648 | tf_op jit(solution)/shard_map/ppermute | solution.py:269
  25.7 8.8 %collective-permute-start.8 = (f32[5,3,16,128]{3,2,1,0:T(8,128)S(1)}, f32[5,3,16,128]{3,2,1,0:T(8,128)S(1)}, u32[]{:S(2)}, u32[]{:S(2)}) collective-permute-start(f32[5,3,16,128]{3,2,1,0:T(8,128)S(1)} %get-tuple-element.22), channel_id=1, source_target_pairs={{2,0},{4,2},{6,4},{8,6},{10,8},{12,10},{14,12},{16,14},{18,16},{20... | collective-permute-start | bytes 368648 | tf_op jit(solution)/shard_map/ppermute | solution.py:270

commit v5 on v4

--- a/solution.py
+++ b/solution.py
@@ -25,6 +25,11 @@
 one_third = 1.0 / 3.0
 two_thirds = 2.0 / 3.0
 
+STAGES = (
+    (("up", "down"), (0.0, 1.0)),
+    (("down", "up"), (0.75, 0.25)),
+    (("up", "down"), (one_third, two_thirds)),
+)
 WIDTH = 3
 TILE = 8
 VMEM = pl.BlockSpec(memory_space=pltpu.VMEM)
@@ -156,25 +161,23 @@
         rest[0][...] = lax.fori_loop(WIDTH, length - WIDTH, fastest, blank)
 
 
-def with_halo(share, coefs, partial_ref, left_ref, right_ref):
+def with_halo(share, coefs, partial_ref, halo_ref, above):
     length = partial_ref.shape[1]
-    steps = [coefs[k] * share for k in range(3)]
+    steps = [coefs[k] * (-share if above else share) for k in range(3)]
     for near in range(WIDTH):
-        left = plane(partial_ref, near)
-        right = plane(partial_ref, length - 1 - near)
+        index = length - 1 - near if above else near
+        state = plane(partial_ref, index)
         for k in range(near + 1, WIDTH + 1):
-            left = [v + steps[k - 1] * left_ref[m, WIDTH + near - k] for m, v in enumerate(left)]
-            right = [v - steps[k - 1] * right_ref[m, k - 1 - near] for m, v in enumerate(right)]
-        yield near, 0, near, left
-        yield length - 1 - near, 1, WIDTH - 1 - near, right
-
-
-def join_kernel(share, coefs, partial_ref, left_ref, right_ref, phase_ref, out_ref, last_ref, leading_ref):
-    for index, side, place, state in with_halo(share, coefs, partial_ref, left_ref, right_ref):
+            place = k - 1 - near if above else WIDTH + near - k
+            state = [value + steps[k - 1] * halo_ref[member, place] for member, value in enumerate(state)]
+        yield index, WIDTH - 1 - near if above else near, state
+
+
+def join_kernel(share, above, coefs, partial_ref, halo_ref, phase_ref, out_ref, edge_ref):
+    for index, place, state in with_halo(share, coefs, partial_ref, halo_ref, above):
         velocity, press_now, *_ = point(state, phase_ref[index])
-        target = last_ref if side else leading_ref
         for member, piece in enumerate(flux(state, velocity, press_now, 0)):
-            target[member, place] = piece
+            edge_ref[member, place] = piece
         for member in range(5):
             out_ref[member, index] = state[member]
 
@@ -193,10 +196,11 @@
     copies = [pltpu.make_async_copy(partial_ref.at[:, inner], out_ref.at[:, inner], semaphores.at[0])]
     copies[0].start()
     largest = inner_ref[...]
-    for index, side, place, state in with_halo(share, coefs, partial_ref, left_ref, right_ref):
-        for member in range(5):
-            edges[side, member, place] = state[member]
-        largest = jnp.maximum(largest, wave_speed(state, phase_ref[index]))
+    for side, halo_ref in enumerate((left_ref, right_ref)):
+        for index, place, state in with_halo(share, coefs, partial_ref, halo_ref, side == 1):
+            for member in range(5):
+                edges[side, member, place] = state[member]
+            largest = jnp.maximum(largest, wave_speed(state, phase_ref[index]))
     for side, start in enumerate((0, length - WIDTH)):
         copies.append(
             pltpu.make_async_copy(edges.at[side], out_ref.at[:, pl.ds(start, WIDTH)], semaphores.at[1 + side])
@@ -231,7 +235,7 @@
     )(*args)
 
 
-def local(fields, phase_map, lagged_speed, step_count):
+def advance(fields, phase_map, lagged_speed, step_count):
     _, length, rows, lanes = fields.shape
     cells = length * rows * lanes
     time_step = cfl_number / lagged_speed[0]
@@ -264,15 +268,16 @@
             pltpu.SemaphoreType.DMA((4,)),
         ],
     )
-    stages = ((0.0, 1.0), (0.75, 0.25), (one_third, two_thirds))
-    for number, weights in enumerate(stages):
-        left = lax.ppermute(last, "gx", up)
-        right = lax.ppermute(leading, "gx", down)
+    edges = {"up": last, "down": leading}
+    for number, ((first, second), weights) in enumerate(STAGES):
+        halos = {}
+        for way in (first, second):
+            halos[way] = lax.ppermute(edges[way], "gx", up if way == "up" else down)
         (sent,) = call(rows_kernel, [row_tile], [VMEM, VMEM], [state, phase_map], flops=cells * 10)
         before = lax.ppermute(sent, "gy", over)
         after = before if across == 2 else lax.ppermute(sent, "gy", back)
-        final = number == 2
-        partial, *inner = call(
+        final = number == len(STAGES) - 1
+        state, *inner = call(
             functools.partial(middle_kernel, weights, number == 0, final),
             [whole, shaped(rows, lanes)] if final else [whole],
             [VMEM] * 6,
@@ -284,21 +289,12 @@
                 pltpu.VMEM((5, length, rows, lanes), jnp.float32),
             ],
         )
-        if not final:
-            state, last, leading = call(
-                functools.partial(join_kernel, weights[1]),
-                [whole, edge, edge],
-                [VMEM] * 5,
-                [coefs, partial, left, right, phase_map],
-                flops=cells * 20,
-                aliases={1: 0},
-            )
-        else:
+        if final:
             advanced, peak = call(
                 functools.partial(final_kernel, weights[1]),
                 [whole, shaped(along * across, lanes)],
                 [VMEM] * 6,
-                [coefs, partial, left, right, phase_map, *inner],
+                [coefs, state, halos["up"], halos["down"], phase_map, *inner],
                 flops=cells * 50,
                 places=[HBM, VMEM],
                 scratch=[
@@ -306,6 +302,17 @@
                     pltpu.SemaphoreType.DMA((3,)),
                 ],
             )
+            break
+        for way in STAGES[number + 1][0]:
+            above = way == "up"
+            state, edges[way] = call(
+                functools.partial(join_kernel, weights[1], above),
+                [whole, edge],
+                [VMEM] * 4,
+                [coefs, state, halos["down" if above else "up"], phase_map],
+                flops=cells * 10,
+                aliases={1: 0},
+            )
     peaks = lax.all_to_all(peak, ("gx", "gy"), 0, 0, tiled=True)
     (largest,) = call(peak_kernel, [shaped(1, 1)], [VMEM], [peaks], flops=1000)
     return (advanced, jnp.reshape(largest, (1,)))
@@ -313,7 +320,7 @@
 
 def solution(mesh):
     return jax.shard_map(
-        local,
+        advance,
         mesh=mesh,
         in_specs=(P(None, "gx", "gy", None), P("gx", "gy", None), P(), P()),
         out_specs=(P(None, "gx", "gy", None), P()),

time: 48.7 us -> 49.8 us (1.023)
  waiting for transfers between devices: 3.92 us -> 12.7 us
  starting transfers between devices: 18.7 us -> 14.7 us
  blocking collectives: 12.6 us -> 8.87 us
    ppermute x9, waiting for transfers between devices: 3.92 us -> 12.7 us  [the longest x6 12.7 us: advance(): halos[way] = lax.ppermute(edges[way], 'gx', up if way == 'up' else down)]
    ppermute x9, starting transfers between devices: 18.7 us -> 14.7 us  [the longest x6 14 us: advance(): halos[way] = lax.ppermute(edges[way], 'gx', up if way == 'up' else down)]
    all_to_all x1, blocking collectives: 12.6 us -> 8.87 us  [advance(): peaks = lax.all_to_all(peak, ('gx', 'gy'), 0, 0, tiled=True)]
    pallas_call x11 -> x13, Pallas kernels: 9.07 us -> 9.08 us  [call(): pl.pallas_call(kernel, out_shape=list(outs), in_specs=specs, out_specs=pl...]
  transfers between devices with their start and end apart: 9 -> 9, of which waited for: 3 -> 5; matrix products, arithmetic and copies ran while one was open for 0% -> 0% of each run, Pallas kernels for 15% -> 15%
where the time goes in v5:
time: 49.8 us; the launch traced here: 49.5 us
  starting transfers between devices  14.7 us (30%)
  waiting for transfers between devices  12.7 us (26%)
  Pallas kernels  9.08 us (18%)
  blocking collectives  8.87 us (18%)
  between operations  2.17 us (4%)
  local copies, waits for them, and re-layouts  2 us (4%)
    ppermute x6, starting transfers between devices, advance(): halos[way] = lax.ppermute(edges[way], 'gx', up if way == 'up' else down)  14 us
    ppermute x6, waiting for transfers between devices, advance(): halos[way] = lax.ppermute(edges[way], 'gx', up if way == 'up' else down)  12.7 us
    pallas_call x13, Pallas kernels, call(): pl.pallas_call(kernel, out_shape=list(outs), in_specs=specs, out_specs=pl...  9.08 us
    all_to_all x1, blocking collectives, advance(): peaks = lax.all_to_all(peak, ('gx', 'gy'), 0, 0, tiled=True)  8.87 us
    unnamed x8, local copies, waits for them, and re-layouts  1.93 us
  transfers between devices with their start and end apart: 9, of which 5 were waited for; matrix products, arithmetic and copies ran while one was open for 0% of the time, Pallas kernels for 15%

profile of v5, /device:TPU:0, one launch (start us, length us, event | category | flops | bytes accessed | tf_op | source)
XLA Modules:
  0.0 49.5 jit_solution(3404311526410570054)
XLA Ops:
  0.6 0.0 copy-start
  0.6 1.0 %copy-done = f32[5,12,16,128]{3,2,1,0:T(8,128)S(1)} copy-done((f32[5,12,16,128]{3,2,1,0:T(8,128)S(1)}, f32[5,12,16,128]{3,2,1,0:T(8,128)}, u32[]{:S(2)}) %copy-start) | copy-done | bytes 491544
  1.7 0.0 copy-start.2
  1.7 0.9 %copy-done.2 = s32[12,16,128]{2,1,0:T(8,128)S(1)} copy-done((s32[12,16,128]{2,1,0:T(8,128)S(1)}, s32[12,16,128]{2,1,0:T(8,128)}, u32[]{:S(2)}) %copy-start.2) | copy-done | bytes 98328
  2.6 0.1 shard_map.59
  2.7 0.0 copy-start.1
  2.7 0.6 %collective-permute-start = (f32[5,12,8,128]{3,2,1,0:T(8,128)S(1)}, f32[5,12,8,128]{3,2,1,0:T(8,128)S(1)}, u32[]{:S(2)}, u32[]{:S(2)}) collective-permute-start(f32[5,12,8,128]{3,2,1,0:T(8,128)S(1)} %shard_map.59), channel_id=1, source_target_pairs={{0,1},{1,0},{2,3},{3,2},{4,5},{5,4},{6,7},{7,6},{8,9},{9,8},{10,11... | collective-permute-start | bytes 737288 | tf_op jit(solution)/shard_map/ppermute | solution.py:277
  3.2 0.0 copy-start.3
  3.3 1.1 %shard_map.61 = (f32[5,3,16,128]{3,2,1,0:T(8,128)S(1)}, f32[5,3,16,128]{3,2,1,0:T(8,128)S(1)}) custom-call(f32[5,12,16,128]{3,2,1,0:T(8,128)} %start_ref.5, s32[12,16,128]{2,1,0:T(8,128)} %phase_ref.23), custom_call_target="tpu_custom_call" | custom-call | flops 491520 | bytes 245760 | tf_op jit(solution)/shard_map/pallas_call | solution.py:226
  4.3 2.6 %collective-permute-start.1 = (f32[5,3,16,128]{3,2,1,0:T(8,128)S(1)}, f32[5,3,16,128]{3,2,1,0:T(8,128)S(1)}, u32[]{:S(2)}, u32[]{:S(2)}) collective-permute-start(f32[5,3,16,128]{3,2,1,0:T(8,128)S(1)} %get-tuple-element.16), channel_id=1, source_target_pairs={{0,2},{2,4},{4,6},{6,8},{8,10},{10,12},{12,14},{14,16},{16,18},{18... | collective-permute-start | bytes 368648 | tf_op jit(solution)/shard_map/ppermute | solution.py:275
  6.9 4.1 %collective-permute-start.2 = (f32[5,3,16,128]{3,2,1,0:T(8,128)S(1)}, f32[5,3,16,128]{3,2,1,0:T(8,128)S(1)}, u32[]{:S(2)}, u32[]{:S(2)}) collective-permute-start(f32[5,3,16,128]{3,2,1,0:T(8,128)S(1)} %get-tuple-element.18), channel_id=1, source_target_pairs={{2,0},{4,2},{6,4},{8,6},{10,8},{12,10},{14,12},{16,14},{18,16},{20... | collective-permute-start | bytes 368648 | tf_op jit(solution)/shard_map/ppermute | solution.py:275
  12.4 0.1 maximum_multiply_fusion
  12.5 0.0 collective-permute-done.before_ref.after_ref
  12.5 0.1 broadcast_in_dim.2.coefs
  12.5 0.0 copy-done.1
  12.5 0.0 copy-done.3
  12.5 1.9 %shard_map.60.partial_ref = f32[5,12,16,128]{3,2,1,0:T(8,128)S(1)} custom-call(f32[4,16,128]{2,1,0:T(8,128)S(1)} %broadcast_in_dim.2.coefs, f32[5,12,16,128]{3,2,1,0:T(8,128)S(1)} %copy-done.1, s32[12,16,128]{2,1,0:T(8,128)S(1)} %copy-done.3, f32[5,12,16,128]{3,2,1,0:T(8,128)S(1)} %copy-done.1, ...), custom_call_target="tpu_custom_call" | custom-call | flops 49152000 | bytes 491520 | tf_op jit(solution)/shard_map/pallas_call | solution.py:226
  14.4 0.5 %collective-permute-done.1.halo_ref = f32[5,3,16,128]{3,2,1,0:T(8,128)S(1)} collective-permute-done((f32[5,3,16,128]{3,2,1,0:T(8,128)S(1)}, f32[5,3,16,128]{3,2,1,0:T(8,128)S(1)}, u32[]{:S(2)}, u32[]{:S(2)}) %collective-permute-start.1) | collective-permute-done | bytes 122912 | tf_op jit(solution)/shard_map/ppermute | solution.py:275
  15.0 0.1 shard_map.62
  15.0 0.0 collective-permute-done.2.halo_ref
  15.0 0.1 shard_map.63
  15.1 0.1 shard_map.64
  15.2 0.1 collective-permute-start.3
  15.3 5.3 %collective-permute-start.4 = (f32[5,3,16,128]{3,2,1,0:T(8,128)S(1)}, f32[5,3,16,128]{3,2,1,0:T(8,128)S(1)}, u32[]{:S(2)}, u32[]{:S(2)}) collective-permute-start(f32[5,3,16,128]{3,2,1,0:T(8,128)S(1)} %get-tuple-element.20), channel_id=1, source_target_pairs={{2,0},{4,2},{6,4},{8,6},{10,8},{12,10},{14,12},{16,14},{18,16},{20... | collective-permute-start | bytes 368648 | tf_op jit(solution)/shard_map/ppermute | solution.py:275
  20.6 0.0 collective-permute-start.5
  20.6 0.0 collective-permute-done.3.before_ref.after_ref
  20.6 1.9 %shard_map.65.partial_ref = f32[5,12,16,128]{3,2,1,0:T(8,128)S(1)} custom-call(f32[4,16,128]{2,1,0:T(8,128)S(1)} %broadcast_in_dim.2.coefs, f32[5,12,16,128]{3,2,1,0:T(8,128)S(1)} %get-tuple-element.19.state_ref, s32[12,16,128]{2,1,0:T(8,128)S(1)} %copy-done.3, f32[5,12,16,128]{3,2,1,0:T(8,128)S(1)} %copy-done.1, ...), custom_call_target="tpu_custom_call" | custom-call | flops 49152000 | bytes 491520 | tf_op jit(solution)/shard_map/pallas_call | solution.py:226
  22.5 1.2 %collective-permute-done.4.halo_ref = f32[5,3,16,128]{3,2,1,0:T(8,128)S(1)} collective-permute-done((f32[5,3,16,128]{3,2,1,0:T(8,128)S(1)}, f32[5,3,16,128]{3,2,1,0:T(8,128)S(1)}, u32[]{:S(2)}, u32[]{:S(2)}) %collective-permute-start.4) | collective-permute-done | bytes 122912 | tf_op jit(solution)/shard_map/ppermute | solution.py:275
  23.8 0.1 shard_map.66
  23.8 5.8 %collective-permute-done.5.halo_ref = f32[5,3,16,128]{3,2,1,0:T(8,128)S(1)} collective-permute-done((f32[5,3,16,128]{3,2,1,0:T(8,128)S(1)}, f32[5,3,16,128]{3,2,1,0:T(8,128)S(1)}, u32[]{:S(2)}, u32[]{:S(2)}) %collective-permute-start.5) | collective-permute-done | bytes 122912 | tf_op jit(solution)/shard_map/ppermute | solution.py:275
  29.7 0.1 shard_map.67
  29.7 0.1 shard_map.68
  29.9 0.1 collective-permute-start.6
  29.9 0.3 collective-permute-start.8
  30.3 1.8 %collective-permute-start.7 = (f32[5,3,16,128]{3,2,1,0:T(8,128)S(1)}, f32[5,3,16,128]{3,2,1,0:T(8,128)S(1)}, u32[]{:S(2)}, u32[]{:S(2)}) collective-permute-start(f32[5,3,16,128]{3,2,1,0:T(8,128)S(1)} %get-tuple-element.25), channel_id=1, source_target_pairs={{0,2},{2,4},{4,6},{6,8},{8,10},{10,12},{12,14},{14,16},{16,18},{18... | collective-permute-start | bytes 368648 | tf_op jit(solution)/shard_map/ppermute | solution.py:275
  32.0 0.0 collective-permute-done.6.before_ref.after_ref
  32.0 2.1 %shard_map.69 = (f32[5,12,16,128]{3,2,1,0:T(8,128)S(1)}, f32[16,128]{1,0:T(8,128)S(1)}) custom-call(f32[4,16,128]{2,1,0:T(8,128)S(1)} %broadcast_in_dim.2.coefs, f32[5,12,16,128]{3,2,1,0:T(8,128)S(1)} %get-tuple-element.23.state_ref, s32[12,16,128]{2,1,0:T(8,128)S(1)} %copy-done.3, f32[5,12,16,128]{3,2,1,0:T(8,128)S(1)} %copy-done.1, ...), custom_call_target="tpu_custom_call" | custom-call | flops 49152000 | bytes 499712 | tf_op jit(solution)/shard_map/pallas_call | solution.py:226
  34.2 2.0 %collective-permute-done.8.right_ref = f32[5,3,16,128]{3,2,1,0:T(8,128)S(1)} collective-permute-done((f32[5,3,16,128]{3,2,1,0:T(8,128)S(1)}, f32[5,3,16,128]{3,2,1,0:T(8,128)S(1)}, u32[]{:S(2)}, u32[]{:S(2)}) %collective-permute-start.8) | collective-permute-done | bytes 122912 | tf_op jit(solution)/shard_map/ppermute | solution.py:275
  36.2 3.1 %collective-permute-done.7.left_ref = f32[5,3,16,128]{3,2,1,0:T(8,128)S(1)} collective-permute-done((f32[5,3,16,128]{3,2,1,0:T(8,128)S(1)}, f32[5,3,16,128]{3,2,1,0:T(8,128)S(1)}, u32[]{:S(2)}, u32[]{:S(2)}) %collective-permute-start.7) | collective-permute-done | bytes 122912 | tf_op jit(solution)/shard_map/ppermute | solution.py:275
  39.3 0.8 %shard_map.70 = (f32[5,12,16,128]{3,2,1,0:T(8,128)}, f32[32,128]{1,0:T(8,128)S(1)}) custom-call(f32[4,16,128]{2,1,0:T(8,128)S(1)} %broadcast_in_dim.2.coefs, f32[5,12,16,128]{3,2,1,0:T(8,128)S(1)} %get-tuple-element.24.partial_ref, f32[5,3,16,128]{3,2,1,0:T(8,128)S(1)} %collective-permute-done.7.left_ref, ...), custom_call_target="tpu_custom_call" | custom-call | flops 1228800 | bytes 507904 | tf_op jit(solution)/shard_map/pallas_call | solution.py:226
  40.1 8.9 %all_to_all.11 = f32[32,1,128]{2,1,0:T(1,128)S(1)} all-to-all(f32[32,1,128]{2,1,0:T(1,128)S(1)} %bitcast.7), channel_id=1, replica_groups=mesh['gx'=16,'gy'=2] {'gx','gy'}, dimensions={0} | all-to-all | bytes 32768 | tf_op jit(solution)/shard_map/all_to_all | solution.py:316
  49.0 0.6 %shard_map.71 = f32[1,1]{1,0:T(1,128)} custom-call(f32[32,128]{1,0:T(8,128)S(1)} %bitcast.6), custom_call_target="tpu_custom_call" | custom-call | flops 1000 | bytes 4 | tf_op jit(solution)/shard_map/pallas_call | solution.py:226
Async XLA Ops:
  0.6 1.0 %copy-start = (f32[5,12,16,128]{3,2,1,0:T(8,128)S(1)}, f32[5,12,16,128]{3,2,1,0:T(8,128)}, u32[]{:S(2)}) copy-start(f32[5,12,16,128]{3,2,1,0:T(8,128)} %start_ref.5) | copy-start | bytes 1474564
  1.7 0.9 %copy-start.2 = (s32[12,16,128]{2,1,0:T(8,128)S(1)}, s32[12,16,128]{2,1,0:T(8,128)}, u32[]{:S(2)}) copy-start(s32[12,16,128]{2,1,0:T(8,128)} %phase_ref.23) | copy-start | bytes 294916
  2.7 9.9 %copy-start.1 = (f32[5,12,16,128]{3,2,1,0:T(8,128)S(1)}, f32[5,12,16,128]{3,2,1,0:T(8,128)}, u32[]{:S(2)}) copy-start(f32[5,12,16,128]{3,2,1,0:T(8,128)} %start_ref.5) | copy-start | bytes 1474564
  2.7 9.8 %collective-permute-start = (f32[5,12,8,128]{3,2,1,0:T(8,128)S(1)}, f32[5,12,8,128]{3,2,1,0:T(8,128)S(1)}, u32[]{:S(2)}, u32[]{:S(2)}) collective-permute-start(f32[5,12,8,128]{3,2,1,0:T(8,128)S(1)} %shard_map.59), channel_id=1, source_target_pairs={{0,1},{1,0},{2,3},{3,2},{4,5},{5,4},{6,7},{7,6},{8,9},{9,8},{10,11... | collective-permute-start | bytes 737288 | tf_op jit(solution)/shard_map/ppermute | solution.py:277
  3.2 9.3 %copy-start.3 = (s32[12,16,128]{2,1,0:T(8,128)S(1)}, s32[12,16,128]{2,1,0:T(8,128)}, u32[]{:S(2)}) copy-start(s32[12,16,128]{2,1,0:T(8,128)} %phase_ref.23) | copy-start | bytes 294916
  4.3 10.6 %collective-permute-start.1 = (f32[5,3,16,128]{3,2,1,0:T(8,128)S(1)}, f32[5,3,16,128]{3,2,1,0:T(8,128)S(1)}, u32[]{:S(2)}, u32[]{:S(2)}) collective-permute-start(f32[5,3,16,128]{3,2,1,0:T(8,128)S(1)} %get-tuple-element.16), channel_id=1, source_target_pairs={{0,2},{2,4},{4,6},{6,8},{8,10},{10,12},{12,14},{14,16},{16,18},{18... | collective-permute-start | bytes 368648 | tf_op jit(solution)/shard_map/ppermute | solution.py:275
  6.9 8.1 %collective-permute-start.2 = (f32[5,3,16,128]{3,2,1,0:T(8,128)S(1)}, f32[5,3,16,128]{3,2,1,0:T(8,128)S(1)}, u32[]{:S(2)}, u32[]{:S(2)}) collective-permute-start(f32[5,3,16,128]{3,2,1,0:T(8,128)S(1)} %get-tuple-element.18), channel_id=1, source_target_pairs={{2,0},{4,2},{6,4},{8,6},{10,8},{12,10},{14,12},{16,14},{18,16},{20... | collective-permute-start | bytes 368648 | tf_op jit(solution)/shard_map/ppermute | solution.py:275
  15.2 5.3 %collective-permute-start.3 = (f32[5,12,8,128]{3,2,1,0:T(8,128)S(1)}, f32[5,12,8,128]{3,2,1,0:T(8,128)S(1)}, u32[]{:S(2)}, u32[]{:S(2)}) collective-permute-start(f32[5,12,8,128]{3,2,1,0:T(8,128)S(1)} %shard_map.64), channel_id=1, source_target_pairs={{0,1},{1,0},{2,3},{3,2},{4,5},{5,4},{6,7},{7,6},{8,9},{9,8},{10,11... | collective-permute-start | bytes 737288 | tf_op jit(solution)/shard_map/ppermute | solution.py:277
  15.3 8.5 %collective-permute-start.4 = (f32[5,3,16,128]{3,2,1,0:T(8,128)S(1)}, f32[5,3,16,128]{3,2,1,0:T(8,128)S(1)}, u32[]{:S(2)}, u32[]{:S(2)}) collective-permute-start(f32[5,3,16,128]{3,2,1,0:T(8,128)S(1)} %get-tuple-element.20), channel_id=1, source_target_pairs={{2,0},{4,2},{6,4},{8,6},{10,8},{12,10},{14,12},{16,14},{18,16},{20... | collective-permute-start | bytes 368648 | tf_op jit(solution)/shard_map/ppermute | solution.py:275
  20.6 9.1 %collective-permute-start.5 = (f32[5,3,16,128]{3,2,1,0:T(8,128)S(1)}, f32[5,3,16,128]{3,2,1,0:T(8,128)S(1)}, u32[]{:S(2)}, u32[]{:S(2)}) collective-permute-start(f32[5,3,16,128]{3,2,1,0:T(8,128)S(1)} %get-tuple-element.22), channel_id=1, source_target_pairs={{0,2},{2,4},{4,6},{6,8},{8,10},{10,12},{12,14},{14,16},{16,18},{18... | collective-permute-start | bytes 368648 | tf_op jit(solution)/shard_map/ppermute | solution.py:275
  29.9 2.2 %collective-permute-start.6 = (f32[5,12,8,128]{3,2,1,0:T(8,128)S(1)}, f32[5,12,8,128]{3,2,1,0:T(8,128)S(1)}, u32[]{:S(2)}, u32[]{:S(2)}) collective-permute-start(f32[5,12,8,128]{3,2,1,0:T(8,128)S(1)} %shard_map.68), channel_id=1, source_target_pairs={{0,1},{1,0},{2,3},{3,2},{4,5},{5,4},{6,7},{7,6},{8,9},{9,8},{10,11... | collective-permute-start | bytes 737288 | tf_op jit(solution)/shard_map/ppermute | solution.py:277
  29.9 6.2 %collective-permute-start.8 = (f32[5,3,16,128]{3,2,1,0:T(8,128)S(1)}, f32[5,3,16,128]{3,2,1,0:T(8,128)S(1)}, u32[]{:S(2)}, u32[]{:S(2)}) collective-permute-start(f32[5,3,16,128]{3,2,1,0:T(8,128)S(1)} %get-tuple-element.26), channel_id=1, source_target_pairs={{2,0},{4,2},{6,4},{8,6},{10,8},{12,10},{14,12},{16,14},{18,16},{20... | collective-permute-start | bytes 368648 | tf_op jit(solution)/shard_map/ppermute | solution.py:275
  30.3 9.0 %collective-permute-start.7 = (f32[5,3,16,128]{3,2,1,0:T(8,128)S(1)}, f32[5,3,16,128]{3,2,1,0:T(8,128)S(1)}, u32[]{:S(2)}, u32[]{:S(2)}) collective-permute-start(f32[5,3,16,128]{3,2,1,0:T(8,128)S(1)} %get-tuple-element.25), channel_id=1, source_target_pairs={{0,2},{2,4},{4,6},{6,8},{8,10},{10,12},{12,14},{14,16},{16,18},{18... | collective-permute-start | bytes 368648 | tf_op jit(solution)/shard_map/ppermute | solution.py:275

commit v6 on v5

--- a/solution.py
+++ b/solution.py
@@ -101,9 +101,8 @@
     lax.fori_loop(0, state_ref.shape[1], body, 0, unroll=2)
 
 
-def middle_kernel(weights, first, final, coefs, state_ref, phase_ref, start_ref, before_ref, after_ref, out_ref, *rest):
+def middle_kernel(weights, first, coefs, state_ref, phase_ref, start_ref, out_ref, xs, ys, zs):
     length, rows, lanes = phase_ref.shape
-    xs, ys, zs = rest[-3:]
     blank = jnp.zeros((rows, lanes), jnp.float32)
     for member in range(5):
         for k in range(WIDTH):
@@ -117,8 +116,8 @@
             xs[member, WIDTH + index] = piece
         for member, piece in enumerate(flux(state, velocity, press_now, 1)):
             ys[member, index, TILE : TILE + rows] = piece
-            ys[member, index, 0:TILE] = before_ref[member, index]
-            ys[member, index, TILE + rows : TILE + rows + TILE] = after_ref[member, index]
+            ys[member, index, 0:TILE] = blank[0:TILE]
+            ys[member, index, TILE + rows : TILE + rows + TILE] = blank[0:TILE]
         for member, piece in enumerate(flux(state, velocity, press_now, 2)):
             zs[member, index] = piece
         return carry
@@ -152,13 +151,37 @@
             out_ref[member, index] = value
         return carry
 
-    lax.fori_loop(0, length, update, 0)
+    lax.fori_loop(0, length, update, 0, unroll=4)
+
+
+def border_kernel(share, final, coefs, partial_ref, phase_ref, before_ref, after_ref, out_ref, *inner_ref):
+    _, length, rows, lanes = partial_ref.shape
+    place = lax.broadcasted_iota(jnp.int32, (TILE, lanes), 0)
+    blank = jnp.zeros((TILE, lanes), jnp.float32)
+    steps = [coefs[k, 0:TILE] * share for k in range(3)]
+    early = [jnp.where(place < k, steps[k - 1], blank) for k in range(1, WIDTH + 1)]
+    late = [jnp.where(place >= TILE - k, steps[k - 1], blank) for k in range(1, WIDTH + 1)]
+
+    def border(index, carry):
+        for member in range(5):
+            before, after = before_ref[member, index], after_ref[member, index]
+            first = partial_ref[member, index, 0:TILE]
+            final = partial_ref[member, index, rows - TILE : rows]
+            for k in range(1, WIDTH + 1):
+                first = first + early[k - 1] * pltpu.roll(before, k, 0)
+                final = final - late[k - 1] * pltpu.roll(after, TILE - k, 0)
+            out_ref[member, index, 0:TILE] = first
+            out_ref[member, index, rows - TILE : rows] = final
+        return carry
+
+    lax.fori_loop(0, length, border, 0, unroll=2)
     if final:
 
         def fastest(index, largest):
             return jnp.maximum(largest, wave_speed(plane(out_ref, index), phase_ref[index]))
 
-        rest[0][...] = lax.fori_loop(WIDTH, length - WIDTH, fastest, blank)
+        blank = jnp.zeros((rows, lanes), jnp.float32)
+        inner_ref[0][...] = lax.fori_loop(WIDTH, length - WIDTH, fastest, blank, unroll=2)
 
 
 def with_halo(share, coefs, partial_ref, halo_ref, above):
@@ -277,17 +300,25 @@
         before = lax.ppermute(sent, "gy", over)
         after = before if across == 2 else lax.ppermute(sent, "gy", back)
         final = number == len(STAGES) - 1
-        state, *inner = call(
-            functools.partial(middle_kernel, weights, number == 0, final),
-            [whole, shaped(rows, lanes)] if final else [whole],
-            [VMEM] * 6,
-            [coefs, state, phase_map, fields, before, after],
-            flops=cells * 2000,
+        (state,) = call(
+            functools.partial(middle_kernel, weights, number == 0),
+            [whole],
+            [VMEM] * 4,
+            [coefs, state, phase_map, fields],
+            flops=cells * 1000,
             scratch=[
                 pltpu.VMEM((5, length + 2 * WIDTH, rows, lanes), jnp.float32),
                 pltpu.VMEM((5, length, rows + 2 * TILE, lanes), jnp.float32),
                 pltpu.VMEM((5, length, rows, lanes), jnp.float32),
             ],
+        )
+        state, *inner = call(
+            functools.partial(border_kernel, weights[1], final),
+            [whole, shaped(rows, lanes)] if final else [whole],
+            [VMEM] * 5,
+            [coefs, state, phase_map, before, after],
+            flops=cells * 20,
+            aliases={1: 0},
         )
         if final:
             advanced, peak = call(

time: 49.8 us -> 49.8 us (level)
  Pallas kernels: 9.08 us -> 7.6 us
  waiting for transfers between devices: 12.7 us -> 14.1 us
    pallas_call x13 -> x16, Pallas kernels: 9.08 us -> 7.6 us  [call(): pl.pallas_call(kernel, out_shape=list(outs), in_specs=specs, out_specs=pl...]
    ppermute x6, waiting for transfers between devices: 12.7 us -> 14.1 us  [advance(): halos[way] = lax.ppermute(edges[way], 'gx', up if way == 'up' else down)]
  transfers between devices with their start and end apart: 9 -> 9, of which waited for: 5 -> 5; matrix products, arithmetic and copies ran while one was open for 0% -> 0% of each run, Pallas kernels for 15% -> 12%
where the time goes in v6:
time: 49.8 us; the launch traced here: 49.5 us
  starting transfers between devices  14.7 us (30%)
  waiting for transfers between devices  14.1 us (28%)
  blocking collectives  8.87 us (18%)
  Pallas kernels  7.6 us (15%)
  between operations  2.2 us (4%)
  local copies, waits for them, and re-layouts  2 us (4%)
    ppermute x6, waiting for transfers between devices, advance(): halos[way] = lax.ppermute(edges[way], 'gx', up if way == 'up' else down)  14.1 us
    ppermute x6, starting transfers between devices, advance(): halos[way] = lax.ppermute(edges[way], 'gx', up if way == 'up' else down)  14 us
    all_to_all x1, blocking collectives, advance(): peaks = lax.all_to_all(peak, ('gx', 'gy'), 0, 0, tiled=True)  8.87 us
    pallas_call x16, Pallas kernels, call(): pl.pallas_call(kernel, out_shape=list(outs), in_specs=specs, out_specs=pl...  7.6 us
    unnamed x8, local copies, waits for them, and re-layouts  1.93 us
  transfers between devices with their start and end apart: 9, of which 5 were waited for; matrix products, arithmetic and copies ran while one was open for 0% of the time, Pallas kernels for 12%

profile of v6, /device:TPU:0, one launch (start us, length us, event | category | flops | bytes accessed | tf_op | source)
XLA Modules:
  0.0 49.5 jit_solution(11174201924063367340)
XLA Ops:
  0.6 0.0 copy-start
  0.6 0.9 %copy-done = s32[12,16,128]{2,1,0:T(8,128)S(1)} copy-done((s32[12,16,128]{2,1,0:T(8,128)S(1)}, s32[12,16,128]{2,1,0:T(8,128)}, u32[]{:S(2)}) %copy-start) | copy-done | bytes 98328
  1.5 0.0 copy-start.2
  1.5 1.0 %copy-done.2 = f32[5,12,16,128]{3,2,1,0:T(8,128)S(1)} copy-done((f32[5,12,16,128]{3,2,1,0:T(8,128)S(1)}, f32[5,12,16,128]{3,2,1,0:T(8,128)}, u32[]{:S(2)}) %copy-start.2) | copy-done | bytes 491544
  2.6 0.1 shard_map.60
  2.7 0.0 copy-start.3
  2.7 0.6 %collective-permute-start = (f32[5,12,8,128]{3,2,1,0:T(8,128)S(1)}, f32[5,12,8,128]{3,2,1,0:T(8,128)S(1)}, u32[]{:S(2)}, u32[]{:S(2)}) collective-permute-start(f32[5,12,8,128]{3,2,1,0:T(8,128)S(1)} %shard_map.60), channel_id=1, source_target_pairs={{0,1},{1,0},{2,3},{3,2},{4,5},{5,4},{6,7},{7,6},{8,9},{9,8},{10,11... | collective-permute-start | bytes 737288 | tf_op jit(solution)/shard_map/ppermute | solution.py:300
  3.2 0.0 copy-start.1
  3.3 1.1 %shard_map.62 = (f32[5,3,16,128]{3,2,1,0:T(8,128)S(1)}, f32[5,3,16,128]{3,2,1,0:T(8,128)S(1)}) custom-call(f32[5,12,16,128]{3,2,1,0:T(8,128)} %start_ref.5, s32[12,16,128]{2,1,0:T(8,128)} %phase_ref.29), custom_call_target="tpu_custom_call" | custom-call | flops 491520 | bytes 245760 | tf_op jit(solution)/shard_map/pallas_call | solution.py:249
  4.3 2.6 %collective-permute-start.1 = (f32[5,3,16,128]{3,2,1,0:T(8,128)S(1)}, f32[5,3,16,128]{3,2,1,0:T(8,128)S(1)}, u32[]{:S(2)}, u32[]{:S(2)}) collective-permute-start(f32[5,3,16,128]{3,2,1,0:T(8,128)S(1)} %get-tuple-element.16), channel_id=1, source_target_pairs={{0,2},{2,4},{4,6},{6,8},{8,10},{10,12},{12,14},{14,16},{16,18},{18... | collective-permute-start | bytes 368648 | tf_op jit(solution)/shard_map/ppermute | solution.py:298
  6.9 4.1 %collective-permute-start.2 = (f32[5,3,16,128]{3,2,1,0:T(8,128)S(1)}, f32[5,3,16,128]{3,2,1,0:T(8,128)S(1)}, u32[]{:S(2)}, u32[]{:S(2)}) collective-permute-start(f32[5,3,16,128]{3,2,1,0:T(8,128)S(1)} %get-tuple-element.18), channel_id=1, source_target_pairs={{2,0},{4,2},{6,4},{8,6},{10,8},{12,10},{14,12},{16,14},{18,16},{20... | collective-permute-start | bytes 368648 | tf_op jit(solution)/shard_map/ppermute | solution.py:298
  12.4 0.1 maximum_multiply_fusion
  12.5 0.1 broadcast_in_dim.2.coefs
  12.5 0.0 copy-done.3
  12.5 0.0 copy-done.1
  12.5 1.2 %shard_map.59.partial_ref = f32[5,12,16,128]{3,2,1,0:T(8,128)S(1)} custom-call(f32[4,16,128]{2,1,0:T(8,128)S(1)} %broadcast_in_dim.2.coefs, f32[5,12,16,128]{3,2,1,0:T(8,128)S(1)} %copy-done.3, s32[12,16,128]{2,1,0:T(8,128)S(1)} %copy-done.1, f32[5,12,16,128]{3,2,1,0:T(8,128)S(1)} %copy-done.3), custom_call_target="tpu_custom_call" | custom-call | flops 24576000 | bytes 491520 | tf_op jit(solution)/shard_map/pallas_call | solution.py:249
  13.7 0.0 collective-permute-done.before_ref.after_ref
  13.7 0.3 shard_map.61.partial_ref
  14.0 0.9 %collective-permute-done.1.halo_ref = f32[5,3,16,128]{3,2,1,0:T(8,128)S(1)} collective-permute-done((f32[5,3,16,128]{3,2,1,0:T(8,128)S(1)}, f32[5,3,16,128]{3,2,1,0:T(8,128)S(1)}, u32[]{:S(2)}, u32[]{:S(2)}) %collective-permute-start.1) | collective-permute-done | bytes 122912 | tf_op jit(solution)/shard_map/ppermute | solution.py:298
  15.0 0.1 shard_map.63
  15.0 0.0 collective-permute-done.2.halo_ref
  15.0 0.1 shard_map.64
  15.1 0.1 shard_map.66
  15.2 0.1 collective-permute-start.3
  15.3 5.3 %collective-permute-start.4 = (f32[5,3,16,128]{3,2,1,0:T(8,128)S(1)}, f32[5,3,16,128]{3,2,1,0:T(8,128)S(1)}, u32[]{:S(2)}, u32[]{:S(2)}) collective-permute-start(f32[5,3,16,128]{3,2,1,0:T(8,128)S(1)} %get-tuple-element.20), channel_id=1, source_target_pairs={{2,0},{4,2},{6,4},{8,6},{10,8},{12,10},{14,12},{16,14},{18,16},{20... | collective-permute-start | bytes 368648 | tf_op jit(solution)/shard_map/ppermute | solution.py:298
  20.6 0.0 collective-permute-start.5
  20.6 1.2 %shard_map.65.partial_ref = f32[5,12,16,128]{3,2,1,0:T(8,128)S(1)} custom-call(f32[4,16,128]{2,1,0:T(8,128)S(1)} %broadcast_in_dim.2.coefs, f32[5,12,16,128]{3,2,1,0:T(8,128)S(1)} %get-tuple-element.19.state_ref, s32[12,16,128]{2,1,0:T(8,128)S(1)} %copy-done.1, f32[5,12,16,128]{3,2,1,0:T(8,128)S(1)} %copy-done.3), custom_call_target="tpu_custom_call" | custom-call | flops 24576000 | bytes 491520 | tf_op jit(solution)/shard_map/pallas_call | solution.py:249
  21.8 0.0 collective-permute-done.3.before_ref.after_ref
  21.8 0.3 shard_map.67.partial_ref
  22.1 1.7 %collective-permute-done.4.halo_ref = f32[5,3,16,128]{3,2,1,0:T(8,128)S(1)} collective-permute-done((f32[5,3,16,128]{3,2,1,0:T(8,128)S(1)}, f32[5,3,16,128]{3,2,1,0:T(8,128)S(1)}, u32[]{:S(2)}, u32[]{:S(2)}) %collective-permute-start.4) | collective-permute-done | bytes 122912 | tf_op jit(solution)/shard_map/ppermute | solution.py:298
  23.8 0.1 shard_map.68
  23.8 5.8 %collective-permute-done.5.halo_ref = f32[5,3,16,128]{3,2,1,0:T(8,128)S(1)} collective-permute-done((f32[5,3,16,128]{3,2,1,0:T(8,128)S(1)}, f32[5,3,16,128]{3,2,1,0:T(8,128)S(1)}, u32[]{:S(2)}, u32[]{:S(2)}) %collective-permute-start.5) | collective-permute-done | bytes 122912 | tf_op jit(solution)/shard_map/ppermute | solution.py:298
  29.7 0.1 shard_map.69
  29.7 0.1 shard_map.71
  29.9 0.1 collective-permute-start.6
  29.9 0.3 collective-permute-start.8
  30.3 1.8 %collective-permute-start.7 = (f32[5,3,16,128]{3,2,1,0:T(8,128)S(1)}, f32[5,3,16,128]{3,2,1,0:T(8,128)S(1)}, u32[]{:S(2)}, u32[]{:S(2)}) collective-permute-start(f32[5,3,16,128]{3,2,1,0:T(8,128)S(1)} %get-tuple-element.25), channel_id=1, source_target_pairs={{0,2},{2,4},{4,6},{6,8},{8,10},{10,12},{12,14},{14,16},{16,18},{18... | collective-permute-start | bytes 368648 | tf_op jit(solution)/shard_map/ppermute | solution.py:298
  32.0 1.2 %shard_map.70.partial_ref = f32[5,12,16,128]{3,2,1,0:T(8,128)S(1)} custom-call(f32[4,16,128]{2,1,0:T(8,128)S(1)} %broadcast_in_dim.2.coefs, f32[5,12,16,128]{3,2,1,0:T(8,128)S(1)} %get-tuple-element.23.state_ref, s32[12,16,128]{2,1,0:T(8,128)S(1)} %copy-done.1, f32[5,12,16,128]{3,2,1,0:T(8,128)S(1)} %copy-done.3), custom_call_target="tpu_custom_call" | custom-call | flops 24576000 | bytes 491520 | tf_op jit(solution)/shard_map/pallas_call | solution.py:249
  33.2 0.0 collective-permute-done.6.before_ref.after_ref
  33.2 0.4 shard_map.72
  33.6 2.6 %collective-permute-done.8.right_ref = f32[5,3,16,128]{3,2,1,0:T(8,128)S(1)} collective-permute-done((f32[5,3,16,128]{3,2,1,0:T(8,128)S(1)}, f32[5,3,16,128]{3,2,1,0:T(8,128)S(1)}, u32[]{:S(2)}, u32[]{:S(2)}) %collective-permute-start.8) | collective-permute-done | bytes 122912 | tf_op jit(solution)/shard_map/ppermute | solution.py:298
  36.2 3.1 %collective-permute-done.7.left_ref = f32[5,3,16,128]{3,2,1,0:T(8,128)S(1)} collective-permute-done((f32[5,3,16,128]{3,2,1,0:T(8,128)S(1)}, f32[5,3,16,128]{3,2,1,0:T(8,128)S(1)}, u32[]{:S(2)}, u32[]{:S(2)}) %collective-permute-start.7) | collective-permute-done | bytes 122912 | tf_op jit(solution)/shard_map/ppermute | solution.py:298
  39.3 0.8 %shard_map.73 = (f32[5,12,16,128]{3,2,1,0:T(8,128)}, f32[32,128]{1,0:T(8,128)S(1)}) custom-call(f32[4,16,128]{2,1,0:T(8,128)S(1)} %broadcast_in_dim.2.coefs, f32[5,12,16,128]{3,2,1,0:T(8,128)S(1)} %get-tuple-element.24.partial_ref, f32[5,3,16,128]{3,2,1,0:T(8,128)S(1)} %collective-permute-done.7.left_ref, ...), custom_call_target="tpu_custom_call" | custom-call | flops 1228800 | bytes 507904 | tf_op jit(solution)/shard_map/pallas_call | solution.py:249
  40.1 8.9 %all_to_all.11 = f32[32,1,128]{2,1,0:T(1,128)S(1)} all-to-all(f32[32,1,128]{2,1,0:T(1,128)S(1)} %bitcast.7), channel_id=1, replica_groups=mesh['gx'=16,'gy'=2] {'gx','gy'}, dimensions={0} | all-to-all | bytes 32768 | tf_op jit(solution)/shard_map/all_to_all | solution.py:347
  48.9 0.6 %shard_map.74 = f32[1,1]{1,0:T(1,128)} custom-call(f32[32,128]{1,0:T(8,128)S(1)} %bitcast.6), custom_call_target="tpu_custom_call" | custom-call | flops 1000 | bytes 4 | tf_op jit(solution)/shard_map/pallas_call | solution.py:249
Async XLA Ops:
  0.6 0.9 %copy-start = (s32[12,16,128]{2,1,0:T(8,128)S(1)}, s32[12,16,128]{2,1,0:T(8,128)}, u32[]{:S(2)}) copy-start(s32[12,16,128]{2,1,0:T(8,128)} %phase_ref.29) | copy-start | bytes 294916
  1.5 1.0 %copy-start.2 = (f32[5,12,16,128]{3,2,1,0:T(8,128)S(1)}, f32[5,12,16,128]{3,2,1,0:T(8,128)}, u32[]{:S(2)}) copy-start(f32[5,12,16,128]{3,2,1,0:T(8,128)} %start_ref.5) | copy-start | bytes 1474564
  2.7 9.9 %copy-start.3 = (f32[5,12,16,128]{3,2,1,0:T(8,128)S(1)}, f32[5,12,16,128]{3,2,1,0:T(8,128)}, u32[]{:S(2)}) copy-start(f32[5,12,16,128]{3,2,1,0:T(8,128)} %start_ref.5) | copy-start | bytes 1474564
  2.7 11.0 %collective-permute-start = (f32[5,12,8,128]{3,2,1,0:T(8,128)S(1)}, f32[5,12,8,128]{3,2,1,0:T(8,128)S(1)}, u32[]{:S(2)}, u32[]{:S(2)}) collective-permute-start(f32[5,12,8,128]{3,2,1,0:T(8,128)S(1)} %shard_map.60), channel_id=1, source_target_pairs={{0,1},{1,0},{2,3},{3,2},{4,5},{5,4},{6,7},{7,6},{8,9},{9,8},{10,11... | collective-permute-start | bytes 737288 | tf_op jit(solution)/shard_map/ppermute | solution.py:300
  3.2 9.3 %copy-start.1 = (s32[12,16,128]{2,1,0:T(8,128)S(1)}, s32[12,16,128]{2,1,0:T(8,128)}, u32[]{:S(2)}) copy-start(s32[12,16,128]{2,1,0:T(8,128)} %phase_ref.29) | copy-start | bytes 294916
  4.3 10.6 %collective-permute-start.1 = (f32[5,3,16,128]{3,2,1,0:T(8,128)S(1)}, f32[5,3,16,128]{3,2,1,0:T(8,128)S(1)}, u32[]{:S(2)}, u32[]{:S(2)}) collective-permute-start(f32[5,3,16,128]{3,2,1,0:T(8,128)S(1)} %get-tuple-element.16), channel_id=1, source_target_pairs={{0,2},{2,4},{4,6},{6,8},{8,10},{10,12},{12,14},{14,16},{16,18},{18... | collective-permute-start | bytes 368648 | tf_op jit(solution)/shard_map/ppermute | solution.py:298
  6.9 8.1 %collective-permute-start.2 = (f32[5,3,16,128]{3,2,1,0:T(8,128)S(1)}, f32[5,3,16,128]{3,2,1,0:T(8,128)S(1)}, u32[]{:S(2)}, u32[]{:S(2)}) collective-permute-start(f32[5,3,16,128]{3,2,1,0:T(8,128)S(1)} %get-tuple-element.18), channel_id=1, source_target_pairs={{2,0},{4,2},{6,4},{8,6},{10,8},{12,10},{14,12},{16,14},{18,16},{20... | collective-permute-start | bytes 368648 | tf_op jit(solution)/shard_map/ppermute | solution.py:298
  15.2 6.5 %collective-permute-start.3 = (f32[5,12,8,128]{3,2,1,0:T(8,128)S(1)}, f32[5,12,8,128]{3,2,1,0:T(8,128)S(1)}, u32[]{:S(2)}, u32[]{:S(2)}) collective-permute-start(f32[5,12,8,128]{3,2,1,0:T(8,128)S(1)} %shard_map.66), channel_id=1, source_target_pairs={{0,1},{1,0},{2,3},{3,2},{4,5},{5,4},{6,7},{7,6},{8,9},{9,8},{10,11... | collective-permute-start | bytes 737288 | tf_op jit(solution)/shard_map/ppermute | solution.py:300
  15.3 8.4 %collective-permute-start.4 = (f32[5,3,16,128]{3,2,1,0:T(8,128)S(1)}, f32[5,3,16,128]{3,2,1,0:T(8,128)S(1)}, u32[]{:S(2)}, u32[]{:S(2)}) collective-permute-start(f32[5,3,16,128]{3,2,1,0:T(8,128)S(1)} %get-tuple-element.20), channel_id=1, source_target_pairs={{2,0},{4,2},{6,4},{8,6},{10,8},{12,10},{14,12},{16,14},{18,16},{20... | collective-permute-start | bytes 368648 | tf_op jit(solution)/shard_map/ppermute | solution.py:298
  20.6 9.1 %collective-permute-start.5 = (f32[5,3,16,128]{3,2,1,0:T(8,128)S(1)}, f32[5,3,16,128]{3,2,1,0:T(8,128)S(1)}, u32[]{:S(2)}, u32[]{:S(2)}) collective-permute-start(f32[5,3,16,128]{3,2,1,0:T(8,128)S(1)} %get-tuple-element.22), channel_id=1, source_target_pairs={{0,2},{2,4},{4,6},{6,8},{8,10},{10,12},{12,14},{14,16},{16,18},{18... | collective-permute-start | bytes 368648 | tf_op jit(solution)/shard_map/ppermute | solution.py:298
  29.9 3.3 %collective-permute-start.6 = (f32[5,12,8,128]{3,2,1,0:T(8,128)S(1)}, f32[5,12,8,128]{3,2,1,0:T(8,128)S(1)}, u32[]{:S(2)}, u32[]{:S(2)}) collective-permute-start(f32[5,12,8,128]{3,2,1,0:T(8,128)S(1)} %shard_map.71), channel_id=1, source_target_pairs={{0,1},{1,0},{2,3},{3,2},{4,5},{5,4},{6,7},{7,6},{8,9},{9,8},{10,11... | collective-permute-start | bytes 737288 | tf_op jit(solution)/shard_map/ppermute | solution.py:300
  29.9 6.2 %collective-permute-start.8 = (f32[5,3,16,128]{3,2,1,0:T(8,128)S(1)}, f32[5,3,16,128]{3,2,1,0:T(8,128)S(1)}, u32[]{:S(2)}, u32[]{:S(2)}) collective-permute-start(f32[5,3,16,128]{3,2,1,0:T(8,128)S(1)} %get-tuple-element.26), channel_id=1, source_target_pairs={{2,0},{4,2},{6,4},{8,6},{10,8},{12,10},{14,12},{16,14},{18,16},{20... | collective-permute-start | bytes 368648 | tf_op jit(solution)/shard_map/ppermute | solution.py:298
  30.3 9.0 %collective-permute-start.7 = (f32[5,3,16,128]{3,2,1,0:T(8,128)S(1)}, f32[5,3,16,128]{3,2,1,0:T(8,128)S(1)}, u32[]{:S(2)}, u32[]{:S(2)}) collective-permute-start(f32[5,3,16,128]{3,2,1,0:T(8,128)S(1)} %get-tuple-element.25), channel_id=1, source_target_pairs={{0,2},{2,4},{4,6},{6,8},{8,10},{10,12},{12,14},{14,16},{16,18},{18... | collective-permute-start | bytes 368648 | tf_op jit(solution)/shard_map/ppermute | solution.py:298

commit v7 on v6

--- a/solution.py
+++ b/solution.py
@@ -211,33 +211,26 @@
     return speed + 3.0 * jnp.sqrt(gamma_cell * (press_now + pinf_cell) * inverse)
 
 
-def final_kernel(
-    share, coefs, partial_ref, left_ref, right_ref, phase_ref, inner_ref, out_ref, peak_ref, edges, semaphores
-):
-    length = partial_ref.shape[1]
-    inner = pl.ds(WIDTH, length - 2 * WIDTH)
-    copies = [pltpu.make_async_copy(partial_ref.at[:, inner], out_ref.at[:, inner], semaphores.at[0])]
-    copies[0].start()
+def final_kernel(share, coefs, partial_ref, left_ref, right_ref, phase_ref, inner_ref, out_ref, peak_ref):
     largest = inner_ref[...]
-    for side, halo_ref in enumerate((left_ref, right_ref)):
-        for index, place, state in with_halo(share, coefs, partial_ref, halo_ref, side == 1):
+    for halo_ref, above in ((left_ref, False), (right_ref, True)):
+        for index, place, state in with_halo(share, coefs, partial_ref, halo_ref, above):
             for member in range(5):
-                edges[side, member, place] = state[member]
+                out_ref[member, index] = state[member]
             largest = jnp.maximum(largest, wave_speed(state, phase_ref[index]))
-    for side, start in enumerate((0, length - WIDTH)):
-        copies.append(
-            pltpu.make_async_copy(edges.at[side], out_ref.at[:, pl.ds(start, WIDTH)], semaphores.at[1 + side])
-        )
-        copies[-1].start()
     largest = jnp.max(largest, axis=0, keepdims=True)
     peak_ref[...] = jnp.broadcast_to(largest, peak_ref.shape)
-    for copy in copies:
-        copy.wait()
-
-
-def peak_kernel(peaks_ref, largest_ref):
+
+
+def output_kernel(state_ref, peaks_ref, advanced_ref, largest_ref, peak, semaphores):
+    whole = pltpu.make_async_copy(state_ref, advanced_ref, semaphores.at[0])
+    whole.start()
     largest = jnp.max(jnp.max(peaks_ref[...], axis=0, keepdims=True), axis=1, keepdims=True)
-    largest_ref[...] = largest
+    peak[...] = jnp.broadcast_to(largest, peak.shape)
+    single = pltpu.make_async_copy(peak, largest_ref, semaphores.at[1])
+    single.start()
+    whole.wait()
+    single.wait()
 
 
 def shaped(*shape):
@@ -321,17 +314,13 @@
             aliases={1: 0},
         )
         if final:
-            advanced, peak = call(
+            state, peak = call(
                 functools.partial(final_kernel, weights[1]),
                 [whole, shaped(along * across, lanes)],
                 [VMEM] * 6,
                 [coefs, state, halos["up"], halos["down"], phase_map, *inner],
                 flops=cells * 50,
-                places=[HBM, VMEM],
-                scratch=[
-                    pltpu.VMEM((2, 5, WIDTH, rows, lanes), jnp.float32),
-                    pltpu.SemaphoreType.DMA((3,)),
-                ],
+                aliases={1: 0},
             )
             break
         for way in STAGES[number + 1][0]:
@@ -345,8 +334,16 @@
                 aliases={1: 0},
             )
     peaks = lax.all_to_all(peak, ("gx", "gy"), 0, 0, tiled=True)
-    (largest,) = call(peak_kernel, [shaped(1, 1)], [VMEM], [peaks], flops=1000)
-    return (advanced, jnp.reshape(largest, (1,)))
+    advanced, largest = call(
+        output_kernel,
+        [whole, shaped(1, lanes)],
+        [VMEM, VMEM],
+        [state, peaks],
+        flops=1000,
+        places=[HBM, HBM],
+        scratch=[pltpu.VMEM((1, lanes), jnp.float32), pltpu.SemaphoreType.DMA((2,))],
+    )
+    return (advanced, largest[0, 0:1])
 
 
 def solution(mesh):

time: 49.8 us -> 49.4 us (level)
  no operation moved by 1% of the time
where the time goes in v7:
time: 49.4 us; the launch traced here: 49.1 us
  starting transfers between devices  14.7 us (30%)
  waiting for transfers between devices  14.1 us (29%)
  blocking collectives  8.87 us (18%)
  Pallas kernels  7.17 us (15%)
  between operations  2.19 us (4%)
  local copies, waits for them, and re-layouts  2 us (4%)
    ppermute x6, waiting for transfers between devices, advance(): halos[way] = lax.ppermute(edges[way], 'gx', up if way == 'up' else down)  14.1 us
    ppermute x6, starting transfers between devices, advance(): halos[way] = lax.ppermute(edges[way], 'gx', up if way == 'up' else down)  14 us
    all_to_all x1, blocking collectives, advance(): peaks = lax.all_to_all(peak, ('gx', 'gy'), 0, 0, tiled=True)  8.87 us
    pallas_call x16, Pallas kernels, call(): pl.pallas_call(kernel, out_shape=list(outs), in_specs=specs, out_specs=pl...  7.17 us
    unnamed x8, local copies, waits for them, and re-layouts  1.93 us
  transfers between devices with their start and end apart: 9, of which 5 were waited for; matrix products, arithmetic and copies ran while one was open for 0% of the time, Pallas kernels for 12%

profile of v7, /device:TPU:0, one launch (start us, length us, event | category | flops | bytes accessed | tf_op | source)
XLA Modules:
  0.0 49.1 jit_solution(6294113260515750628)
XLA Ops:
  0.6 0.0 copy-start
  0.6 0.9 %copy-done = s32[12,16,128]{2,1,0:T(8,128)S(1)} copy-done((s32[12,16,128]{2,1,0:T(8,128)S(1)}, s32[12,16,128]{2,1,0:T(8,128)}, u32[]{:S(2)}) %copy-start) | copy-done | bytes 98328
  1.5 0.0 copy-start.2
  1.5 1.0 %copy-done.2 = f32[5,12,16,128]{3,2,1,0:T(8,128)S(1)} copy-done((f32[5,12,16,128]{3,2,1,0:T(8,128)S(1)}, f32[5,12,16,128]{3,2,1,0:T(8,128)}, u32[]{:S(2)}) %copy-start.2) | copy-done | bytes 491544
  2.6 0.1 shard_map.60
  2.7 0.0 copy-start.3
  2.7 0.6 %collective-permute-start = (f32[5,12,8,128]{3,2,1,0:T(8,128)S(1)}, f32[5,12,8,128]{3,2,1,0:T(8,128)S(1)}, u32[]{:S(2)}, u32[]{:S(2)}) collective-permute-start(f32[5,12,8,128]{3,2,1,0:T(8,128)S(1)} %shard_map.60), channel_id=1, source_target_pairs={{0,1},{1,0},{2,3},{3,2},{4,5},{5,4},{6,7},{7,6},{8,9},{9,8},{10,11... | collective-permute-start | bytes 737288 | tf_op jit(solution)/shard_map/ppermute | solution.py:293
  3.2 0.0 copy-start.1
  3.3 1.1 %shard_map.62 = (f32[5,3,16,128]{3,2,1,0:T(8,128)S(1)}, f32[5,3,16,128]{3,2,1,0:T(8,128)S(1)}) custom-call(f32[5,12,16,128]{3,2,1,0:T(8,128)} %start_ref.5, s32[12,16,128]{2,1,0:T(8,128)} %phase_ref.29), custom_call_target="tpu_custom_call" | custom-call | flops 491520 | bytes 245760 | tf_op jit(solution)/shard_map/pallas_call | solution.py:242
  4.3 2.6 %collective-permute-start.1 = (f32[5,3,16,128]{3,2,1,0:T(8,128)S(1)}, f32[5,3,16,128]{3,2,1,0:T(8,128)S(1)}, u32[]{:S(2)}, u32[]{:S(2)}) collective-permute-start(f32[5,3,16,128]{3,2,1,0:T(8,128)S(1)} %get-tuple-element.18), channel_id=1, source_target_pairs={{0,2},{2,4},{4,6},{6,8},{8,10},{10,12},{12,14},{14,16},{16,18},{18... | collective-permute-start | bytes 368648 | tf_op jit(solution)/shard_map/ppermute | solution.py:291
  6.9 4.1 %collective-permute-start.2 = (f32[5,3,16,128]{3,2,1,0:T(8,128)S(1)}, f32[5,3,16,128]{3,2,1,0:T(8,128)S(1)}, u32[]{:S(2)}, u32[]{:S(2)}) collective-permute-start(f32[5,3,16,128]{3,2,1,0:T(8,128)S(1)} %get-tuple-element.20), channel_id=1, source_target_pairs={{2,0},{4,2},{6,4},{8,6},{10,8},{12,10},{14,12},{16,14},{18,16},{20... | collective-permute-start | bytes 368648 | tf_op jit(solution)/shard_map/ppermute | solution.py:291
  12.4 0.1 maximum_multiply_fusion
  12.5 0.1 broadcast_in_dim.2.coefs
  12.5 0.0 copy-done.3
  12.5 0.0 copy-done.1
  12.5 1.2 %shard_map.59.partial_ref = f32[5,12,16,128]{3,2,1,0:T(8,128)S(1)} custom-call(f32[4,16,128]{2,1,0:T(8,128)S(1)} %broadcast_in_dim.2.coefs, f32[5,12,16,128]{3,2,1,0:T(8,128)S(1)} %copy-done.3, s32[12,16,128]{2,1,0:T(8,128)S(1)} %copy-done.1, f32[5,12,16,128]{3,2,1,0:T(8,128)S(1)} %copy-done.3), custom_call_target="tpu_custom_call" | custom-call | flops 24576000 | bytes 491520 | tf_op jit(solution)/shard_map/pallas_call | solution.py:242
  13.7 0.0 collective-permute-done.before_ref.after_ref
  13.7 0.3 shard_map.61.partial_ref
  14.0 0.9 %collective-permute-done.1.halo_ref = f32[5,3,16,128]{3,2,1,0:T(8,128)S(1)} collective-permute-done((f32[5,3,16,128]{3,2,1,0:T(8,128)S(1)}, f32[5,3,16,128]{3,2,1,0:T(8,128)S(1)}, u32[]{:S(2)}, u32[]{:S(2)}) %collective-permute-start.1) | collective-permute-done | bytes 122912 | tf_op jit(solution)/shard_map/ppermute | solution.py:291
  15.0 0.1 shard_map.63
  15.0 0.0 collective-permute-done.2.halo_ref
  15.0 0.1 shard_map.64
  15.1 0.1 shard_map.66
  15.2 0.1 collective-permute-start.3
  15.3 5.3 %collective-permute-start.4 = (f32[5,3,16,128]{3,2,1,0:T(8,128)S(1)}, f32[5,3,16,128]{3,2,1,0:T(8,128)S(1)}, u32[]{:S(2)}, u32[]{:S(2)}) collective-permute-start(f32[5,3,16,128]{3,2,1,0:T(8,128)S(1)} %get-tuple-element.22), channel_id=1, source_target_pairs={{2,0},{4,2},{6,4},{8,6},{10,8},{12,10},{14,12},{16,14},{18,16},{20... | collective-permute-start | bytes 368648 | tf_op jit(solution)/shard_map/ppermute | solution.py:291
  20.6 0.0 collective-permute-start.5
  20.6 1.2 %shard_map.65.partial_ref = f32[5,12,16,128]{3,2,1,0:T(8,128)S(1)} custom-call(f32[4,16,128]{2,1,0:T(8,128)S(1)} %broadcast_in_dim.2.coefs, f32[5,12,16,128]{3,2,1,0:T(8,128)S(1)} %get-tuple-element.21.state_ref, s32[12,16,128]{2,1,0:T(8,128)S(1)} %copy-done.1, f32[5,12,16,128]{3,2,1,0:T(8,128)S(1)} %copy-done.3), custom_call_target="tpu_custom_call" | custom-call | flops 24576000 | bytes 491520 | tf_op jit(solution)/shard_map/pallas_call | solution.py:242
  21.8 0.0 collective-permute-done.3.before_ref.after_ref
  21.8 0.3 shard_map.67.partial_ref
  22.1 1.7 %collective-permute-done.4.halo_ref = f32[5,3,16,128]{3,2,1,0:T(8,128)S(1)} collective-permute-done((f32[5,3,16,128]{3,2,1,0:T(8,128)S(1)}, f32[5,3,16,128]{3,2,1,0:T(8,128)S(1)}, u32[]{:S(2)}, u32[]{:S(2)}) %collective-permute-start.4) | collective-permute-done | bytes 122912 | tf_op jit(solution)/shard_map/ppermute | solution.py:291
  23.8 0.1 shard_map.68
  23.8 5.8 %collective-permute-done.5.halo_ref = f32[5,3,16,128]{3,2,1,0:T(8,128)S(1)} collective-permute-done((f32[5,3,16,128]{3,2,1,0:T(8,128)S(1)}, f32[5,3,16,128]{3,2,1,0:T(8,128)S(1)}, u32[]{:S(2)}, u32[]{:S(2)}) %collective-permute-start.5) | collective-permute-done | bytes 122912 | tf_op jit(solution)/shard_map/ppermute | solution.py:291
  29.7 0.1 shard_map.69
  29.7 0.1 shard_map.71
  29.9 0.1 collective-permute-start.6
  29.9 0.3 collective-permute-start.8
  30.3 1.8 %collective-permute-start.7 = (f32[5,3,16,128]{3,2,1,0:T(8,128)S(1)}, f32[5,3,16,128]{3,2,1,0:T(8,128)S(1)}, u32[]{:S(2)}, u32[]{:S(2)}) collective-permute-start(f32[5,3,16,128]{3,2,1,0:T(8,128)S(1)} %get-tuple-element.27), channel_id=1, source_target_pairs={{0,2},{2,4},{4,6},{6,8},{8,10},{10,12},{12,14},{14,16},{16,18},{18... | collective-permute-start | bytes 368648 | tf_op jit(solution)/shard_map/ppermute | solution.py:291
  32.0 1.2 %shard_map.70.partial_ref = f32[5,12,16,128]{3,2,1,0:T(8,128)S(1)} custom-call(f32[4,16,128]{2,1,0:T(8,128)S(1)} %broadcast_in_dim.2.coefs, f32[5,12,16,128]{3,2,1,0:T(8,128)S(1)} %get-tuple-element.25.state_ref, s32[12,16,128]{2,1,0:T(8,128)S(1)} %copy-done.1, f32[5,12,16,128]{3,2,1,0:T(8,128)S(1)} %copy-done.3), custom_call_target="tpu_custom_call" | custom-call | flops 24576000 | bytes 491520 | tf_op jit(solution)/shard_map/pallas_call | solution.py:242
  33.2 0.0 collective-permute-done.6.before_ref.after_ref
  33.2 0.4 shard_map.72
  33.6 2.6 %collective-permute-done.8.right_ref = f32[5,3,16,128]{3,2,1,0:T(8,128)S(1)} collective-permute-done((f32[5,3,16,128]{3,2,1,0:T(8,128)S(1)}, f32[5,3,16,128]{3,2,1,0:T(8,128)S(1)}, u32[]{:S(2)}, u32[]{:S(2)}) %collective-permute-start.8) | collective-permute-done | bytes 122912 | tf_op jit(solution)/shard_map/ppermute | solution.py:291
  36.2 3.1 %collective-permute-done.7.left_ref = f32[5,3,16,128]{3,2,1,0:T(8,128)S(1)} collective-permute-done((f32[5,3,16,128]{3,2,1,0:T(8,128)S(1)}, f32[5,3,16,128]{3,2,1,0:T(8,128)S(1)}, u32[]{:S(2)}, u32[]{:S(2)}) %collective-permute-start.7) | collective-permute-done | bytes 122912 | tf_op jit(solution)/shard_map/ppermute | solution.py:291
  39.3 0.2 shard_map.73
  39.4 8.9 %all_to_all.11 = f32[32,1,128]{2,1,0:T(1,128)S(1)} all-to-all(f32[32,1,128]{2,1,0:T(1,128)S(1)} %bitcast.8), channel_id=1, replica_groups=mesh['gx'=16,'gy'=2] {'gx','gy'}, dimensions={0} | all-to-all | bytes 32768 | tf_op jit(solution)/shard_map/all_to_all | solution.py:336
  48.3 0.8 %shard_map.74 = (f32[5,12,16,128]{3,2,1,0:T(8,128)}, f32[1,128]{1,0:T(1,128)}) custom-call(f32[5,12,16,128]{3,2,1,0:T(8,128)S(1)} %get-tuple-element.30.state_ref, f32[32,128]{1,0:T(8,128)S(1)} %bitcast.7), custom_call_target="tpu_custom_call" | custom-call | flops 1000 | bytes 492032 | tf_op jit(solution)/shard_map/pallas_call | solution.py:242
Async XLA Ops:
  0.6 0.9 %copy-start = (s32[12,16,128]{2,1,0:T(8,128)S(1)}, s32[12,16,128]{2,1,0:T(8,128)}, u32[]{:S(2)}) copy-start(s32[12,16,128]{2,1,0:T(8,128)} %phase_ref.29) | copy-start | bytes 294916
  1.5 1.0 %copy-start.2 = (f32[5,12,16,128]{3,2,1,0:T(8,128)S(1)}, f32[5,12,16,128]{3,2,1,0:T(8,128)}, u32[]{:S(2)}) copy-start(f32[5,12,16,128]{3,2,1,0:T(8,128)} %start_ref.5) | copy-start | bytes 1474564
  2.7 9.9 %copy-start.3 = (f32[5,12,16,128]{3,2,1,0:T(8,128)S(1)}, f32[5,12,16,128]{3,2,1,0:T(8,128)}, u32[]{:S(2)}) copy-start(f32[5,12,16,128]{3,2,1,0:T(8,128)} %start_ref.5) | copy-start | bytes 1474564
  2.7 11.0 %collective-permute-start = (f32[5,12,8,128]{3,2,1,0:T(8,128)S(1)}, f32[5,12,8,128]{3,2,1,0:T(8,128)S(1)}, u32[]{:S(2)}, u32[]{:S(2)}) collective-permute-start(f32[5,12,8,128]{3,2,1,0:T(8,128)S(1)} %shard_map.60), channel_id=1, source_target_pairs={{0,1},{1,0},{2,3},{3,2},{4,5},{5,4},{6,7},{7,6},{8,9},{9,8},{10,11... | collective-permute-start | bytes 737288 | tf_op jit(solution)/shard_map/ppermute | solution.py:293
  3.2 9.3 %copy-start.1 = (s32[12,16,128]{2,1,0:T(8,128)S(1)}, s32[12,16,128]{2,1,0:T(8,128)}, u32[]{:S(2)}) copy-start(s32[12,16,128]{2,1,0:T(8,128)} %phase_ref.29) | copy-start | bytes 294916
  4.3 10.6 %collective-permute-start.1 = (f32[5,3,16,128]{3,2,1,0:T(8,128)S(1)}, f32[5,3,16,128]{3,2,1,0:T(8,128)S(1)}, u32[]{:S(2)}, u32[]{:S(2)}) collective-permute-start(f32[5,3,16,128]{3,2,1,0:T(8,128)S(1)} %get-tuple-element.18), channel_id=1, source_target_pairs={{0,2},{2,4},{4,6},{6,8},{8,10},{10,12},{12,14},{14,16},{16,18},{18... | collective-permute-start | bytes 368648 | tf_op jit(solution)/shard_map/ppermute | solution.py:291
  6.9 8.1 %collective-permute-start.2 = (f32[5,3,16,128]{3,2,1,0:T(8,128)S(1)}, f32[5,3,16,128]{3,2,1,0:T(8,128)S(1)}, u32[]{:S(2)}, u32[]{:S(2)}) collective-permute-start(f32[5,3,16,128]{3,2,1,0:T(8,128)S(1)} %get-tuple-element.20), channel_id=1, source_target_pairs={{2,0},{4,2},{6,4},{8,6},{10,8},{12,10},{14,12},{16,14},{18,16},{20... | collective-permute-start | bytes 368648 | tf_op jit(solution)/shard_map/ppermute | solution.py:291
  15.2 6.5 %collective-permute-start.3 = (f32[5,12,8,128]{3,2,1,0:T(8,128)S(1)}, f32[5,12,8,128]{3,2,1,0:T(8,128)S(1)}, u32[]{:S(2)}, u32[]{:S(2)}) collective-permute-start(f32[5,12,8,128]{3,2,1,0:T(8,128)S(1)} %shard_map.66), channel_id=1, source_target_pairs={{0,1},{1,0},{2,3},{3,2},{4,5},{5,4},{6,7},{7,6},{8,9},{9,8},{10,11... | collective-permute-start | bytes 737288 | tf_op jit(solution)/shard_map/ppermute | solution.py:293
  15.3 8.4 %collective-permute-start.4 = (f32[5,3,16,128]{3,2,1,0:T(8,128)S(1)}, f32[5,3,16,128]{3,2,1,0:T(8,128)S(1)}, u32[]{:S(2)}, u32[]{:S(2)}) collective-permute-start(f32[5,3,16,128]{3,2,1,0:T(8,128)S(1)} %get-tuple-element.22), channel_id=1, source_target_pairs={{2,0},{4,2},{6,4},{8,6},{10,8},{12,10},{14,12},{16,14},{18,16},{20... | collective-permute-start | bytes 368648 | tf_op jit(solution)/shard_map/ppermute | solution.py:291
  20.6 9.1 %collective-permute-start.5 = (f32[5,3,16,128]{3,2,1,0:T(8,128)S(1)}, f32[5,3,16,128]{3,2,1,0:T(8,128)S(1)}, u32[]{:S(2)}, u32[]{:S(2)}) collective-permute-start(f32[5,3,16,128]{3,2,1,0:T(8,128)S(1)} %get-tuple-element.24), channel_id=1, source_target_pairs={{0,2},{2,4},{4,6},{6,8},{8,10},{10,12},{12,14},{14,16},{16,18},{18... | collective-permute-start | bytes 368648 | tf_op jit(solution)/shard_map/ppermute | solution.py:291
  29.9 3.3 %collective-permute-start.6 = (f32[5,12,8,128]{3,2,1,0:T(8,128)S(1)}, f32[5,12,8,128]{3,2,1,0:T(8,128)S(1)}, u32[]{:S(2)}, u32[]{:S(2)}) collective-permute-start(f32[5,12,8,128]{3,2,1,0:T(8,128)S(1)} %shard_map.71), channel_id=1, source_target_pairs={{0,1},{1,0},{2,3},{3,2},{4,5},{5,4},{6,7},{7,6},{8,9},{9,8},{10,11... | collective-permute-start | bytes 737288 | tf_op jit(solution)/shard_map/ppermute | solution.py:293
  29.9 6.2 %collective-permute-start.8 = (f32[5,3,16,128]{3,2,1,0:T(8,128)S(1)}, f32[5,3,16,128]{3,2,1,0:T(8,128)S(1)}, u32[]{:S(2)}, u32[]{:S(2)}) collective-permute-start(f32[5,3,16,128]{3,2,1,0:T(8,128)S(1)} %get-tuple-element.28), channel_id=1, source_target_pairs={{2,0},{4,2},{6,4},{8,6},{10,8},{12,10},{14,12},{16,14},{18,16},{20... | collective-permute-start | bytes 368648 | tf_op jit(solution)/shard_map/ppermute | solution.py:291
  30.3 9.0 %collective-permute-start.7 = (f32[5,3,16,128]{3,2,1,0:T(8,128)S(1)}, f32[5,3,16,128]{3,2,1,0:T(8,128)S(1)}, u32[]{:S(2)}, u32[]{:S(2)}) collective-permute-start(f32[5,3,16,128]{3,2,1,0:T(8,128)S(1)} %get-tuple-element.27), channel_id=1, source_target_pairs={{0,2},{2,4},{4,6},{6,8},{8,10},{10,12},{12,14},{14,16},{16,18},{18... | collective-permute-start | bytes 368648 | tf_op jit(solution)/shard_map/ppermute | solution.py:291

commit v8 on v7

--- a/solution.py
+++ b/solution.py
@@ -122,7 +122,7 @@
             zs[member, index] = piece
         return carry
 
-    lax.fori_loop(0, length, fill, 0, unroll=2)
+    lax.fori_loop(0, length, fill, 0, unroll=4)
     keep, share = weights
     steps = [coefs[k] * share for k in range(3)]
     source = coefs[3] * share
@@ -151,10 +151,10 @@
             out_ref[member, index] = value
         return carry
 
-    lax.fori_loop(0, length, update, 0, unroll=4)
-
-
-def border_kernel(share, final, coefs, partial_ref, phase_ref, before_ref, after_ref, out_ref, *inner_ref):
+    lax.fori_loop(0, length, update, 0, unroll=6)
+
+
+def border_kernel(share, final, coefs, partial_ref, phase_ref, before_ref, after_ref, out_ref, *rest):
     _, length, rows, lanes = partial_ref.shape
     place = lax.broadcasted_iota(jnp.int32, (TILE, lanes), 0)
     blank = jnp.zeros((TILE, lanes), jnp.float32)
@@ -174,14 +174,19 @@
             out_ref[member, index, rows - TILE : rows] = final
         return carry
 
-    lax.fori_loop(0, length, border, 0, unroll=2)
+    lax.fori_loop(0, length, border, 0, unroll=4)
     if final:
+        inner_ref, advanced_ref, semaphore = rest
+        inner = pl.ds(WIDTH, length - 2 * WIDTH)
+        copy = pltpu.make_async_copy(out_ref.at[:, inner], advanced_ref.at[:, inner], semaphore)
+        copy.start()
 
         def fastest(index, largest):
             return jnp.maximum(largest, wave_speed(plane(out_ref, index), phase_ref[index]))
 
         blank = jnp.zeros((rows, lanes), jnp.float32)
-        inner_ref[0][...] = lax.fori_loop(WIDTH, length - WIDTH, fastest, blank, unroll=2)
+        inner_ref[...] = lax.fori_loop(WIDTH, length - WIDTH, fastest, blank, unroll=3)
+        copy.wait()
 
 
 def with_halo(share, coefs, partial_ref, halo_ref, above):
@@ -222,15 +227,19 @@
     peak_ref[...] = jnp.broadcast_to(largest, peak_ref.shape)
 
 
-def output_kernel(state_ref, peaks_ref, advanced_ref, largest_ref, peak, semaphores):
-    whole = pltpu.make_async_copy(state_ref, advanced_ref, semaphores.at[0])
-    whole.start()
+def output_kernel(state_ref, peaks_ref, inner_ref, advanced_ref, largest_ref, peak, semaphores):
+    length = state_ref.shape[1]
+    copies = []
+    for side, start in enumerate((0, length - WIDTH)):
+        near = pl.ds(start, WIDTH)
+        copies.append(pltpu.make_async_copy(state_ref.at[:, near], advanced_ref.at[:, near], semaphores.at[side]))
+        copies[side].start()
     largest = jnp.max(jnp.max(peaks_ref[...], axis=0, keepdims=True), axis=1, keepdims=True)
     peak[...] = jnp.broadcast_to(largest, peak.shape)
-    single = pltpu.make_async_copy(peak, largest_ref, semaphores.at[1])
-    single.start()
-    whole.wait()
-    single.wait()
+    copies.append(pltpu.make_async_copy(peak, largest_ref, semaphores.at[2]))
+    copies[2].start()
+    for copy in copies:
+        copy.wait()
 
 
 def shaped(*shape):
@@ -307,18 +316,20 @@
         )
         state, *inner = call(
             functools.partial(border_kernel, weights[1], final),
-            [whole, shaped(rows, lanes)] if final else [whole],
+            [whole, shaped(rows, lanes), whole] if final else [whole],
             [VMEM] * 5,
             [coefs, state, phase_map, before, after],
             flops=cells * 20,
             aliases={1: 0},
+            places=[VMEM, VMEM, HBM] if final else None,
+            scratch=[pltpu.SemaphoreType.DMA] if final else (),
         )
         if final:
             state, peak = call(
                 functools.partial(final_kernel, weights[1]),
                 [whole, shaped(along * across, lanes)],
                 [VMEM] * 6,
-                [coefs, state, halos["up"], halos["down"], phase_map, *inner],
+                [coefs, state, halos["up"], halos["down"], phase_map, inner[0]],
                 flops=cells * 50,
                 aliases={1: 0},
             )
@@ -337,11 +348,12 @@
     advanced, largest = call(
         output_kernel,
         [whole, shaped(1, lanes)],
-        [VMEM, VMEM],
-        [state, peaks],
+        [VMEM, VMEM, HBM],
+        [state, peaks, inner[1]],
         flops=1000,
         places=[HBM, HBM],
-        scratch=[pltpu.VMEM((1, lanes), jnp.float32), pltpu.SemaphoreType.DMA((2,))],
+        scratch=[pltpu.VMEM((1, lanes), jnp.float32), pltpu.SemaphoreType.DMA((3,))],
+        aliases={2: 0},
     )
     return (advanced, largest[0, 0:1])
 

time: 49.4 us -> 49.3 us (level)
  no operation moved by 1% of the time
where the time goes in v8:
time: 49.3 us; the launch traced here: 49 us
  starting transfers between devices  14.7 us (30%)
  waiting for transfers between devices  13.8 us (28%)
  blocking collectives  8.87 us (18%)
  Pallas kernels  7.45 us (15%)
  between operations  2.19 us (4%)
  local copies, waits for them, and re-layouts  2 us (4%)
    ppermute x6, starting transfers between devices, advance(): halos[way] = lax.ppermute(edges[way], 'gx', up if way == 'up' else down)  14 us
    ppermute x6, waiting for transfers between devices, advance(): halos[way] = lax.ppermute(edges[way], 'gx', up if way == 'up' else down)  13.8 us
    all_to_all x1, blocking collectives, advance(): peaks = lax.all_to_all(peak, ('gx', 'gy'), 0, 0, tiled=True)  8.87 us
    pallas_call x16, Pallas kernels, call(): pl.pallas_call(kernel, out_shape=list(outs), in_specs=specs, out_specs=pl...  7.45 us
    unnamed x8, local copies, waits for them, and re-layouts  1.93 us
  transfers between devices with their start and end apart: 9, of which 5 were waited for; matrix products, arithmetic and copies ran while one was open for 0% of the time, Pallas kernels for 12%

profile of v8, /device:TPU:0, one launch (start us, length us, event | category | flops | bytes accessed | tf_op | source)
XLA Modules:
  0.0 49.0 jit_solution(15306737644674989340)
XLA Ops:
  0.6 0.0 copy-start
  0.6 0.9 %copy-done = s32[12,16,128]{2,1,0:T(8,128)S(1)} copy-done((s32[12,16,128]{2,1,0:T(8,128)S(1)}, s32[12,16,128]{2,1,0:T(8,128)}, u32[]{:S(2)}) %copy-start) | copy-done | bytes 98328
  1.5 0.0 copy-start.2
  1.5 1.0 %copy-done.2 = f32[5,12,16,128]{3,2,1,0:T(8,128)S(1)} copy-done((f32[5,12,16,128]{3,2,1,0:T(8,128)S(1)}, f32[5,12,16,128]{3,2,1,0:T(8,128)}, u32[]{:S(2)}) %copy-start.2) | copy-done | bytes 491544
  2.6 0.1 shard_map.60
  2.7 0.0 copy-start.3
  2.7 0.6 %collective-permute-start = (f32[5,12,8,128]{3,2,1,0:T(8,128)S(1)}, f32[5,12,8,128]{3,2,1,0:T(8,128)S(1)}, u32[]{:S(2)}, u32[]{:S(2)}) collective-permute-start(f32[5,12,8,128]{3,2,1,0:T(8,128)S(1)} %shard_map.60), channel_id=1, source_target_pairs={{0,1},{1,0},{2,3},{3,2},{4,5},{5,4},{6,7},{7,6},{8,9},{9,8},{10,11... | collective-permute-start | bytes 737288 | tf_op jit(solution)/shard_map/ppermute | solution.py:302
  3.2 0.0 copy-start.1
  3.3 1.1 %shard_map.62 = (f32[5,3,16,128]{3,2,1,0:T(8,128)S(1)}, f32[5,3,16,128]{3,2,1,0:T(8,128)S(1)}) custom-call(f32[5,12,16,128]{3,2,1,0:T(8,128)} %start_ref.5, s32[12,16,128]{2,1,0:T(8,128)} %phase_ref.29), custom_call_target="tpu_custom_call" | custom-call | flops 491520 | bytes 245760 | tf_op jit(solution)/shard_map/pallas_call | solution.py:251
  4.3 2.6 %collective-permute-start.1 = (f32[5,3,16,128]{3,2,1,0:T(8,128)S(1)}, f32[5,3,16,128]{3,2,1,0:T(8,128)S(1)}, u32[]{:S(2)}, u32[]{:S(2)}) collective-permute-start(f32[5,3,16,128]{3,2,1,0:T(8,128)S(1)} %get-tuple-element.19), channel_id=1, source_target_pairs={{0,2},{2,4},{4,6},{6,8},{8,10},{10,12},{12,14},{14,16},{16,18},{18... | collective-permute-start | bytes 368648 | tf_op jit(solution)/shard_map/ppermute | solution.py:300
  6.9 4.1 %collective-permute-start.2 = (f32[5,3,16,128]{3,2,1,0:T(8,128)S(1)}, f32[5,3,16,128]{3,2,1,0:T(8,128)S(1)}, u32[]{:S(2)}, u32[]{:S(2)}) collective-permute-start(f32[5,3,16,128]{3,2,1,0:T(8,128)S(1)} %get-tuple-element.21), channel_id=1, source_target_pairs={{2,0},{4,2},{6,4},{8,6},{10,8},{12,10},{14,12},{16,14},{18,16},{20... | collective-permute-start | bytes 368648 | tf_op jit(solution)/shard_map/ppermute | solution.py:300
  12.4 0.1 maximum_multiply_fusion
  12.5 0.1 broadcast_in_dim.2.coefs
  12.5 0.0 copy-done.3
  12.5 0.0 copy-done.1
  12.5 1.1 %shard_map.59.partial_ref = f32[5,12,16,128]{3,2,1,0:T(8,128)S(1)} custom-call(f32[4,16,128]{2,1,0:T(8,128)S(1)} %broadcast_in_dim.2.coefs, f32[5,12,16,128]{3,2,1,0:T(8,128)S(1)} %copy-done.3, s32[12,16,128]{2,1,0:T(8,128)S(1)} %copy-done.1, f32[5,12,16,128]{3,2,1,0:T(8,128)S(1)} %copy-done.3), custom_call_target="tpu_custom_call" | custom-call | flops 24576000 | bytes 491520 | tf_op jit(solution)/shard_map/pallas_call | solution.py:251
  13.6 0.0 collective-permute-done.before_ref.after_ref
  13.6 0.3 shard_map.61.partial_ref
  13.9 1.0 %collective-permute-done.1.halo_ref = f32[5,3,16,128]{3,2,1,0:T(8,128)S(1)} collective-permute-done((f32[5,3,16,128]{3,2,1,0:T(8,128)S(1)}, f32[5,3,16,128]{3,2,1,0:T(8,128)S(1)}, u32[]{:S(2)}, u32[]{:S(2)}) %collective-permute-start.1) | collective-permute-done | bytes 122912 | tf_op jit(solution)/shard_map/ppermute | solution.py:300
  15.0 0.1 shard_map.63
  15.0 0.0 collective-permute-done.2.halo_ref
  15.0 0.1 shard_map.64
  15.1 0.1 shard_map.66
  15.2 0.1 collective-permute-start.3
  15.3 5.3 %collective-permute-start.4 = (f32[5,3,16,128]{3,2,1,0:T(8,128)S(1)}, f32[5,3,16,128]{3,2,1,0:T(8,128)S(1)}, u32[]{:S(2)}, u32[]{:S(2)}) collective-permute-start(f32[5,3,16,128]{3,2,1,0:T(8,128)S(1)} %get-tuple-element.23), channel_id=1, source_target_pairs={{2,0},{4,2},{6,4},{8,6},{10,8},{12,10},{14,12},{16,14},{18,16},{20... | collective-permute-start | bytes 368648 | tf_op jit(solution)/shard_map/ppermute | solution.py:300
  20.6 0.0 collective-permute-start.5
  20.6 1.1 %shard_map.65.partial_ref = f32[5,12,16,128]{3,2,1,0:T(8,128)S(1)} custom-call(f32[4,16,128]{2,1,0:T(8,128)S(1)} %broadcast_in_dim.2.coefs, f32[5,12,16,128]{3,2,1,0:T(8,128)S(1)} %get-tuple-element.22.state_ref, s32[12,16,128]{2,1,0:T(8,128)S(1)} %copy-done.1, f32[5,12,16,128]{3,2,1,0:T(8,128)S(1)} %copy-done.3), custom_call_target="tpu_custom_call" | custom-call | flops 24576000 | bytes 491520 | tf_op jit(solution)/shard_map/pallas_call | solution.py:251
  21.7 0.0 collective-permute-done.3.before_ref.after_ref
  21.7 0.3 shard_map.67.partial_ref
  22.0 1.8 %collective-permute-done.4.halo_ref = f32[5,3,16,128]{3,2,1,0:T(8,128)S(1)} collective-permute-done((f32[5,3,16,128]{3,2,1,0:T(8,128)S(1)}, f32[5,3,16,128]{3,2,1,0:T(8,128)S(1)}, u32[]{:S(2)}, u32[]{:S(2)}) %collective-permute-start.4) | collective-permute-done | bytes 122912 | tf_op jit(solution)/shard_map/ppermute | solution.py:300
  23.8 0.1 shard_map.68
  23.8 5.8 %collective-permute-done.5.halo_ref = f32[5,3,16,128]{3,2,1,0:T(8,128)S(1)} collective-permute-done((f32[5,3,16,128]{3,2,1,0:T(8,128)S(1)}, f32[5,3,16,128]{3,2,1,0:T(8,128)S(1)}, u32[]{:S(2)}, u32[]{:S(2)}) %collective-permute-start.5) | collective-permute-done | bytes 122912 | tf_op jit(solution)/shard_map/ppermute | solution.py:300
  29.7 0.1 shard_map.69
  29.7 0.1 shard_map.71
  29.9 0.1 collective-permute-start.6
  29.9 0.3 collective-permute-start.8
  30.3 1.8 %collective-permute-start.7 = (f32[5,3,16,128]{3,2,1,0:T(8,128)S(1)}, f32[5,3,16,128]{3,2,1,0:T(8,128)S(1)}, u32[]{:S(2)}, u32[]{:S(2)}) collective-permute-start(f32[5,3,16,128]{3,2,1,0:T(8,128)S(1)} %get-tuple-element.28), channel_id=1, source_target_pairs={{0,2},{2,4},{4,6},{6,8},{8,10},{10,12},{12,14},{14,16},{16,18},{18... | collective-permute-start | bytes 368648 | tf_op jit(solution)/shard_map/ppermute | solution.py:300
  32.0 1.1 %shard_map.70.partial_ref = f32[5,12,16,128]{3,2,1,0:T(8,128)S(1)} custom-call(f32[4,16,128]{2,1,0:T(8,128)S(1)} %broadcast_in_dim.2.coefs, f32[5,12,16,128]{3,2,1,0:T(8,128)S(1)} %get-tuple-element.26.state_ref, s32[12,16,128]{2,1,0:T(8,128)S(1)} %copy-done.1, f32[5,12,16,128]{3,2,1,0:T(8,128)S(1)} %copy-done.3), custom_call_target="tpu_custom_call" | custom-call | flops 24576000 | bytes 491520 | tf_op jit(solution)/shard_map/pallas_call | solution.py:251
  33.1 0.0 collective-permute-done.6.before_ref.after_ref
  33.1 1.0 %shard_map.72 = (f32[5,12,16,128]{3,2,1,0:T(8,128)S(1)}, f32[16,128]{1,0:T(8,128)S(1)}, f32[5,12,16,128]{3,2,1,0:T(8,128)}) custom-call(f32[4,16,128]{2,1,0:T(8,128)S(1)} %broadcast_in_dim.2.coefs, f32[5,12,16,128]{3,2,1,0:T(8,128)S(1)} %shard_map.70.partial_ref, s32[12,16,128]{2,1,0:T(8,128)S(1)} %copy-done.1, ...), custom_call_target="tpu_custom_call", output_to_operand_aliasing={{0}: (1, {})} | custom-call | flops 491520 | bytes 991232 | tf_op jit(solution)/shard_map/pallas_call | solution.py:251
  34.1 2.1 %collective-permute-done.8.right_ref = f32[5,3,16,128]{3,2,1,0:T(8,128)S(1)} collective-permute-done((f32[5,3,16,128]{3,2,1,0:T(8,128)S(1)}, f32[5,3,16,128]{3,2,1,0:T(8,128)S(1)}, u32[]{:S(2)}, u32[]{:S(2)}) %collective-permute-start.8) | collective-permute-done | bytes 122912 | tf_op jit(solution)/shard_map/ppermute | solution.py:300
  36.2 3.1 %collective-permute-done.7.left_ref = f32[5,3,16,128]{3,2,1,0:T(8,128)S(1)} collective-permute-done((f32[5,3,16,128]{3,2,1,0:T(8,128)S(1)}, f32[5,3,16,128]{3,2,1,0:T(8,128)S(1)}, u32[]{:S(2)}, u32[]{:S(2)}) %collective-permute-start.7) | collective-permute-done | bytes 122912 | tf_op jit(solution)/shard_map/ppermute | solution.py:300
  39.3 0.2 shard_map.73
  39.4 8.9 %all_to_all.11 = f32[32,1,128]{2,1,0:T(1,128)S(1)} all-to-all(f32[32,1,128]{2,1,0:T(1,128)S(1)} %bitcast.8), channel_id=1, replica_groups=mesh['gx'=16,'gy'=2] {'gx','gy'}, dimensions={0} | all-to-all | bytes 32768 | tf_op jit(solution)/shard_map/all_to_all | solution.py:347
  48.3 0.7 %shard_map.74 = (f32[5,12,16,128]{3,2,1,0:T(8,128)}, f32[1,128]{1,0:T(1,128)}) custom-call(f32[5,12,16,128]{3,2,1,0:T(8,128)S(1)} %get-tuple-element.31.state_ref, f32[32,128]{1,0:T(8,128)S(1)} %bitcast.7, f32[5,12,16,128]{3,2,1,0:T(8,128)} %get-tuple-element.33.inner_ref), custom_call_target="tpu_custom_call", output_to_operand_aliasing={{0}: (2, {})} | custom-call | flops 1000 | bytes 492032 | tf_op jit(solution)/shard_map/pallas_call | solution.py:251
Async XLA Ops:
  0.6 0.9 %copy-start = (s32[12,16,128]{2,1,0:T(8,128)S(1)}, s32[12,16,128]{2,1,0:T(8,128)}, u32[]{:S(2)}) copy-start(s32[12,16,128]{2,1,0:T(8,128)} %phase_ref.29) | copy-start | bytes 294916
  1.5 1.0 %copy-start.2 = (f32[5,12,16,128]{3,2,1,0:T(8,128)S(1)}, f32[5,12,16,128]{3,2,1,0:T(8,128)}, u32[]{:S(2)}) copy-start(f32[5,12,16,128]{3,2,1,0:T(8,128)} %start_ref.5) | copy-start | bytes 1474564
  2.7 9.9 %copy-start.3 = (f32[5,12,16,128]{3,2,1,0:T(8,128)S(1)}, f32[5,12,16,128]{3,2,1,0:T(8,128)}, u32[]{:S(2)}) copy-start(f32[5,12,16,128]{3,2,1,0:T(8,128)} %start_ref.5) | copy-start | bytes 1474564
  2.7 10.9 %collective-permute-start = (f32[5,12,8,128]{3,2,1,0:T(8,128)S(1)}, f32[5,12,8,128]{3,2,1,0:T(8,128)S(1)}, u32[]{:S(2)}, u32[]{:S(2)}) collective-permute-start(f32[5,12,8,128]{3,2,1,0:T(8,128)S(1)} %shard_map.60), channel_id=1, source_target_pairs={{0,1},{1,0},{2,3},{3,2},{4,5},{5,4},{6,7},{7,6},{8,9},{9,8},{10,11... | collective-permute-start | bytes 737288 | tf_op jit(solution)/shard_map/ppermute | solution.py:302
  3.2 9.3 %copy-start.1 = (s32[12,16,128]{2,1,0:T(8,128)S(1)}, s32[12,16,128]{2,1,0:T(8,128)}, u32[]{:S(2)}) copy-start(s32[12,16,128]{2,1,0:T(8,128)} %phase_ref.29) | copy-start | bytes 294916
  4.3 10.6 %collective-permute-start.1 = (f32[5,3,16,128]{3,2,1,0:T(8,128)S(1)}, f32[5,3,16,128]{3,2,1,0:T(8,128)S(1)}, u32[]{:S(2)}, u32[]{:S(2)}) collective-permute-start(f32[5,3,16,128]{3,2,1,0:T(8,128)S(1)} %get-tuple-element.19), channel_id=1, source_target_pairs={{0,2},{2,4},{4,6},{6,8},{8,10},{10,12},{12,14},{14,16},{16,18},{18... | collective-permute-start | bytes 368648 | tf_op jit(solution)/shard_map/ppermute | solution.py:300
  6.9 8.1 %collective-permute-start.2 = (f32[5,3,16,128]{3,2,1,0:T(8,128)S(1)}, f32[5,3,16,128]{3,2,1,0:T(8,128)S(1)}, u32[]{:S(2)}, u32[]{:S(2)}) collective-permute-start(f32[5,3,16,128]{3,2,1,0:T(8,128)S(1)} %get-tuple-element.21), channel_id=1, source_target_pairs={{2,0},{4,2},{6,4},{8,6},{10,8},{12,10},{14,12},{16,14},{18,16},{20... | collective-permute-start | bytes 368648 | tf_op jit(solution)/shard_map/ppermute | solution.py:300
  15.2 6.4 %collective-permute-start.3 = (f32[5,12,8,128]{3,2,1,0:T(8,128)S(1)}, f32[5,12,8,128]{3,2,1,0:T(8,128)S(1)}, u32[]{:S(2)}, u32[]{:S(2)}) collective-permute-start(f32[5,12,8,128]{3,2,1,0:T(8,128)S(1)} %shard_map.66), channel_id=1, source_target_pairs={{0,1},{1,0},{2,3},{3,2},{4,5},{5,4},{6,7},{7,6},{8,9},{9,8},{10,11... | collective-permute-start | bytes 737288 | tf_op jit(solution)/shard_map/ppermute | solution.py:302
  15.3 8.4 %collective-permute-start.4 = (f32[5,3,16,128]{3,2,1,0:T(8,128)S(1)}, f32[5,3,16,128]{3,2,1,0:T(8,128)S(1)}, u32[]{:S(2)}, u32[]{:S(2)}) collective-permute-start(f32[5,3,16,128]{3,2,1,0:T(8,128)S(1)} %get-tuple-element.23), channel_id=1, source_target_pairs={{2,0},{4,2},{6,4},{8,6},{10,8},{12,10},{14,12},{16,14},{18,16},{20... | collective-permute-start | bytes 368648 | tf_op jit(solution)/shard_map/ppermute | solution.py:300
  20.6 9.1 %collective-permute-start.5 = (f32[5,3,16,128]{3,2,1,0:T(8,128)S(1)}, f32[5,3,16,128]{3,2,1,0:T(8,128)S(1)}, u32[]{:S(2)}, u32[]{:S(2)}) collective-permute-start(f32[5,3,16,128]{3,2,1,0:T(8,128)S(1)} %get-tuple-element.25), channel_id=1, source_target_pairs={{0,2},{2,4},{4,6},{6,8},{8,10},{10,12},{12,14},{14,16},{16,18},{18... | collective-permute-start | bytes 368648 | tf_op jit(solution)/shard_map/ppermute | solution.py:300
  29.9 3.3 %collective-permute-start.6 = (f32[5,12,8,128]{3,2,1,0:T(8,128)S(1)}, f32[5,12,8,128]{3,2,1,0:T(8,128)S(1)}, u32[]{:S(2)}, u32[]{:S(2)}) collective-permute-start(f32[5,12,8,128]{3,2,1,0:T(8,128)S(1)} %shard_map.71), channel_id=1, source_target_pairs={{0,1},{1,0},{2,3},{3,2},{4,5},{5,4},{6,7},{7,6},{8,9},{9,8},{10,11... | collective-permute-start | bytes 737288 | tf_op jit(solution)/shard_map/ppermute | solution.py:302
  29.9 6.2 %collective-permute-start.8 = (f32[5,3,16,128]{3,2,1,0:T(8,128)S(1)}, f32[5,3,16,128]{3,2,1,0:T(8,128)S(1)}, u32[]{:S(2)}, u32[]{:S(2)}) collective-permute-start(f32[5,3,16,128]{3,2,1,0:T(8,128)S(1)} %get-tuple-element.29), channel_id=1, source_target_pairs={{2,0},{4,2},{6,4},{8,6},{10,8},{12,10},{14,12},{16,14},{18,16},{20... | collective-permute-start | bytes 368648 | tf_op jit(solution)/shard_map/ppermute | solution.py:300
  30.3 9.0 %collective-permute-start.7 = (f32[5,3,16,128]{3,2,1,0:T(8,128)S(1)}, f32[5,3,16,128]{3,2,1,0:T(8,128)S(1)}, u32[]{:S(2)}, u32[]{:S(2)}) collective-permute-start(f32[5,3,16,128]{3,2,1,0:T(8,128)S(1)} %get-tuple-element.28), channel_id=1, source_target_pairs={{0,2},{2,4},{4,6},{6,8},{8,10},{10,12},{12,14},{14,16},{16,18},{18... | collective-permute-start | bytes 368648 | tf_op jit(solution)/shard_map/ppermute | solution.py:300

commit v9 on v8

--- a/solution.py
+++ b/solution.py
@@ -297,9 +297,10 @@
     for number, ((first, second), weights) in enumerate(STAGES):
         halos = {}
         for way in (first, second):
-            halos[way] = lax.ppermute(edges[way], "gx", up if way == "up" else down)
+            sent = edges[way].reshape(-1, lanes)
+            halos[way] = lax.ppermute(sent, "gx", up if way == "up" else down).reshape(edge.shape)
         (sent,) = call(rows_kernel, [row_tile], [VMEM, VMEM], [state, phase_map], flops=cells * 10)
-        before = lax.ppermute(sent, "gy", over)
+        before = lax.ppermute(sent.reshape(-1, lanes), "gy", over).reshape(sent.shape)
         after = before if across == 2 else lax.ppermute(sent, "gy", back)
         final = number == len(STAGES) - 1
         (state,) = call(

time: 49.3 us -> 49.3 us (level)
  no operation moved by 1% of the time
where the time goes in v9:
time: 49.3 us; the launch traced here: 49 us
  starting transfers between devices  14.7 us (30%)
  waiting for transfers between devices  13.8 us (28%)
  blocking collectives  8.87 us (18%)
  Pallas kernels  7.45 us (15%)
  between operations  2.19 us (4%)
  local copies, waits for them, and re-layouts  2 us (4%)
    ppermute x6, starting transfers between devices, advance(): lax.ppermute(sent, 'gx', up if way == 'up' else down).reshape(edge.shape)  14 us
    ppermute x6, waiting for transfers between devices, advance(): lax.ppermute(sent, 'gx', up if way == 'up' else down).reshape(edge.shape)  13.8 us
    all_to_all x1, blocking collectives, advance(): peaks = lax.all_to_all(peak, ('gx', 'gy'), 0, 0, tiled=True)  8.87 us
    pallas_call x16, Pallas kernels, call(): pl.pallas_call(kernel, out_shape=list(outs), in_specs=specs, out_specs=pl...  7.45 us
    unnamed x8, local copies, waits for them, and re-layouts  1.93 us
  transfers between devices with their start and end apart: 9, of which 5 were waited for; matrix products, arithmetic and copies ran while one was open for 0% of the time, Pallas kernels for 12%

profile of v9, /device:TPU:0, one launch (start us, length us, event | category | flops | bytes accessed | tf_op | source)
XLA Modules:
  0.0 49.0 jit_solution(5732687203198598107)
XLA Ops:
  0.6 0.0 copy-start
  0.6 0.9 %copy-done = s32[12,16,128]{2,1,0:T(8,128)S(1)} copy-done((s32[12,16,128]{2,1,0:T(8,128)S(1)}, s32[12,16,128]{2,1,0:T(8,128)}, u32[]{:S(2)}) %copy-start) | copy-done | bytes 98328
  1.5 0.0 copy-start.2
  1.5 1.0 %copy-done.2 = f32[5,12,16,128]{3,2,1,0:T(8,128)S(1)} copy-done((f32[5,12,16,128]{3,2,1,0:T(8,128)S(1)}, f32[5,12,16,128]{3,2,1,0:T(8,128)}, u32[]{:S(2)}) %copy-start.2) | copy-done | bytes 491544
  2.6 0.1 shard_map.60
  2.7 0.0 copy-start.3
  2.7 0.6 %collective-permute-start = (f32[480,128]{1,0:T(8,128)S(1)}, f32[480,128]{1,0:T(8,128)S(1)}, u32[]{:S(2)}, u32[]{:S(2)}) collective-permute-start(f32[480,128]{1,0:T(8,128)S(1)} %bitcast.31), channel_id=1, source_target_pairs={{0,1},{1,0},{2,3},{3,2},{4,5},{5,4},{6,7},{7,6},{8,9},{9,8},{10,11... | collective-permute-start | bytes 737288 | tf_op jit(solution)/shard_map/ppermute | solution.py:303
  3.2 0.0 copy-start.1
  3.3 1.1 %shard_map.62 = (f32[5,3,16,128]{3,2,1,0:T(8,128)S(1)}, f32[5,3,16,128]{3,2,1,0:T(8,128)S(1)}) custom-call(f32[5,12,16,128]{3,2,1,0:T(8,128)} %start_ref.5, s32[12,16,128]{2,1,0:T(8,128)} %phase_ref.29), custom_call_target="tpu_custom_call" | custom-call | flops 491520 | bytes 245760 | tf_op jit(solution)/shard_map/pallas_call | solution.py:251
  4.3 2.6 %collective-permute-start.1 = (f32[240,128]{1,0:T(8,128)S(1)}, f32[240,128]{1,0:T(8,128)S(1)}, u32[]{:S(2)}, u32[]{:S(2)}) collective-permute-start(f32[240,128]{1,0:T(8,128)S(1)} %bitcast.43), channel_id=1, source_target_pairs={{0,2},{2,4},{4,6},{6,8},{8,10},{10,12},{12,14},{14,16},{16,18},{18... | collective-permute-start | bytes 368648 | tf_op jit(solution)/shard_map/ppermute | solution.py:301
  6.9 4.1 %collective-permute-start.2 = (f32[240,128]{1,0:T(8,128)S(1)}, f32[240,128]{1,0:T(8,128)S(1)}, u32[]{:S(2)}, u32[]{:S(2)}) collective-permute-start(f32[240,128]{1,0:T(8,128)S(1)} %bitcast.42), channel_id=1, source_target_pairs={{2,0},{4,2},{6,4},{8,6},{10,8},{12,10},{14,12},{16,14},{18,16},{20... | collective-permute-start | bytes 368648 | tf_op jit(solution)/shard_map/ppermute | solution.py:301
  12.4 0.1 maximum_multiply_fusion
  12.5 0.1 broadcast_in_dim.2.coefs
  12.5 0.0 copy-done.3
  12.5 0.0 copy-done.1
  12.5 1.1 %shard_map.59.partial_ref = f32[5,12,16,128]{3,2,1,0:T(8,128)S(1)} custom-call(f32[4,16,128]{2,1,0:T(8,128)S(1)} %broadcast_in_dim.2.coefs, f32[5,12,16,128]{3,2,1,0:T(8,128)S(1)} %copy-done.3, s32[12,16,128]{2,1,0:T(8,128)S(1)} %copy-done.1, f32[5,12,16,128]{3,2,1,0:T(8,128)S(1)} %copy-done.3), custom_call_target="tpu_custom_call" | custom-call | flops 24576000 | bytes 491520 | tf_op jit(solution)/shard_map/pallas_call | solution.py:251
  13.6 0.0 collective-permute-done
  13.6 0.3 shard_map.61.partial_ref
  13.9 1.0 %collective-permute-done.1 = f32[240,128]{1,0:T(8,128)S(1)} collective-permute-done((f32[240,128]{1,0:T(8,128)S(1)}, f32[240,128]{1,0:T(8,128)S(1)}, u32[]{:S(2)}, u32[]{:S(2)}) %collective-permute-start.1) | collective-permute-done | bytes 122912 | tf_op jit(solution)/shard_map/ppermute | solution.py:301
  15.0 0.1 shard_map.63
  15.0 0.0 collective-permute-done.2
  15.0 0.1 shard_map.64
  15.1 0.1 shard_map.66
  15.2 0.1 collective-permute-start.3
  15.3 5.3 %collective-permute-start.4 = (f32[240,128]{1,0:T(8,128)S(1)}, f32[240,128]{1,0:T(8,128)S(1)}, u32[]{:S(2)}, u32[]{:S(2)}) collective-permute-start(f32[240,128]{1,0:T(8,128)S(1)} %bitcast.45), channel_id=1, source_target_pairs={{2,0},{4,2},{6,4},{8,6},{10,8},{12,10},{14,12},{16,14},{18,16},{20... | collective-permute-start | bytes 368648 | tf_op jit(solution)/shard_map/ppermute | solution.py:301
  20.6 0.0 collective-permute-start.5
  20.6 1.1 %shard_map.65.partial_ref = f32[5,12,16,128]{3,2,1,0:T(8,128)S(1)} custom-call(f32[4,16,128]{2,1,0:T(8,128)S(1)} %broadcast_in_dim.2.coefs, f32[5,12,16,128]{3,2,1,0:T(8,128)S(1)} %get-tuple-element.22.state_ref, s32[12,16,128]{2,1,0:T(8,128)S(1)} %copy-done.1, f32[5,12,16,128]{3,2,1,0:T(8,128)S(1)} %copy-done.3), custom_call_target="tpu_custom_call" | custom-call | flops 24576000 | bytes 491520 | tf_op jit(solution)/shard_map/pallas_call | solution.py:251
  21.7 0.0 collective-permute-done.3
  21.7 0.3 shard_map.67.partial_ref
  22.0 1.8 %collective-permute-done.4 = f32[240,128]{1,0:T(8,128)S(1)} collective-permute-done((f32[240,128]{1,0:T(8,128)S(1)}, f32[240,128]{1,0:T(8,128)S(1)}, u32[]{:S(2)}, u32[]{:S(2)}) %collective-permute-start.4) | collective-permute-done | bytes 122912 | tf_op jit(solution)/shard_map/ppermute | solution.py:301
  23.8 0.1 shard_map.68
  23.8 5.8 %collective-permute-done.5 = f32[240,128]{1,0:T(8,128)S(1)} collective-permute-done((f32[240,128]{1,0:T(8,128)S(1)}, f32[240,128]{1,0:T(8,128)S(1)}, u32[]{:S(2)}, u32[]{:S(2)}) %collective-permute-start.5) | collective-permute-done | bytes 122912 | tf_op jit(solution)/shard_map/ppermute | solution.py:301
  29.7 0.1 shard_map.69
  29.7 0.1 shard_map.71
  29.9 0.1 collective-permute-start.6
  29.9 0.3 collective-permute-start.8
  30.3 1.8 %collective-permute-start.7 = (f32[240,128]{1,0:T(8,128)S(1)}, f32[240,128]{1,0:T(8,128)S(1)}, u32[]{:S(2)}, u32[]{:S(2)}) collective-permute-start(f32[240,128]{1,0:T(8,128)S(1)} %bitcast.44), channel_id=1, source_target_pairs={{0,2},{2,4},{4,6},{6,8},{8,10},{10,12},{12,14},{14,16},{16,18},{18... | collective-permute-start | bytes 368648 | tf_op jit(solution)/shard_map/ppermute | solution.py:301
  32.0 1.1 %shard_map.70.partial_ref = f32[5,12,16,128]{3,2,1,0:T(8,128)S(1)} custom-call(f32[4,16,128]{2,1,0:T(8,128)S(1)} %broadcast_in_dim.2.coefs, f32[5,12,16,128]{3,2,1,0:T(8,128)S(1)} %get-tuple-element.26.state_ref, s32[12,16,128]{2,1,0:T(8,128)S(1)} %copy-done.1, f32[5,12,16,128]{3,2,1,0:T(8,128)S(1)} %copy-done.3), custom_call_target="tpu_custom_call" | custom-call | flops 24576000 | bytes 491520 | tf_op jit(solution)/shard_map/pallas_call | solution.py:251
  33.1 0.0 collective-permute-done.6
  33.1 1.0 %shard_map.72 = (f32[5,12,16,128]{3,2,1,0:T(8,128)S(1)}, f32[16,128]{1,0:T(8,128)S(1)}, f32[5,12,16,128]{3,2,1,0:T(8,128)}) custom-call(f32[4,16,128]{2,1,0:T(8,128)S(1)} %broadcast_in_dim.2.coefs, f32[5,12,16,128]{3,2,1,0:T(8,128)S(1)} %shard_map.70.partial_ref, s32[12,16,128]{2,1,0:T(8,128)S(1)} %copy-done.1, ...), custom_call_target="tpu_custom_call", output_to_operand_aliasing={{0}: (1, {})} | custom-call | flops 491520 | bytes 991232 | tf_op jit(solution)/shard_map/pallas_call | solution.py:251
  34.1 2.1 %collective-permute-done.8 = f32[240,128]{1,0:T(8,128)S(1)} collective-permute-done((f32[240,128]{1,0:T(8,128)S(1)}, f32[240,128]{1,0:T(8,128)S(1)}, u32[]{:S(2)}, u32[]{:S(2)}) %collective-permute-start.8) | collective-permute-done | bytes 122912 | tf_op jit(solution)/shard_map/ppermute | solution.py:301
  36.2 3.1 %collective-permute-done.7 = f32[240,128]{1,0:T(8,128)S(1)} collective-permute-done((f32[240,128]{1,0:T(8,128)S(1)}, f32[240,128]{1,0:T(8,128)S(1)}, u32[]{:S(2)}, u32[]{:S(2)}) %collective-permute-start.7) | collective-permute-done | bytes 122912 | tf_op jit(solution)/shard_map/ppermute | solution.py:301
  39.3 0.2 shard_map.73
  39.4 8.9 %all_to_all.11 = f32[32,1,128]{2,1,0:T(1,128)S(1)} all-to-all(f32[32,1,128]{2,1,0:T(1,128)S(1)} %bitcast.41), channel_id=1, replica_groups=mesh['gx'=16,'gy'=2] {'gx','gy'}, dimensions={0} | all-to-all | bytes 32768 | tf_op jit(solution)/shard_map/all_to_all | solution.py:348
  48.3 0.7 %shard_map.74 = (f32[5,12,16,128]{3,2,1,0:T(8,128)}, f32[1,128]{1,0:T(1,128)}) custom-call(f32[5,12,16,128]{3,2,1,0:T(8,128)S(1)} %get-tuple-element.31.state_ref, f32[32,128]{1,0:T(8,128)S(1)} %bitcast.40, f32[5,12,16,128]{3,2,1,0:T(8,128)} %get-tuple-element.33.inner_ref), custom_call_target="tpu_custom_call", output_to_operand_aliasing={{0}: (2, {})} | custom-call | flops 1000 | bytes 492032 | tf_op jit(solution)/shard_map/pallas_call | solution.py:251
Async XLA Ops:
  0.6 0.9 %copy-start = (s32[12,16,128]{2,1,0:T(8,128)S(1)}, s32[12,16,128]{2,1,0:T(8,128)}, u32[]{:S(2)}) copy-start(s32[12,16,128]{2,1,0:T(8,128)} %phase_ref.29) | copy-start | bytes 294916
  1.5 1.0 %copy-start.2 = (f32[5,12,16,128]{3,2,1,0:T(8,128)S(1)}, f32[5,12,16,128]{3,2,1,0:T(8,128)}, u32[]{:S(2)}) copy-start(f32[5,12,16,128]{3,2,1,0:T(8,128)} %start_ref.5) | copy-start | bytes 1474564
  2.7 9.9 %copy-start.3 = (f32[5,12,16,128]{3,2,1,0:T(8,128)S(1)}, f32[5,12,16,128]{3,2,1,0:T(8,128)}, u32[]{:S(2)}) copy-start(f32[5,12,16,128]{3,2,1,0:T(8,128)} %start_ref.5) | copy-start | bytes 1474564
  2.7 10.9 %collective-permute-start = (f32[480,128]{1,0:T(8,128)S(1)}, f32[480,128]{1,0:T(8,128)S(1)}, u32[]{:S(2)}, u32[]{:S(2)}) collective-permute-start(f32[480,128]{1,0:T(8,128)S(1)} %bitcast.31), channel_id=1, source_target_pairs={{0,1},{1,0},{2,3},{3,2},{4,5},{5,4},{6,7},{7,6},{8,9},{9,8},{10,11... | collective-permute-start | bytes 737288 | tf_op jit(solution)/shard_map/ppermute | solution.py:303
  3.2 9.3 %copy-start.1 = (s32[12,16,128]{2,1,0:T(8,128)S(1)}, s32[12,16,128]{2,1,0:T(8,128)}, u32[]{:S(2)}) copy-start(s32[12,16,128]{2,1,0:T(8,128)} %phase_ref.29) | copy-start | bytes 294916
  4.3 10.6 %collective-permute-start.1 = (f32[240,128]{1,0:T(8,128)S(1)}, f32[240,128]{1,0:T(8,128)S(1)}, u32[]{:S(2)}, u32[]{:S(2)}) collective-permute-start(f32[240,128]{1,0:T(8,128)S(1)} %bitcast.43), channel_id=1, source_target_pairs={{0,2},{2,4},{4,6},{6,8},{8,10},{10,12},{12,14},{14,16},{16,18},{18... | collective-permute-start | bytes 368648 | tf_op jit(solution)/shard_map/ppermute | solution.py:301
  6.9 8.1 %collective-permute-start.2 = (f32[240,128]{1,0:T(8,128)S(1)}, f32[240,128]{1,0:T(8,128)S(1)}, u32[]{:S(2)}, u32[]{:S(2)}) collective-permute-start(f32[240,128]{1,0:T(8,128)S(1)} %bitcast.42), channel_id=1, source_target_pairs={{2,0},{4,2},{6,4},{8,6},{10,8},{12,10},{14,12},{16,14},{18,16},{20... | collective-permute-start | bytes 368648 | tf_op jit(solution)/shard_map/ppermute | solution.py:301
  15.2 6.4 %collective-permute-start.3 = (f32[480,128]{1,0:T(8,128)S(1)}, f32[480,128]{1,0:T(8,128)S(1)}, u32[]{:S(2)}, u32[]{:S(2)}) collective-permute-start(f32[480,128]{1,0:T(8,128)S(1)} %bitcast.32), channel_id=1, source_target_pairs={{0,1},{1,0},{2,3},{3,2},{4,5},{5,4},{6,7},{7,6},{8,9},{9,8},{10,11... | collective-permute-start | bytes 737288 | tf_op jit(solution)/shard_map/ppermute | solution.py:303
  15.3 8.4 %collective-permute-start.4 = (f32[240,128]{1,0:T(8,128)S(1)}, f32[240,128]{1,0:T(8,128)S(1)}, u32[]{:S(2)}, u32[]{:S(2)}) collective-permute-start(f32[240,128]{1,0:T(8,128)S(1)} %bitcast.45), channel_id=1, source_target_pairs={{2,0},{4,2},{6,4},{8,6},{10,8},{12,10},{14,12},{16,14},{18,16},{20... | collective-permute-start | bytes 368648 | tf_op jit(solution)/shard_map/ppermute | solution.py:301
  20.6 9.1 %collective-permute-start.5 = (f32[240,128]{1,0:T(8,128)S(1)}, f32[240,128]{1,0:T(8,128)S(1)}, u32[]{:S(2)}, u32[]{:S(2)}) collective-permute-start(f32[240,128]{1,0:T(8,128)S(1)} %bitcast.46), channel_id=1, source_target_pairs={{0,2},{2,4},{4,6},{6,8},{8,10},{10,12},{12,14},{14,16},{16,18},{18... | collective-permute-start | bytes 368648 | tf_op jit(solution)/shard_map/ppermute | solution.py:301
  29.9 3.3 %collective-permute-start.6 = (f32[480,128]{1,0:T(8,128)S(1)}, f32[480,128]{1,0:T(8,128)S(1)}, u32[]{:S(2)}, u32[]{:S(2)}) collective-permute-start(f32[480,128]{1,0:T(8,128)S(1)} %bitcast.33), channel_id=1, source_target_pairs={{0,1},{1,0},{2,3},{3,2},{4,5},{5,4},{6,7},{7,6},{8,9},{9,8},{10,11... | collective-permute-start | bytes 737288 | tf_op jit(solution)/shard_map/ppermute | solution.py:303
  29.9 6.2 %collective-permute-start.8 = (f32[240,128]{1,0:T(8,128)S(1)}, f32[240,128]{1,0:T(8,128)S(1)}, u32[]{:S(2)}, u32[]{:S(2)}) collective-permute-start(f32[240,128]{1,0:T(8,128)S(1)} %bitcast.47), channel_id=1, source_target_pairs={{2,0},{4,2},{6,4},{8,6},{10,8},{12,10},{14,12},{16,14},{18,16},{20... | collective-permute-start | bytes 368648 | tf_op jit(solution)/shard_map/ppermute | solution.py:301
  30.3 9.0 %collective-permute-start.7 = (f32[240,128]{1,0:T(8,128)S(1)}, f32[240,128]{1,0:T(8,128)S(1)}, u32[]{:S(2)}, u32[]{:S(2)}) collective-permute-start(f32[240,128]{1,0:T(8,128)S(1)} %bitcast.44), channel_id=1, source_target_pairs={{0,2},{2,4},{4,6},{6,8},{8,10},{10,12},{12,14},{14,16},{16,18},{18... | collective-permute-start | bytes 368648 | tf_op jit(solution)/shard_map/ppermute | solution.py:301
